TPU v7x, 32 devices: a whole 2x2x4 slice. The times are simulated.
32 devices in a mesh: dp: 4 (over z), tensor: 8 (over y, x, core).
Axes of the slice: x: 2, y: 2, z: 4, core: 2. Of those that a mesh axis runs over, the one named last changes fastest.
Arguments:
- residual: float32 [4096, 1536], P(('dp', 'tensor')), may hold values from -6 to 6
- cotangent: float32 [4096, 1536], P(('dp', 'tensor')), may hold values from -6 to 6
- segments: int32 [4, 1024], P('dp'), may hold values from 0 to 2, never falling along the last dimension, each value on 1 to 512 neighbouring positions
- norm_gain: float32 [2, 1536], replicated, may hold values from 0.1 to 1.9
- inner_weight: bfloat16 [2, 2, 1536, 3072], P(None, None, None, 'tensor'), may hold values from -0.15625 to 0.15625
- state_weight: bfloat16 [2, 1536, 256], replicated, may hold values from -0.15625 to 0.15625
- step_weight: bfloat16 [2, 1536, 48], P(None, None, 'tensor'), may hold values from -0.15625 to 0.15625
- step_bias: float32 [2, 48], P(None, 'tensor'), may hold values from -6.9 to -2.25
- decay_log: float32 [2, 48], P(None, 'tensor'), may hold values from 0 to 2.77
- skip_gain: float32 [2, 48], P(None, 'tensor'), may hold values from 0.5 to 1.5
- conv_weight: float32 [2, 4, 3072], P(None, None, 'tensor'), may hold values from -3 to 3
- conv_bias: float32 [2, 3072], P(None, 'tensor'), may hold values from -0.5 to 0.5
- state_conv_weight: float32 [2, 4, 256], replicated, may hold values from -3 to 3
- state_conv_bias: float32 [2, 256], replicated, may hold values from -0.5 to 0.5
- gate_gain: float32 [2, 3072], P(None, 'tensor'), may hold values from 0.1 to 1.9
- out_weight: bfloat16 [2, 3072, 1536], P(None, 'tensor'), may hold values from -0.109375 to 0.109375
Outputs:
- block_output: float32 [4096, 1536], P(('dp', 'tensor'))
- input_grad: float32 [4096, 1536], P(('dp', 'tensor'))
- grad_norm_gain: float32 [2, 1536], P(None, ('dp', 'tensor'))
- grad_inner_weight: float32 [2, 2, 1536, 3072], P(None, None, 'dp', 'tensor')
- grad_state_weight: float32 [2, 1536, 256], P(None, ('dp', 'tensor'))
- grad_step_weight: float32 [2, 1536, 48], P(None, 'dp', 'tensor')
- grad_step_bias: float32 [2, 48], P(None, 'tensor')
- grad_decay_log: float32 [2, 48], P(None, 'tensor')
- grad_skip_gain: float32 [2, 48], P(None, 'tensor')
- grad_conv_weight: float32 [2, 4, 3072], P(None, None, 'tensor')
- grad_conv_bias: float32 [2, 3072], P(None, 'tensor')
- grad_state_conv_weight: float32 [2, 4, 256], replicated
- grad_state_conv_bias: float32 [2, 256], replicated
- grad_gate_gain: float32 [2, 3072], P(None, 'tensor')
- grad_out_weight: float32 [2, 3072, 1536], P(None, 'tensor', 'dp')
Inputs may be any that keep to these rules, and one draw needn't show every extreme that they name: `segments`: each row numbers its sequences from 0 in order, never falling; a sequence has 1 to 512 tokens, and one sequence of each row has exactly 512.
All inputs are finite; a program needn't handle non-finite values.
Results may differ from a plain program's by a relative error of at most 0.029.
Values may be sent and summed in bfloat16 or wider, within the bound.
A program may use at most 192 MiB of HBM per device.

v0:
```python
import jax
import jax.numpy as jnp
from jax import lax
from jax.sharding import PartitionSpec as P

D = 1536
INNER = 3072
SPAN = 256
LAYERS = 2


EPS = 1e-05
HIGH = lax.Precision.HIGHEST


def shifted(array, offset, fill):
    head = jnp.full((offset,) + array.shape[1:], fill, array.dtype)
    return jnp.concatenate([head, array[:-offset]], axis=0)


def causal_conv(values, kernel, bias, segment):
    result = bias[None, :] + kernel[0][None, :] * values
    for offset in range(1, kernel.shape[0]):
        keep = (shifted(segment, offset, -1) == segment).astype(values.dtype)
        result = result + kernel[offset][None, :] * shifted(values, offset, 0.0) * keep[:, None]
    return result


def state_scan(inputs, step_size, rate, in_state, out_state, skip_gain, segment):
    length, heads, width = inputs.shape
    count = length // SPAN
    half_width = in_state.shape[1]
    log_decay = -step_size * rate[None, :]
    cumul = jnp.cumsum(log_decay.reshape(count, SPAN, heads), axis=1)
    cumul_head = jnp.transpose(cumul, (0, 2, 1))
    seg_blocks = segment.reshape(count, SPAN)
    block_in = inputs.reshape(count, SPAN, heads, width)
    weighted = block_in * step_size.reshape(count, SPAN, heads)[..., None]
    in_blocks = in_state.reshape(count, SPAN, half_width)
    out_blocks = out_state.reshape(count, SPAN, half_width)
    causal = jnp.arange(SPAN)[:, None] >= jnp.arange(SPAN)[None, :]
    same = (seg_blocks[:, :, None] == seg_blocks[:, None, :]) & causal[None]
    keep_mask = same.astype(inputs.dtype)[:, None]
    differ = cumul_head[:, :, :, None] - cumul_head[:, :, None, :]
    decay_mat = jnp.exp(jnp.where(same[:, None], differ, 0.0)) * keep_mask
    scores = jnp.einsum("ctn,csn->cts", out_blocks, in_blocks, precision=HIGH)
    intra = jnp.einsum("chts,cshp->cthp", decay_mat * scores[:, None], weighted, precision=HIGH)
    last = cumul_head[:, :, -1]
    tail_keep = (seg_blocks == seg_blocks[:, -1:]).astype(inputs.dtype)
    to_end = jnp.exp(last[:, :, None] - cumul_head) * tail_keep[:, None, :]
    span_states = jnp.einsum("chs,cshp,csn->chpn", to_end, weighted, in_blocks, precision=HIGH)
    prev_seg = jnp.concatenate([jnp.full((1,), -1, segment.dtype), seg_blocks[:-1, -1]])
    carry_keep = (seg_blocks[:, -1] == prev_seg).astype(inputs.dtype)
    carry_decay = jnp.exp(last) * carry_keep[:, None]

    def advance(current, items):
        factor, fresh = items
        return (factor[:, None, None] * current + fresh, current)

    _, entering = lax.scan(
        advance, jnp.zeros((heads, width, half_width), inputs.dtype), (carry_decay, span_states)
    )
    head_keep = (seg_blocks == prev_seg[:, None]).astype(inputs.dtype)
    from_state = jnp.exp(cumul_head) * head_keep[:, None, :]
    inter = jnp.einsum("chq,cqn,chpn->cqhp", from_state, out_blocks, entering, precision=HIGH)
    result = intra + inter + skip_gain[None, None, :, None] * block_in
    return result.reshape(length, heads * width)


def mixer_core(floats, segment):
    (
        gate_in,
        value_in,
        state_in,
        step_in,
        conv_weight,
        conv_bias,
        state_conv_weight,
        state_conv_bias,
        step_bias,
        decay_log,
        skip_gain,
    ) = floats
    heads = step_in.shape[1]
    length = value_in.shape[0]
    values = jax.nn.silu(causal_conv(value_in, conv_weight, conv_bias, segment))
    states = jax.nn.silu(causal_conv(state_in, state_conv_weight, state_conv_bias, segment))
    half_width = states.shape[1] // 2
    step_size = jax.nn.softplus(step_in + step_bias[None, :])
    scanned = state_scan(
        values.reshape(length, heads, values.shape[1] // heads),
        step_size,
        jnp.exp(decay_log),
        states[:, :half_width],
        states[:, half_width:],
        skip_gain,
        segment,
    )
    return scanned * jax.nn.silu(gate_in)


def contract_rows(left, right):
    return lax.dot_general(
        left, right, (((0,), (0,)), ((), ())), preferred_element_type=jnp.float32
    )


def contract_cols(left, right):
    return lax.dot_general(
        left, right, (((1,), (1,)), ((), ())), preferred_element_type=jnp.float32
    )


def forward_layer(resid, segment, params):
    (
        norm_gain,
        inner_weight,
        state_weight,
        step_weight,
        step_bias,
        decay_log,
        skip_gain,
        conv_weight,
        conv_bias,
        state_conv_weight,
        state_conv_bias,
        gate_gain,
        out_weight,
    ) = params
    rows = resid.shape[0]
    row_scale = lax.rsqrt(jnp.mean(resid * resid, axis=1) + EPS)
    normed_rows = (resid * row_scale[:, None] * norm_gain[None, :]).astype(jnp.bfloat16)
    normed = lax.all_gather(normed_rows, "tensor", axis=0, tiled=True)
    gate_in = jnp.dot(normed, inner_weight[0], preferred_element_type=jnp.float32)
    value_in = jnp.dot(normed, inner_weight[1], preferred_element_type=jnp.float32)
    state_in = jnp.dot(normed, state_weight, preferred_element_type=jnp.float32)
    step_in = jnp.dot(normed, step_weight, preferred_element_type=jnp.float32)
    floats = (
        gate_in,
        value_in,
        state_in,
        step_in,
        conv_weight,
        conv_bias,
        state_conv_weight,
        state_conv_bias,
        step_bias,
        decay_log,
        skip_gain,
    )
    gated = mixer_core(floats, segment)
    partial_square = jnp.sum(gated * gated, axis=1)
    scaled_in = (gated * gate_gain[None, :]).astype(jnp.bfloat16)
    total_square = lax.psum(partial_square, "tensor")
    gate_scale = lax.rsqrt(total_square / INNER + EPS)
    mixed = lax.psum_scatter(
        (
            gate_scale[:, None] * jnp.dot(scaled_in, out_weight, preferred_element_type=jnp.float32)
        ).astype(jnp.bfloat16),
        "tensor",
        scatter_dimension=0,
        tiled=True,
    ).astype(jnp.float32)
    row_gate = lax.dynamic_slice_in_dim(gate_scale, lax.axis_index("tensor") * rows, rows, 0)
    saved = (resid, row_scale, normed_rows, normed, floats, gated, row_gate, scaled_in, mixed)
    return (resid + mixed, saved)


def backward_layer(saved, grad_out, segment, params):
    (
        norm_gain,
        inner_weight,
        state_weight,
        step_weight,
        step_bias,
        decay_log,
        skip_gain,
        conv_weight,
        conv_bias,
        state_conv_weight,
        state_conv_bias,
        gate_gain,
        out_weight,
    ) = params
    resid, row_scale, normed_rows, normed, floats, gated, row_gate, scaled_in, mixed = saved
    sent_rows = (row_gate[:, None] * grad_out).astype(jnp.bfloat16)
    mean_rows = -0.5 * row_gate * row_gate * jnp.sum(mixed * grad_out, axis=1)
    sent = lax.all_gather(sent_rows, "tensor", axis=0, tiled=True)
    mean_grad = lax.all_gather(mean_rows, "tensor", axis=0, tiled=True)
    grad_out_weight = contract_rows(scaled_in, sent)
    grad_scaled = contract_cols(sent, out_weight)
    grad_gate_gain = jnp.sum(grad_scaled * gated, axis=0)
    grad_gated = grad_scaled * gate_gain[None, :] + 2.0 / INNER * mean_grad[:, None] * gated
    pullback = jax.vjp(lambda *items: mixer_core(items, segment), *floats)[1]
    grads = pullback(grad_gated)
    rounded_gate = grads[0].astype(jnp.bfloat16)
    rounded_value = grads[1].astype(jnp.bfloat16)
    rounded_step = grads[3].astype(jnp.bfloat16)
    partial_normed = (
        contract_cols(rounded_gate, inner_weight[0])
        + contract_cols(rounded_value, inner_weight[1])
        + contract_cols(rounded_step, step_weight)
    )
    grad_rows, state_rows = (
        lax.psum_scatter(
            partial_normed.astype(jnp.bfloat16), "tensor", scatter_dimension=0, tiled=True
        ).astype(jnp.float32),
        lax.psum_scatter(
            grads[2].astype(jnp.bfloat16), "tensor", scatter_dimension=0, tiled=True
        ).astype(jnp.float32),
    )
    rounded_state = state_rows.astype(jnp.bfloat16)
    grad_normed = grad_rows + contract_cols(rounded_state, state_weight)
    grad_inner = jnp.stack(
        [contract_rows(normed, rounded_gate), contract_rows(normed, rounded_value)]
    )
    grad_state_weight = contract_rows(normed_rows, rounded_state)
    grad_step_weight = contract_rows(normed, rounded_step)
    weighted = grad_normed * norm_gain[None, :]
    grad_norm_gain = jnp.sum(grad_normed * resid * row_scale[:, None], axis=0)
    inner_sum = jnp.sum(weighted * resid, axis=1)
    grad_resid = (
        grad_out
        + row_scale[:, None] * weighted
        - resid * (row_scale * row_scale * row_scale * inner_sum / D)[:, None]
    )
    layer_grads = (
        grad_norm_gain,
        grad_inner,
        grad_state_weight,
        grad_step_weight,
        grads[8],
        grads[9],
        grads[10],
        grads[4],
        grads[5],
        grads[6],
        grads[7],
        grad_gate_gain,
        grad_out_weight,
    )
    return (grad_resid, layer_grads)


def shards(
    residual,
    cotangent,
    segments,
    norm_gain,
    inner_weight,
    state_weight,
    step_weight,
    step_bias,
    decay_log,
    skip_gain,
    conv_weight,
    conv_bias,
    state_conv_weight,
    state_conv_bias,
    gate_gain,
    out_weight,
):
    weights = (
        norm_gain,
        inner_weight,
        state_weight,
        step_weight,
        step_bias,
        decay_log,
        skip_gain,
        conv_weight,
        conv_bias,
        state_conv_weight,
        state_conv_bias,
        gate_gain,
        out_weight,
    )
    segment = segments[0]
    hidden = residual
    saved_all = []
    for layer in range(LAYERS):
        hidden, saved = forward_layer(hidden, segment, tuple((item[layer] for item in weights)))
        saved_all.append(saved)
    grad_hidden = cotangent
    per_layer = [None] * LAYERS
    for layer in range(LAYERS - 1, -1, -1):
        grad_hidden, per_layer[layer] = backward_layer(
            saved_all[layer], grad_hidden, segment, tuple((item[layer] for item in weights))
        )
    stacked = [
        jnp.stack([per_layer[layer][field] for layer in range(LAYERS)]) for field in range(13)
    ]
    head_big = (
        lax.psum_scatter(
            stacked[1].astype(jnp.bfloat16), "dp", scatter_dimension=2, tiled=True
        ).astype(jnp.float32),
        lax.psum_scatter(
            stacked[3].astype(jnp.bfloat16), "dp", scatter_dimension=1, tiled=True
        ).astype(jnp.float32),
        lax.psum_scatter(
            stacked[12].astype(jnp.bfloat16), "dp", scatter_dimension=2, tiled=True
        ).astype(jnp.float32),
    )
    head_small = lax.psum(
        (stacked[4], stacked[5], stacked[6], stacked[7], stacked[8], stacked[11]), "dp"
    )
    shared = (
        lax.psum_scatter(stacked[2], ("dp", "tensor"), scatter_dimension=1, tiled=True),
        lax.psum_scatter(stacked[0], ("dp", "tensor"), scatter_dimension=1, tiled=True),
    )
    shared_small = lax.psum((stacked[9], stacked[10]), ("dp", "tensor"))
    return (
        hidden,
        grad_hidden,
        shared[1],
        head_big[0],
        shared[0],
        head_big[1],
        head_small[0],
        head_small[1],
        head_small[2],
        head_small[3],
        head_small[4],
        shared_small[0],
        shared_small[1],
        head_small[5],
        head_big[2],
    )


def solution(mesh):
    return jax.shard_map(
        shards,
        mesh=mesh,
        in_specs=(
            P(("dp", "tensor"), None),
            P(("dp", "tensor"), None),
            P("dp", None),
            P(),
            P(None, None, None, "tensor"),
            P(),
            P(None, None, "tensor"),
            P(None, "tensor"),
            P(None, "tensor"),
            P(None, "tensor"),
            P(None, None, "tensor"),
            P(None, "tensor"),
            P(),
            P(),
            P(None, "tensor"),
            P(None, "tensor", None),
        ),
        out_specs=(
            P(("dp", "tensor"), None),
            P(("dp", "tensor"), None),
            P(None, ("dp", "tensor")),
            P(None, None, "dp", "tensor"),
            P(None, ("dp", "tensor"), None),
            P(None, "dp", "tensor"),
            P(None, "tensor"),
            P(None, "tensor"),
            P(None, "tensor"),
            P(None, None, "tensor"),
            P(None, "tensor"),
            P(),
            P(),
            P(None, "tensor"),
            P(None, "tensor", "dp"),
        ),
        check_vma=False,
    )
```

profile of v0, /device:TPU:0, one launch (start us, length us, event | category | flops | bytes accessed | tf_op | source)
XLA Modules:
  0.0 1154.0 jit_solution(4340343625140786474)
XLA Ops:
  19.7 27.0 %all-gather.7.cloned.1.call-done = bf16[1024,1536]{1,0:T(8,128)(2,1)} async-done(((bf16[128,1536]{1,0:T(8,128)(2,1)}), bf16[1024,1536]{1,0:T(8,128)(2,1)}) %all-gather.7.cloned.1.call-update) | async-done | bytes 3145744 | tf_op jit(solution)/shard_map/all_gather | solution.py:133
  54.5 7.2 reduce-window.40
  76.2 6.9 while.94
  84.6 9.0 fusion.22
  101.1 5.3 multiply_reduce_fusion.21
  106.4 13.1 %psum.70 = f32[1024]{0:T(1024)S(1)} all-reduce(f32[1024]{0:T(1024)S(1)} %get-tuple-element.866), channel_id=1, replica_groups=mesh['dp'=4,'tensor'=8] {'tensor'}, use_global_device_ids=true, to_apply=%region_6.7 | all-reduce | flops 1024 | bytes 8192 | tf_op jit(solution)/shard_map/psum | solution.py:154
  119.5 5.2 multiply_convert_fusion.1
  124.8 46.1 %reduce-scatter.18.cloned.1.call-done = bf16[128,1536]{1,0:T(8,128)(2,1)} async-done(((bf16[1024,1536]{1,0:T(8,128)(2,1)}), bf16[128,1536]{1,0:T(8,128)(2,1)}) %reduce-scatter.18.cloned.1.call-update) | async-done | bytes 393232 | tf_op jit(solution)/shard_map/reduce_scatter | solution.py:156
  174.0 32.3 %all-gather.9.cloned.1.call-done = bf16[1024,1536]{1,0:T(8,128)(2,1)} async-done(((bf16[128,1536]{1,0:T(8,128)(2,1)}), bf16[1024,1536]{1,0:T(8,128)(2,1)}) %all-gather.9.cloned.1.call-update) | async-done | bytes 3145744 | tf_op jit(solution)/shard_map/all_gather | solution.py:133
  209.9 7.6 reduce-window.44
  243.7 6.9 while.95
  252.9 9.3 fusion.14
  269.5 6.3 multiply_reduce_fusion.20
  275.8 13.1 %psum.71 = f32[1024]{0:T(1024)S(1)} all-reduce(f32[1024]{0:T(1024)S(1)} %get-tuple-element.856), channel_id=1, replica_groups=mesh['dp'=4,'tensor'=8] {'tensor'}, use_global_device_ids=true, to_apply=%region_14.15 | all-reduce | flops 1024 | bytes 8192 | tf_op jit(solution)/shard_map/psum | solution.py:154
  288.9 5.2 multiply_convert_fusion
  294.2 46.2 %reduce-scatter.20.cloned.1.call-done = bf16[128,1536]{1,0:T(8,128)(2,1)} async-done(((bf16[1024,1536]{1,0:T(8,128)(2,1)}), bf16[128,1536]{1,0:T(8,128)(2,1)}) %reduce-scatter.20.cloned.1.call-update) | async-done | bytes 393232 | tf_op jit(solution)/shard_map/reduce_scatter | solution.py:156
  348.9 14.5 %while.96 = (s32[]{:T(128)}, f32[6,64,128]{2,1,0:T(8,128)S(1)}, f32[4,6,64,128]{3,2,1,0:T(8,128)}, f32[4,6,1,1]{1,3,2,0:T(1,128)}, f32[4,6]{1,0:T(4,128)}, /*index=5*/f32[4,6,64,128]{3,2,1,0:T(8,128)}, s32[]{:T(128)}, s32[]{:T(128)}) while((s32[]{:T(128)}, f32[6,64,128]{2,1,0:T(8,128)S(1)}, f32[4,6,64,128]{3,2,1,0:T(8,128)}, ...), condition=%wide.region_19.21_spmd.clone, body=%wide.region_18.20_spmd.clone.sunk | while | flops 196611 | bytes 984256 | solution.py:60
  366.3 9.2 fusion.93
  381.1 8.9 all-gather
  390.0 8.8 multiply_reduce_fusion.16
  413.8 10.1 while.97
  423.9 4.5 fusion.134
  432.0 10.0 fusion.25
  451.2 6.1 fusion.143
  457.3 6.1 multiply_reduce_fusion.19
  476.6 6.3 fusion.147
  484.9 30.2 %reduce-window.50 = f32[4,6,2,128]{3,2,1,0:T(2,128)S(1)} reduce-window(f32[4,6,2,128]{3,2,1,0:T(2,128)S(1)} %reshape.685, f32[]{:T(128)} %constant.204.clone.1), window={size=1x1x1x128 pad=0_0x0_0x0_0x0_127}, to_apply=%region_28.30 | reduce-window | flops 780288 | bytes 49156 | tf_op jit(solution)/shard_map/reduce-window.6
  516.3 7.4 add_convert_fusion.1
  524.7 45.1 %reduce-scatter.22.cloned.1.call-done = bf16[128,1536]{1,0:T(8,128)(2,1)} async-done(((bf16[1024,1536]{1,0:T(8,128)(2,1)}), bf16[128,1536]{1,0:T(8,128)(2,1)}) %reduce-scatter.22.cloned.1.call-update) | async-done | bytes 393232 | tf_op jit(solution)/shard_map/reduce_scatter | solution.py:205
  577.7 4.5 while.98
  584.2 7.4 fusion.87
  598.6 8.7 all-gather.1
  607.3 8.3 multiply_reduce_fusion.17
  627.6 7.6 while.99
  642.2 10.3 fusion.27
  661.7 6.1 fusion.154
  667.8 6.7 multiply_reduce_fusion.18
  686.2 6.4 fusion.158
  694.5 30.2 %reduce-window.56 = f32[4,6,2,128]{3,2,1,0:T(2,128)S(1)} reduce-window(f32[4,6,2,128]{3,2,1,0:T(2,128)S(1)} %reshape.686, f32[]{:T(128)} %constant.204.clone.1), window={size=1x1x1x128 pad=0_0x0_0x0_0x0_127}, to_apply=%region_46.48 | reduce-window | flops 780288 | bytes 49156 | tf_op jit(solution)/shard_map/reduce-window.10
  725.3 7.3 add_convert_fusion
  750.2 6.9 copy.562
  774.2 4.6 reduce-scatter.26.cloned.1.call-done
  782.7 4.4 pad_maximum_fusion
  792.3 19.7 %all-reduce.49 = (f32[2,6]{1,0:T(2,128)}, f32[2,6]{1,0:T(2,128)}, f32[2,6]{1,0:T(2,128)}, f32[2,4,384]{2,1,0:T(4,128)}, f32[2,384]{1,0:T(2,128)}, /*index=5*/f32[2,384]{1,0:T(2,128)}) all-reduce(f32[2,6]{1,0:T(2,128)S(1)} %pad_maximum_fusion.10, f32[2,6]{1,0:T(2,128)S(1)} %pad_maximum_fusion.11, ...), channel_id=1, replica_groups=mesh['dp'=4,'tensor'=8] {'dp'}, use_global_device_ids=true, to_apply=%region_60.62 | all-reduce | flops 4644 | bytes 37152 | tf_op jit(solution)/shard_map/psum | solution.py:304
  812.1 40.9 %all-reduce.48 = (f32[2,4,256]{2,1,0:T(4,128)}, f32[2,256]{1,0:T(2,128)}) all-reduce(f32[2,4,256]{2,1,0:T(4,128)S(1)} %pad_maximum_fusion.6, f32[2,256]{1,0:T(2,128)S(1)} %pad_maximum_fusion.9), channel_id=1, replica_groups=mesh['dp'=4,'tensor'=8] {'dp','tensor'}, use_global_device_ids=true, to_apply=%region_89.91 | all-reduce | flops 2560 | bytes 20480 | tf_op jit(solution)/shard_map/psum | solution.py:311
  860.4 91.5 %reduce-scatter.34.cloned.1.call-done = f32[48,2]{1,0:T(8,128)} async-done(((f32[1536,2]{1,0:T(8,128)}), f32[48,2]{1,0:T(8,128)}) %reduce-scatter.34.cloned.1.call-update) | async-done | bytes 400
  953.2 85.2 %reduce-scatter.30.cloned.1.call-done = bf16[2,2,384,384]{3,2,1,0:T(8,128)(2,1)} async-done(((bf16[2,2,1536,384]{3,2,1,0:T(8,128)(2,1)}), bf16[2,2,384,384]{3,2,1,0:T(8,128)(2,1)}) %reduce-scatter.30.cloned.1.call-update) | async-done | bytes 1179664 | tf_op jit(solution)/shard_map/reduce_scatter | solution.py:294
  1041.2 105.8 %reduce-scatter.32.cloned.1.call-done = f32[2,48,256]{2,1,0:T(8,128)} async-done(((f32[2,1536,256]{2,1,0:T(8,128)}), f32[2,48,256]{2,1,0:T(8,128)}) %reduce-scatter.32.cloned.1.call-update) | async-done | bytes 98320 | tf_op jit(solution)/shard_map/reduce_scatter | solution.py:308
  (900 shorter events, 309.5 us)
Async XLA Ops:
  7.3 39.5 %all-gather.7.cloned.1.call-start = ((), (), s32[]{:S(2)}) async-start(), calls=%async_computation.11 | async-start | bytes 3538944 | tf_op jit(solution)/shard_map/all_gather | solution.py:133
  8.2 164.0 %copy-start.121 = (f32[1536]{0:T(1024)}, f32[1536]{0:T(1024)S(1)}, u32[]{:S(2)}) copy-start(f32[1536]{0:T(1024)S(1)} %get-tuple-element.730) | copy-start | bytes 18436
  9.5 37.3 %copy-start.60 = (bf16[2,1536,256]{2,1,0:T(8,128)(2,1)S(1)}, bf16[2,1536,256]{2,1,0:T(8,128)(2,1)}, u32[]{:S(2)}) copy-start(bf16[2,1536,256]{2,1,0:T(8,128)(2,1)} %param.34) | copy-start | bytes 4718596
  11.7 159.3 %reduce-scatter.18.cloned.1.call-start = ((), (), s32[]{:S(2)}) async-start(), calls=%async_computation.12 | async-start | bytes 3538944 | tf_op jit(solution)/shard_map/reduce_scatter | solution.py:156
  18.2 200.1 %copy-start.124 = (f32[4,256]{1,0:T(4,128)}, f32[4,256]{1,0:T(4,128)S(1)}, u32[]{:S(2)}) copy-start(f32[4,256]{1,0:T(4,128)S(1)} %get-tuple-element.927) | copy-start | bytes 12292
  19.7 33.2 %copy-start.112 = (bf16[1,1536,6]{1,0,2:T(2,128)(2,1)}, bf16[1,1536,6]{1,0,2:T(2,128)(2,1)S(1)}, u32[]{:S(2)}) copy-start(bf16[1,1536,6]{1,0,2:T(2,128)(2,1)S(1)} %get-tuple-element.908) | copy-start | bytes 55300
  19.7 186.6 %copy-start.114 = (bf16[1,1536,6]{1,0,2:T(2,128)(2,1)}, bf16[1,1536,6]{1,0,2:T(2,128)(2,1)S(1)}, u32[]{:S(2)}) copy-start(bf16[1,1536,6]{1,0,2:T(2,128)(2,1)S(1)} %get-tuple-element.907) | copy-start | bytes 55300
  19.7 30.0 %copy-start.174 = (f32[1,1,256]{2,1,0:T(1,128)S(1)}, f32[1,1,256]{2,1,0:T(1,128)}, u32[]{:S(2)}) copy-start(f32[1,1,256]{2,1,0:T(1,128)} %get-tuple-element.924) | copy-start | bytes 3076
  19.7 30.0 %copy-start.176 = (f32[1,1,256]{2,1,0:T(1,128)S(1)}, f32[1,1,256]{2,1,0:T(1,128)}, u32[]{:S(2)}) copy-start(f32[1,1,256]{2,1,0:T(1,128)} %get-tuple-element.921) | copy-start | bytes 3076
  19.7 30.0 %copy-start.178 = (f32[1,1,256]{2,1,0:T(1,128)S(1)}, f32[1,1,256]{2,1,0:T(1,128)}, u32[]{:S(2)}) copy-start(f32[1,1,256]{2,1,0:T(1,128)} %get-tuple-element.922) | copy-start | bytes 3076
  19.7 30.0 %copy-start.180 = (f32[1,1,256]{2,1,0:T(1,128)S(1)}, f32[1,1,256]{2,1,0:T(1,128)}, u32[]{:S(2)}) copy-start(f32[1,1,256]{2,1,0:T(1,128)} %get-tuple-element.923) | copy-start | bytes 3076
  19.7 30.0 %copy-start.226 = (f32[1,256]{1,0:T(1,128)S(1)}, f32[1,256]{1,0:T(1,128)}, u32[]{:S(2)}) copy-start(f32[1,256]{1,0:T(1,128)} %get-tuple-element.933) | copy-start | bytes 3076
  63.2 30.5 %copy-start.88 = (f32[4,256,6]{1,2,0:T(8,128)}, f32[4,256,6]{1,2,0:T(8,128)S(1)}, u32[]{:S(2)}) copy-start(f32[4,256,6]{1,2,0:T(8,128)S(1)} %get-tuple-element.916) | copy-start | bytes 73732
  70.9 22.8 %copy-start.4 = (f32[4,256,6,64]{1,0,3,2:T(4,128)}, f32[4,256,6,64]{1,0,3,2:T(4,128)S(1)}, u32[]{:S(2)}) copy-start(f32[4,256,6,64]{1,0,3,2:T(4,128)S(1)} %reshape_reshape.6) | copy-start | bytes 4718596
  124.7 46.2 %copy-start.19 = (f32[128,1536]{1,0:T(8,128)S(1)}, f32[128,1536]{1,0:T(8,128)}, u32[]{:S(2)}) copy-start(f32[128,1536]{1,0:T(8,128)} %param.29) | copy-start | bytes 2359300
  124.7 81.5 %copy-start.201 = (f32[6]{0:T(128)S(1)}, f32[6]{0:T(128)}, u32[]{:S(2)}) copy-start(f32[6]{0:T(128)} %get-tuple-element.953) | copy-start | bytes 76
  124.7 81.5 %copy-start.211 = (f32[6]{0:T(128)S(1)}, f32[6]{0:T(128)}, u32[]{:S(2)}) copy-start(f32[6]{0:T(128)} %get-tuple-element.938) | copy-start | bytes 76
  124.7 81.5 %all-gather.9.cloned.1.call-start = ((), (), s32[]{:S(2)}) async-start(), calls=%async_computation.13 | async-start | bytes 3538944 | tf_op jit(solution)/shard_map/all_gather | solution.py:133
  172.1 37.7 %copy-start.247 = (f32[128]{0:T(128)}, f32[128]{0:T(128)S(1)}, u32[]{:S(2)}) copy-start(f32[128]{0:T(128)S(1)} %get-tuple-element.864) | copy-start | bytes 1540
  172.1 37.7 %copy-start.209 = (f32[128]{0:T(128)}, f32[128]{0:T(128)S(1)}, u32[]{:S(2)}) copy-start(f32[128]{0:T(128)S(1)} %add_rsqrt_fusion.2) | copy-start | bytes 1540
  173.9 166.4 %reduce-scatter.20.cloned.1.call-start = ((), (), s32[]{:S(2)}) async-start(), calls=%async_computation.14 | async-start | bytes 3538944 | tf_op jit(solution)/shard_map/reduce_scatter | solution.py:156
  209.8 27.1 %copy-start.72 = (f32[1024,6]{0,1:T(8,128)}, f32[1024,6]{0,1:T(8,128)S(1)}, u32[]{:S(2)}) copy-start(f32[1024,6]{0,1:T(8,128)S(1)} %get-tuple-element.909) | copy-start | bytes 73732
  218.7 34.1 %copy-start.150 = (f32[4,6,256]{2,1,0:T(8,128)}, f32[4,6,256]{2,1,0:T(8,128)S(1)}, u32[]{:S(2)}) copy-start(f32[4,6,256]{2,1,0:T(8,128)S(1)} %get-tuple-element.915) | copy-start | bytes 73732
  218.7 43.5 %copy-start.90 = (f32[4,256,6]{1,2,0:T(8,128)}, f32[4,256,6]{1,2,0:T(8,128)S(1)}, u32[]{:S(2)}) copy-start(f32[4,256,6]{1,2,0:T(8,128)S(1)} %get-tuple-element.913) | copy-start | bytes 73732
  294.1 95.9 %all-gather.11.cloned.1.call-start = ((), (), s32[]{:S(2)}) async-start(), calls=%async_computation.15 | async-start | bytes 3538944 | tf_op jit(solution)/shard_map/all_gather | solution.py:188
  343.3 181.4 %reduce-scatter.24.cloned.1.call-start = ((), (), s32[]{:S(2)}) async-start(), calls=%async_computation.17 | async-start | bytes 589824 | tf_op jit(solution)/shard_map/reduce_scatter | solution.py:208
  450.6 119.2 %reduce-scatter.22.cloned.1.call-start = ((), (), s32[]{:S(2)}) async-start(), calls=%async_computation.16 | async-start | bytes 3538944 | tf_op jit(solution)/shard_map/reduce_scatter | solution.py:205
  483.1 32.5 %copy-start.111 = (f32[1024,6]{0,1:T(8,128)S(1)}, f32[1024,6]{0,1:T(8,128)}, u32[]{:S(2)}) copy-start(f32[1024,6]{0,1:T(8,128)} %get-tuple-element.944) | copy-start | bytes 73732
  483.1 32.5 %copy-start.202 = (f32[6]{0:T(128)S(1)}, f32[6]{0:T(128)}, u32[]{:S(2)}) copy-start(f32[6]{0:T(128)} %get-tuple-element.953) | copy-start | bytes 76
  483.1 33.2 %copy-start.115 = (bf16[1,1536,6]{1,0,2:T(2,128)(2,1)S(1)}, bf16[1,1536,6]{1,0,2:T(2,128)(2,1)}, u32[]{:S(2)}) copy-start(bf16[1,1536,6]{1,0,2:T(2,128)(2,1)} %copy-done.114) | copy-start | bytes 55300
  523.7 46.2 %copy-start.33 = (f32[128,1536]{1,0:T(8,128)S(1)}, f32[128,1536]{1,0:T(8,128)}, u32[]{:S(2)}) copy-start(f32[128,1536]{1,0:T(8,128)} %copy-done.32) | copy-start | bytes 2359300
  523.7 46.2 %copy-start.62 = (bf16[2,1536,256]{2,1,0:T(8,128)(2,1)S(1)}, bf16[2,1536,256]{2,1,0:T(8,128)(2,1)}, u32[]{:S(2)}) copy-start(bf16[2,1536,256]{2,1,0:T(8,128)(2,1)} %param.34) | copy-start | bytes 4718596
  523.7 46.2 %copy-start.122 = (f32[1536]{0:T(1024)S(1)}, f32[1536]{0:T(1024)}, u32[]{:S(2)}) copy-start(f32[1536]{0:T(1024)} %copy-done.121) | copy-start | bytes 18436
  523.7 46.2 %copy-start.210 = (f32[128]{0:T(128)S(1)}, f32[128]{0:T(128)}, u32[]{:S(2)}) copy-start(f32[128]{0:T(128)} %copy-done.209) | copy-start | bytes 1540
  523.7 48.3 %copy-start.248 = (f32[128]{0:T(128)S(1)}, f32[128]{0:T(128)}, u32[]{:S(2)}) copy-start(f32[128]{0:T(128)} %copy-done.247) | copy-start | bytes 1540
  523.7 48.3 %copy-start.67 = (bf16[128,1536]{1,0:T(8,128)(2,1)S(1)}, bf16[128,1536]{1,0:T(8,128)(2,1)}, u32[]{:S(2)}) copy-start(bf16[128,1536]{1,0:T(8,128)(2,1)} %reduce-scatter.20.cloned.1.call-done) | copy-start | bytes 1179652
  523.7 83.6 %all-gather.13.cloned.1.call-start = ((), (), s32[]{:S(2)}) async-start(), calls=%async_computation.18 | async-start | bytes 3538944 | tf_op jit(solution)/shard_map/all_gather | solution.py:188
  574.9 199.3 %reduce-scatter.28.cloned.1.call-start = ((), (), s32[]{:S(2)}) async-start(), calls=%async_computation.20 | async-start | bytes 589824 | tf_op jit(solution)/shard_map/reduce_scatter | solution.py:208
  661.5 117.4 %reduce-scatter.26.cloned.1.call-start = ((), (), s32[]{:S(2)}) async-start(), calls=%async_computation.19 | async-start | bytes 3538944 | tf_op jit(solution)/shard_map/reduce_scatter | solution.py:205
  692.6 32.5 %copy-start.110 = (f32[1024,6]{0,1:T(8,128)S(1)}, f32[1024,6]{0,1:T(8,128)}, u32[]{:S(2)}) copy-start(f32[1024,6]{0,1:T(8,128)} %get-tuple-element.942) | copy-start | bytes 73732
  692.6 32.5 %copy-start.145 = (f32[4,256,6]{1,2,0:T(8,128)S(1)}, f32[4,256,6]{1,2,0:T(8,128)}, u32[]{:S(2)}) copy-start(f32[4,256,6]{1,2,0:T(8,128)} %get-tuple-element.884) | copy-start | bytes 73732
  692.6 32.5 %copy-start.200 = (f32[6]{0:T(128)S(1)}, f32[6]{0:T(128)}, u32[]{:S(2)}) copy-start(f32[6]{0:T(128)} %get-tuple-element.952) | copy-start | bytes 76
  692.7 32.6 %copy-start.113 = (bf16[1,1536,6]{1,0,2:T(2,128)(2,1)S(1)}, bf16[1,1536,6]{1,0,2:T(2,128)(2,1)}, u32[]{:S(2)}) copy-start(bf16[1,1536,6]{1,0,2:T(2,128)(2,1)} %copy-done.112) | copy-start | bytes 55300
  732.7 120.3 %reduce-scatter.36.cloned.1.call-start = ((), (), s32[]{:S(2)}) async-start(), calls=%async_computation.24 | async-start | bytes 491520
  744.5 110.2 %reduce-scatter.38.cloned.1.call-start = ((), (), s32[]{:S(2)}) async-start(), calls=%async_computation.25 | async-start | bytes 2949120
  760.8 191.1 %reduce-scatter.34.cloned.1.call-start = ((), (), s32[]{:S(2)}) async-start(), calls=%async_computation.23 | async-start | bytes 811008
  782.7 255.7 %reduce-scatter.30.cloned.1.call-start = ((), (), s32[]{:S(2)}) async-start(), calls=%async_computation.21 | async-start | bytes 5898240 | tf_op jit(solution)/shard_map/reduce_scatter | solution.py:294
  787.2 359.8 %reduce-scatter.32.cloned.1.call-start = ((), (), s32[]{:S(2)}) async-start(), calls=%async_computation.22 | async-start | bytes 3244032 | tf_op jit(solution)/shard_map/reduce_scatter | solution.py:308
  (217 other events, 994.5 us)
Sparse Core Ops, SparseCore 0:
  11.8 34.9 all-gather.6
  124.8 46.0 reduce-scatter.17
  174.0 32.1 all-gather.8
  294.2 46.0 reduce-scatter.19
  343.4 32.1 all-gather.10
  450.7 34.1 reduce-scatter.23
  523.8 45.9 reduce-scatter.21
  575.1 32.1 all-gather.12
  661.6 34.0 reduce-scatter.27
  732.8 46.0 reduce-scatter.25
  781.1 20.7 reduce-scatter.35
  804.1 47.0 reduce-scatter.37
  856.3 95.5 reduce-scatter.33
  954.0 84.3 reduce-scatter.29
  1044.2 102.6 reduce-scatter.31
where the time goes:
time: 1170 us; the launch traced here: 1150 us
  waiting for transfers between devices  484 us (41%)
  matrix products  244 us (21%)
  other arithmetic  186 us (16%)
  local copies, waits for them, and re-layouts  116 us (10%)
  blocking collectives  104 us (9%)
  between operations  17.8 us (2%)
    reduce_scatter x1, waiting for transfers between devices, shards(): lax.psum_scatter(stacked[2], ('dp', 'tensor'), scatter_dimension=1, tiled...  106 us
    reduce_scatter x2, waiting for transfers between devices, forward_layer(): lax.psum_scatter((gate_scale[:, None] * jnp.dot(scaled_in, out_weight, pr...  92.3 us
    unnamed x18, waiting for transfers between devices  91.7 us
    reduce_scatter x1, waiting for transfers between devices, shards(): lax.psum_scatter(stacked[1].astype(jnp.bfloat16), 'dp', scatter_dimension...  85.2 us
    another operation x12, other arithmetic  75.7 us
    dot_general x8, matrix products, state_scan(): jnp.einsum('chts,cshp->cthp', decay_mat * scores[:, None], weighted, prec...  68 us
    dot_general x10, matrix products, contract_cols(): lax.dot_general(left, right, (((1,), (1,)), ((), ())), preferred_element_...  61.5 us
    all_gather x2, waiting for transfers between devices, forward_layer(): normed = lax.all_gather(normed_rows, 'tensor', axis=0, tiled=True)  59.3 us
  transfers between devices with their start and end apart: 15, of which 9 were waited for; matrix products, arithmetic and copies ran while one was open for 23% of the time, Pallas kernels for 0%

commit v1 on v0

v1 whole, which is shorter than its diff:
```python
import functools
import jax
import jax.numpy as jnp
from jax import lax
from jax.experimental import pallas as pl
from jax.experimental.pallas import tpu as pltpu

from jax.sharding import PartitionSpec as P

EPS = 1e-05
HIGH = lax.Precision.HIGHEST
F32 = jnp.float32
BF = jnp.bfloat16
VM = 60 * 1024 * 1024


def dot(a, b):
    return lax.dot_general(a, b, (((1,), (0,)), ((), ())), preferred_element_type=F32)


def dot_t(a, b):
    return lax.dot_general(a, b, (((1,), (1,)), ((), ())), preferred_element_type=F32)


def t_dot(a, b):
    return lax.dot_general(a, b, (((0,), (0,)), ((), ())), preferred_element_type=F32)


def exact(a, b):
    return lax.dot_general(
        a, b, (((1,), (0,)), ((), ())), preferred_element_type=F32, precision=HIGH
    )


def sigmoid(x):
    return 1.0 / (1.0 + jnp.exp(-x))


def softplus(x):
    return jnp.maximum(x, 0.0) + jnp.log1p(jnp.exp(-jnp.abs(x)))


def tiles_of(inner, width):
    return [
        (start, min(128, inner - start), start // width, min(128, inner - start) // width)
        for start in range(0, inner, 128)
    ]


def expand(cols, inner, width):
    rows = cols.shape[0]
    parts = []
    for _, wide, first, number in tiles_of(inner, width):
        lane = lax.broadcasted_iota(jnp.int32, (rows, wide), 1)
        value = jnp.broadcast_to(cols[:, first : first + 1], (rows, wide))
        for j in range(1, number):
            value = jnp.where(lane >= j * width, cols[:, first + j : first + j + 1], value)
        parts.append(value)
    return parts[0] if len(parts) == 1 else jnp.concatenate(parts, axis=1)


def head_sum_matrix(inner, heads, width):
    row = lax.broadcasted_iota(jnp.int32, (inner, heads), 0)
    col = lax.broadcasted_iota(jnp.int32, (inner, heads), 1)
    return ((row >= col * width) & (row < (col + 1) * width)).astype(BF)


def head_sum(value, inner, heads, width):
    ones = head_sum_matrix(inner, heads, width)
    high = value.astype(BF)
    low = (value - high.astype(F32)).astype(BF)
    return dot(high, ones) + dot(low, ones)


def head_split(tile, width, number):
    if number == 1:
        return tile
    lane = lax.broadcasted_iota(jnp.int32, tile.shape, 1)
    zero = jnp.zeros_like(tile)
    return jnp.concatenate(
        [
            jnp.where((lane >= j * width) & (lane < (j + 1) * width), tile, zero)
            for j in range(number)
        ],
        axis=0,
    )


def pair_mask(seg_col, seg_row):
    rows, cols = seg_col.shape[0], seg_row.shape[1]
    row = lax.broadcasted_iota(jnp.int32, (rows, cols), 0)
    col = lax.broadcasted_iota(jnp.int32, (rows, cols), 1)
    return (row >= col) & (seg_col == seg_row)


def lower_ones(size):
    row = lax.broadcasted_iota(jnp.int32, (size, size), 0)
    col = lax.broadcasted_iota(jnp.int32, (size, size), 1)
    return (row >= col).astype(F32)


def turned(value):
    return jnp.transpose(value)


def column_of(tile):
    rows = tile.shape[1]
    return jnp.transpose(jnp.broadcast_to(tile[0:1, :], (rows, rows)))[:, 0:1]


def tile_of(column):
    rows = column.shape[0]
    return jnp.transpose(jnp.broadcast_to(column, (rows, rows)))[0:8, :]


def forward_kernel(
    layer, heads, width, inner_all,
    nb_ref, meta_ref, segrow_ref, win_ref, wst_ref, wstep_ref, wout_ref,
    cw_ref, cb_ref, scw_ref, scb_ref, sb_ref, dl_ref, sk_ref, gg_ref,
    g_ref, v_ref, pv_ref, s_ref, ps_ref, d_ref, y_ref, sp_ref, part_ref, psq_ref,
    state, vbuf, sbuf,
):
    size, inner = g_ref.shape
    half = s_ref.shape[1] // 2
    at = slice(layer, layer + 1)

    @pl.when(pl.program_id(0) == 0)
    def _():
        state[...] = jnp.zeros_like(state)
        vbuf[...] = jnp.zeros_like(vbuf)
        sbuf[...] = jnp.zeros_like(sbuf)

    nb = nb_ref[...]
    gate = dot(nb, win_ref[0])
    g_ref[...] = gate
    value = dot(nb, win_ref[1])
    v_ref[...] = value.astype(BF)
    raw = dot(nb, wst_ref[...])
    s_ref[...] = raw.astype(BF)
    step_in = dot(nb, wstep_ref[...])
    d_ref[...] = step_in

    meta = meta_ref[...]

    def conv(buf, now, w_ref, b_row):
        buf[8:, :] = now
        total = b_row + w_ref[0:1, :] * now
        for k in range(1, w_ref.shape[0]):
            total = total + w_ref[k : k + 1, :] * (buf[8 - k : 8 - k + size, :] * meta[:, k : k + 1])
        buf[0:8, :] = now[size - 8 :, :]
        return total

    pre_v = conv(vbuf, value, cw_ref, cb_ref[at, :])
    pv_ref[...] = pre_v
    pre_s = conv(sbuf, raw, scw_ref, scb_ref[at, :])
    ps_ref[...] = pre_s
    x = pre_v * sigmoid(pre_v)
    st = pre_s * sigmoid(pre_s)
    b_mat = st[:, :half].astype(BF)
    c_mat = st[:, half:].astype(BF)
    dt = softplus(step_in + sb_ref[at, :])
    log_decay = -dt * jnp.exp(dl_ref[at, :])
    cum = exact(lower_ones(size), log_decay)
    cum_t = turned(cum)
    last = cum[size - 1 : size, :]
    xt = (x * expand(dt, inner, width)).astype(BF)
    from_state = jnp.exp(cum) * meta[:, 4:5]
    to_end = jnp.exp(last - cum) * meta[:, 5:6]
    carry = jnp.exp(last) * meta[0:1, 6:7]
    before = state[...]
    before_b = before.astype(BF)
    sp_ref[...] = before_b
    scores = dot_t(c_mat, b_mat)
    mask = pair_mask(meta[:, 0:1], segrow_ref[0:1, :])
    parts = []
    for start, wide, first, number in tiles_of(inner, width):
        mats = []
        for h in range(first, first + number):
            differ = cum[:, h : h + 1] - cum_t[h : h + 1, :]
            mats.append((jnp.exp(jnp.where(mask, differ, -1e30)) * scores).astype(BF))
        left = mats[0] if number == 1 else jnp.concatenate(mats, axis=1)
        parts.append(dot(left, head_split(xt[:, start : start + wide], width, number)))
    intra = parts[0] if len(parts) == 1 else jnp.concatenate(parts, axis=1)
    inter = dot(c_mat, before_b) * expand(from_state, inner, width)
    y = intra + inter + expand(sk_ref[at, :], inner, width) * x
    y_ref[...] = y
    ended = (xt.astype(F32) * expand(to_end, inner, width)).astype(BF)
    state[...] = expand(carry, inner, width) * before + t_dot(b_mat, ended)
    gated = y * (gate * sigmoid(gate))
    square = jnp.sum(gated * gated, axis=1, keepdims=True)
    psq_ref[...] = tile_of(square)
    scaled = (gated * gg_ref[at, :]).astype(BF)
    part_ref[...] = dot(scaled, wout_ref[...]).astype(BF)


def layer_block(shape, layer, buffered=True):
    block = (None,) + tuple(shape[1:])
    return pl.BlockSpec(
        block, lambda c: (layer,) + (0,) * (len(shape) - 1), pipeline_mode=pl.Buffered(1)
    )


def whole_block(shape):
    return pl.BlockSpec(tuple(shape), lambda c: (0,) * len(shape), pipeline_mode=pl.Buffered(1))


def forward_compute(layer, size, normed, meta, segrow, w):
    tokens, depth = normed.shape
    inner = w["inner_weight"].shape[3]
    heads = w["step_weight"].shape[2]
    width = inner // heads
    both = w["state_weight"].shape[2]
    half = both // 2
    count = tokens // size
    rows = lambda wide: pl.BlockSpec((size, wide), lambda c: (c, 0))
    kernel = functools.partial(forward_kernel, layer, heads, width, None)
    out = lambda wide, kind: jax.ShapeDtypeStruct((tokens, wide), kind)
    return pl.pallas_call(
        kernel,
        grid=(count,),
        out_shape=(
            out(inner, F32), out(inner, BF), out(inner, F32), out(both, BF), out(both, F32),
            out(heads, F32), out(inner, F32),
            jax.ShapeDtypeStruct((count, half, inner), BF),
            out(depth, BF),
            jax.ShapeDtypeStruct((count * 8, size), F32),
        ),
        in_specs=[
            rows(depth), rows(8), pl.BlockSpec((8, size), lambda c: (0, c)),
            layer_block(w["inner_weight"].shape, layer),
            layer_block(w["state_weight"].shape, layer),
            layer_block(w["step_weight"].shape, layer),
            layer_block(w["out_weight"].shape, layer),
            layer_block(w["conv_weight"].shape, layer),
            whole_block(w["conv_bias"].shape),
            layer_block(w["state_conv_weight"].shape, layer),
            whole_block(w["state_conv_bias"].shape),
            whole_block(w["step_bias"].shape),
            whole_block(w["decay_log"].shape),
            whole_block(w["skip_gain"].shape),
            whole_block(w["gate_gain"].shape),
        ],
        out_specs=(
            rows(inner), rows(inner), rows(inner), rows(both), rows(both), rows(heads), rows(inner),
            pl.BlockSpec((None, half, inner), lambda c: (c, 0, 0)),
            rows(depth),
            pl.BlockSpec((8, size), lambda c: (c, 0)),
        ),
        scratch_shapes=[
            pltpu.VMEM((half, inner), F32),
            pltpu.VMEM((size + 8, inner), F32),
            pltpu.VMEM((size + 8, both), F32),
        ],
        compiler_params=pltpu.CompilerParams(vmem_limit_bytes=VM),
        name="forward_mix",
    )(
        normed, meta, segrow, w["inner_weight"], w["state_weight"], w["step_weight"], w["out_weight"],
        w["conv_weight"], w["conv_bias"], w["state_conv_weight"], w["state_conv_bias"],
        w["step_bias"], w["decay_log"], w["skip_gain"], w["gate_gain"],
    )


def token_meta(segment, size):
    tokens = segment.shape[0]
    seg = segment.astype(F32)

    def back(k):
        return jnp.concatenate([jnp.full((k,), -1.0, F32), seg[:-k]])

    blocks = seg.reshape(-1, size)
    gone = jnp.full((1,), -1.0, F32)
    before = jnp.concatenate([gone, blocks[:-1, -1]])
    after = jnp.concatenate([blocks[1:, 0], gone])
    per = lambda v: jnp.broadcast_to(v[:, None], blocks.shape)
    end = per(blocks[:, -1])
    columns = [
        seg,
        (back(1) == seg).astype(F32),
        (back(2) == seg).astype(F32),
        (back(3) == seg).astype(F32),
        (blocks == per(before)).astype(F32).reshape(-1),
        (blocks == end).astype(F32).reshape(-1),
        (end == per(before)).astype(F32).reshape(-1),
        (blocks == per(after)).astype(F32).reshape(-1),
    ]
    rows = jnp.stack(columns)
    return rows.T, rows


def backward_kernel(
    layer, heads, width, inner_all,
    sent_ref, mean_ref, meta_ref, segrow_ref, g_ref, v_ref, pv_ref, s_ref, ps_ref, d_ref, y_ref, sp_ref,
    win_ref, wst_ref, wstep_ref, wout_ref,
    cw_ref, scw_ref, sb_ref, dl_ref, sk_ref, gg_ref,
    rg_ref, rv_ref, rs_ref, rd_ref, sc_ref, part_ref,
    gcw_ref, gcb_ref, gscw_ref, gscb_ref, ggg_ref, gsk_ref, gsb_ref, gdl_ref,
    state, vbuf, sbuf,
):
    size, inner = g_ref.shape
    half = s_ref.shape[1] // 2
    at = slice(layer, layer + 1)

    @pl.when(pl.program_id(0) == 0)
    def _():
        for ref in (state, vbuf, sbuf, gcw_ref, gcb_ref, gscw_ref, gscb_ref, ggg_ref, gsk_ref, gsb_ref, gdl_ref):
            ref[...] = jnp.zeros_like(ref)

    meta = meta_ref[...]
    sent = sent_ref[...]
    gate, y = g_ref[...], y_ref[...]
    gate_sig = sigmoid(gate)
    silu_gate = gate * gate_sig
    gated = y * silu_gate
    gain = gg_ref[at, :]
    sc_ref[...] = (gated * gain).astype(BF)
    grad_scaled = dot_t(sent, wout_ref[...])
    ggg_ref[...] += jnp.sum(grad_scaled * gated, axis=0, keepdims=True)
    grad_gated = grad_scaled * gain + (2.0 / inner_all) * column_of(mean_ref[...]) * gated
    rg = (grad_gated * y * (gate_sig * (1.0 + gate * (1.0 - gate_sig)))).astype(BF)
    rg_ref[...] = rg
    dy = grad_gated * silu_gate
    pre_v, pre_s = pv_ref[...], ps_ref[...]
    sig_v, sig_s = sigmoid(pre_v), sigmoid(pre_s)
    x = pre_v * sig_v
    st = pre_s * sig_s
    b_mat = st[:, :half].astype(BF)
    c_mat = st[:, half:].astype(BF)
    raw_step = d_ref[...] + sb_ref[at, :]
    dt = softplus(raw_step)
    rate = jnp.exp(dl_ref[at, :])
    log_decay = -dt * rate
    cum = exact(lower_ones(size), log_decay)
    cum_t = turned(cum)
    last = cum[size - 1 : size, :]
    dt_all = expand(dt, inner, width)
    skip_all = expand(sk_ref[at, :], inner, width)
    xt = (x * dt_all).astype(BF)
    dy_b = dy.astype(BF)
    from_state = expand(jnp.exp(cum) * meta[:, 4:5], inner, width)
    to_end = expand(jnp.exp(last - cum) * meta[:, 5:6], inner, width)
    carry = expand(jnp.exp(last) * meta[0:1, 6:7], inner, width)
    gsk_ref[...] += jnp.sum(dy * x, axis=0, keepdims=True)
    scores = dot_t(c_mat, b_mat)
    mask = pair_mask(meta[:, 0:1], segrow_ref[0:1, :])
    d_scores = jnp.zeros((size, size), F32)
    parts = []
    for start, wide, first, number in tiles_of(inner, width):
        dy_split = head_split(dy_b[:, start : start + wide], width, number)
        d_mats = dot_t(dy_split, xt[:, start : start + wide])
        mats = []
        for j in range(number):
            h = first + j
            differ = cum[:, h : h + 1] - cum_t[h : h + 1, :]
            decay = jnp.exp(jnp.where(mask, differ, -1e30))
            mats.append((decay * scores).astype(BF))
            d_scores = d_scores + d_mats[j * size : (j + 1) * size, :] * decay
        left = mats[0] if number == 1 else jnp.concatenate(mats, axis=0)
        parts.append(t_dot(left, dy_split))
    intra = parts[0] if len(parts) == 1 else jnp.concatenate(parts, axis=1)
    d_scores = d_scores.astype(BF)
    before = sp_ref[...]
    after = state[...]
    after_b = after.astype(BF)
    dy_in = (dy * from_state).astype(BF)
    ended = (xt.astype(F32) * to_end).astype(BF)
    from_later = dot(b_mat, after_b) * to_end
    d_xt = intra + from_later
    d_c = dot(d_scores, b_mat) + dot_t(dy_in, before)
    d_b = t_dot(d_scores, c_mat) + dot_t(ended, after_b)
    across = carry * jnp.sum(before.astype(F32) * after, axis=0, keepdims=True)
    state[...] = carry * after + t_dot(c_mat, dy_in)
    xt_f = xt.astype(F32)
    sums = head_sum(
        jnp.concatenate(
            [
                dy_b.astype(F32) * (y - skip_all * x) - xt_f * intra,
                xt_f * from_later,
                x * d_xt,
                jnp.broadcast_to(across, (8, inner)),
            ],
            axis=0,
        ),
        inner, heads, width,
    )
    seg_col, seg_row = meta[:, 0:1], segrow_ref[0:1, :]
    d_log = (
        exact(later_ones(seg_col, seg_row), sums[0:size])
        + exact(earlier_ones(seg_col, seg_row), sums[size : 2 * size])
        + sums[3 * size : 3 * size + 1]
    )
    d_step = sums[2 * size : 3 * size] - rate * d_log
    gdl_ref[...] += jnp.sum(d_log * log_decay, axis=0, keepdims=True)
    d_raw = d_step * sigmoid(raw_step)
    gsb_ref[...] += jnp.sum(d_raw, axis=0, keepdims=True)
    rd = d_raw.astype(BF)
    rd_ref[...] = rd
    d_x = dy * skip_all + d_xt * dt_all
    d_pre_v = d_x * (sig_v * (1.0 + pre_v * (1.0 - sig_v)))
    d_st = jnp.concatenate([d_b, d_c], axis=1)
    d_pre_s = d_st * (sig_s * (1.0 + pre_s * (1.0 - sig_s)))

    def conv(buf, now, w_ref, value, gw_ref, gb_ref):
        taps = w_ref.shape[0]
        gb_ref[...] += jnp.sum(now, axis=0, keepdims=True)
        total = w_ref[0:1, :] * now
        gw_ref[0:1, :] += jnp.sum(now * value, axis=0, keepdims=True)
        for k in range(1, taps):
            kept = now * meta[:, k : k + 1]
            buf[k - 1, 0:size, :] = kept
            moved = buf[k - 1, k : k + size, :]
            buf[k - 1, size : size + 8, :] = kept[0:8, :]
            total = total + w_ref[k : k + 1, :] * moved
            gw_ref[k : k + 1, :] += jnp.sum(moved * value, axis=0, keepdims=True)
        return total

    rv = conv(vbuf, d_pre_v, cw_ref, v_ref[...].astype(F32), gcw_ref, gcb_ref).astype(BF)
    rv_ref[...] = rv
    rs = conv(sbuf, d_pre_s, scw_ref, s_ref[...].astype(F32), gscw_ref, gscb_ref).astype(BF)
    rs_ref[...] = rs
    total = dot_t(rg, win_ref[0]) + dot_t(rv, win_ref[1]) + dot_t(rs, wst_ref[...]) + dot_t(rd, wstep_ref[...])
    part_ref[...] = total.astype(BF)


def later_ones(seg_col, seg_row):
    rows, cols = seg_col.shape[0], seg_row.shape[1]
    row = lax.broadcasted_iota(jnp.int32, (rows, cols), 0)
    col = lax.broadcasted_iota(jnp.int32, (rows, cols), 1)
    return ((row <= col) & (seg_col == seg_row)).astype(F32)


def earlier_ones(seg_col, seg_row):
    rows, cols = seg_col.shape[0], seg_row.shape[1]
    row = lax.broadcasted_iota(jnp.int32, (rows, cols), 0)
    col = lax.broadcasted_iota(jnp.int32, (rows, cols), 1)
    return ((row > col) & (seg_col == seg_row)).astype(F32)


def backward_compute(layer, size, inner_all, sent, mean, meta, segrow, saved, w):
    g, v, pv, s, ps, d, y, sp = saved
    tokens, depth = sent.shape
    inner = w["inner_weight"].shape[3]
    heads = w["step_weight"].shape[2]
    width = inner // heads
    both = w["state_weight"].shape[2]
    half = both // 2
    taps = w["conv_weight"].shape[1]
    count = tokens // size
    rows = lambda wide: pl.BlockSpec((size, wide), lambda c: (count - 1 - c, 0))
    kernel = functools.partial(backward_kernel, layer, heads, width, inner_all)
    out = lambda wide, kind: jax.ShapeDtypeStruct((tokens, wide), kind)
    small = [(taps, inner), (1, inner), (taps, both), (1, both), (1, inner), (1, inner), (1, heads), (1, heads)]
    return pl.pallas_call(
        kernel,
        grid=(count,),
        out_shape=(
            out(inner, BF), out(inner, BF), out(both, BF), out(heads, BF), out(inner, BF), out(depth, BF),
            *[jax.ShapeDtypeStruct(shape, F32) for shape in small],
        ),
        in_specs=[
            rows(depth), pl.BlockSpec((8, size), lambda c: (count - 1 - c, 0)), rows(8),
            pl.BlockSpec((8, size), lambda c: (0, count - 1 - c)),
            rows(inner), rows(inner), rows(inner), rows(both), rows(both), rows(heads), rows(inner),
            pl.BlockSpec((None, half, inner), lambda c: (count - 1 - c, 0, 0)),
            layer_block(w["inner_weight"].shape, layer),
            layer_block(w["state_weight"].shape, layer),
            layer_block(w["step_weight"].shape, layer),
            layer_block(w["out_weight"].shape, layer),
            layer_block(w["conv_weight"].shape, layer),
            layer_block(w["state_conv_weight"].shape, layer),
            whole_block(w["step_bias"].shape),
            whole_block(w["decay_log"].shape),
            whole_block(w["skip_gain"].shape),
            whole_block(w["gate_gain"].shape),
        ],
        out_specs=(
            rows(inner), rows(inner), rows(both), rows(heads), rows(inner), rows(depth),
            *[pl.BlockSpec(shape, lambda c: (0, 0)) for shape in small],
        ),
        scratch_shapes=[
            pltpu.VMEM((half, inner), F32),
            pltpu.VMEM((taps - 1, size + 8, inner), F32),
            pltpu.VMEM((taps - 1, size + 8, both), F32),
        ],
        compiler_params=pltpu.CompilerParams(vmem_limit_bytes=VM),
        name="backward_mix",
    )(
        sent, mean, meta, segrow, g, v, pv, s, ps, d, y, sp,
        w["inner_weight"], w["state_weight"], w["step_weight"], w["out_weight"],
        w["conv_weight"], w["state_conv_weight"],
        w["step_bias"], w["decay_log"], w["skip_gain"], w["gate_gain"],
    )


def weight_kernel(normed_ref, sent_ref, sc_ref, rg_ref, rv_ref, rs_ref, rd_ref, gin_ref, gst_ref, gsd_ref, gout_ref):
    nb = normed_ref[...]
    gin_ref[0] = t_dot(nb, rg_ref[...]).astype(BF)
    gin_ref[1] = t_dot(nb, rv_ref[...]).astype(BF)
    gst_ref[...] = t_dot(nb, rs_ref[...]).astype(BF)
    gsd_ref[...] = t_dot(nb, rd_ref[...]).astype(BF)
    gout_ref[...] = t_dot(sc_ref[...], sent_ref[...]).astype(BF)


def weight_compute(normed, sent, sc, rg, rv, rs, rd):
    tokens, depth = normed.shape
    inner, both, heads = rg.shape[1], rs.shape[1], rd.shape[1]
    step = 256
    whole = lambda wide: pl.BlockSpec((tokens, wide), lambda i: (0, 0), pipeline_mode=pl.Buffered(1))
    cols = pl.BlockSpec((tokens, step), lambda i: (0, i))
    return pl.pallas_call(
        weight_kernel,
        grid=(depth // step,),
        out_shape=(
            jax.ShapeDtypeStruct((2, depth, inner), BF),
            jax.ShapeDtypeStruct((depth, both), BF),
            jax.ShapeDtypeStruct((depth, heads), BF),
            jax.ShapeDtypeStruct((inner, depth), BF),
        ),
        in_specs=[cols, cols, whole(inner), whole(inner), whole(inner), whole(both), whole(heads)],
        out_specs=(
            pl.BlockSpec((2, step, inner), lambda i: (0, i, 0)),
            pl.BlockSpec((step, both), lambda i: (i, 0)),
            pl.BlockSpec((step, heads), lambda i: (i, 0)),
            pl.BlockSpec((inner, step), lambda i: (0, i)),
        ),
        compiler_params=pltpu.CompilerParams(vmem_limit_bytes=VM),
        name="weight_grads",
    )(normed, sent, sc, rg, rv, rs, rd)


AXIS = "tensor"


def span_of(dims):
    found = [0]
    for d in dims:
        found = found + [r ^ d for r in found]
    return found


class Exchange:
    def __init__(self, size):
        self.size = size
        links = [1 << b for b in range(1, size.bit_length() - 1)]
        self.links = links
        self.orders = [links, links[::-1]]
        self.offsets = sorted(span_of(links), key=lambda r: -bin(r).count("1"))

    def reduce_steps(self, q):
        order = self.orders[q]
        steps = []
        for i, d in enumerate(order):
            for s in sorted(span_of(order[i + 1 :]), key=lambda r: -bin(r).count("1")):
                steps.append((i, d ^ s))
        return steps + [(len(order), 0)]

    def gather_dims(self, q):
        return self.orders[q] + [1]

    def gather_last(self, q, r):
        dims = self.gather_dims(q)
        return max([i for i, d in enumerate(dims) if r & d], default=-1)

    def gather_steps(self, q):
        dims = self.gather_dims(q)
        found = [r for r in range(1, self.size)]
        return sorted(found, key=lambda r: (self.gather_last(q, r), r & (r - 1) != 0))


def remote(src, dst, send, recv, target):
    return pltpu.make_async_remote_copy(
        src_ref=src, dst_ref=dst, send_sem=send, recv_sem=recv,
        device_id={AXIS: target}, device_id_type=pl.DeviceIdType.MESH,
    )


def greet(targets):
    barrier = pltpu.get_barrier_semaphore()
    for target in targets:
        pl.semaphore_signal(barrier, inc=1, device_id={AXIS: target}, device_id_type=pl.DeviceIdType.MESH)
    pl.semaphore_wait(barrier, len(targets))


def block_rows(block, rows, half, q):
    return pl.ds(pl.multiple_of(block * rows + q * half, half), half)


def comm_kernel(ex, rows, spec, middle, *refs):
    refs = list(refs)
    take = lambda k: [refs.pop(0) for _ in range(k)]
    part_ref = take(1)[0] if spec["reduce"] else None
    psq_ref = take(1)[0] if spec["squares"] else None
    ins = take(spec["n_in"])
    out_ref = take(1)[0] if spec["gather"] else None
    mean_out = take(1)[0] if spec["means"] else None
    outs = take(spec["n_out"])
    me = lax.axis_index(AXIS)
    n = ex.size
    half = rows // 2
    peers = [me ^ r for r in range(1, n)]
    partners = peers if (spec["squares"] or spec["means"]) else [me ^ d for d in ex.links + [1]]
    greet(partners)
    pending = []

    total = None
    if spec["reduce"]:
        own, pair, stage, got = take(4)
        load_sem, pair_send, pair_recv, link_send, link_recv = take(5)
        if spec["squares"]:
            sq_buf, sq_send, sq_recv = take(3)
        slot_of = {r: i for i, r in enumerate(ex.offsets)}
        loads = {}
        for r in ex.offsets:
            i = slot_of[r]
            loads[r] = pltpu.make_async_copy(
                part_ref.at[pl.ds(pl.multiple_of((me ^ r) * rows, rows), rows), :], own.at[i], load_sem.at[i]
            )
            loads[r].start()
        pairs = {}
        for r in ex.offsets:
            i = slot_of[r]
            pairs[r] = remote(
                part_ref.at[pl.ds(pl.multiple_of((me ^ r ^ 1) * rows, rows), rows), :], pair.at[i],
                pair_send.at[i], pair_recv.at[i], me ^ 1,
            )
            pairs[r].start()
        squares = []
        if spec["squares"]:
            for r in range(1, n):
                copy = remote(
                    psq_ref.at[pl.ds(pl.multiple_of((me ^ r) * 8, 8), 8), :], sq_buf.at[r],
                    sq_send.at[r], sq_recv.at[r], me ^ r,
                )
                copy.start()
                squares.append(copy)
        ready = set()
        index = {}
        for q in range(2):
            for i, r in ex.reduce_steps(q):
                for j in range(i):
                    index[(q, j, r)] = len(index)
        arrivals = {}
        steps = [ex.reduce_steps(q) for q in range(2)]
        final = [None, None]
        for k in range(len(steps[0])):
            for q in range(2):
                i, r = steps[q][k]
                if r not in ready:
                    loads[r].wait()
                    pairs[r].wait_recv()
                    ready.add(r)
                piece = pl.ds(q * half, half)
                value = own[slot_of[r], piece, :].astype(F32) + pair[slot_of[r], piece, :].astype(F32)
                for j in range(i):
                    arrivals[(q, j, r)].wait_recv()
                    value = value + got[index[(q, j, r)]].astype(F32)
                if r == 0:
                    final[q] = value
                    continue
                d = ex.orders[q][i]
                s = q * (n // 2) + slot_of[r]
                stage[s] = value.astype(BF)
                at = index[(q, i, r ^ d)]
                copy = remote(stage.at[s], got.at[at], link_send.at[s], link_recv.at[at], me ^ d)
                copy.start()
                arrivals[(q, i, r ^ d)] = copy
                pending.append(copy)
        total = jnp.concatenate(final, axis=0)
        pending.extend(pairs.values())
        square = None
        if spec["squares"]:
            square = psq_ref[pl.ds(pl.multiple_of(me * 8, 8), 8), :]
            for r, copy in enumerate(squares, 1):
                copy.wait_recv()
                square = square + sq_buf[r]
            pending.extend(squares)
    result = middle(total, column_of(square) if spec["squares"] else None, ins, outs)
    if spec["gather"]:
        row_buf, own_sem, send_sem, recv_sem = take(4)
        sent_rows, mean = result
        row_buf[...] = sent_rows
        copies = {}

        def forward(q, r):
            dims = ex.gather_dims(q)
            block = me ^ r
            place = block_rows(block, rows, half, q)
            src = row_buf.at[pl.ds(q * half, half), :] if r == 0 else out_ref.at[place, :]
            return [
                (i, remote(src, out_ref.at[place, :], send_sem.at[q, r ^ dims[i]], recv_sem.at[q, r ^ dims[i]], me ^ dims[i]), r ^ dims[i])
                for i in range(ex.gather_last(q, r) + 1, len(dims))
            ]

        first = [forward(q, 0) for q in range(2)]
        for i in range(len(first[0])):
            for q in range(2):
                _, copy, r = first[q][i]
                copy.start()
                copies[(q, r)] = copy
        local = pltpu.make_async_copy(
            row_buf, out_ref.at[pl.ds(pl.multiple_of(me * rows, rows), rows), :], own_sem
        )
        local.start()
        mean_copies = []
        if spec["means"]:
            mean_buf, mean_send, mean_recv = take(3)
            tile = tile_of(mean)
            mean_buf[...] = tile
            mine = pl.ds(pl.multiple_of(me * 8, 8), 8)
            for r in range(1, n):
                copy = remote(mean_buf, mean_out.at[mine, :], mean_send.at[r], mean_recv.at[r], me ^ r)
                copy.start()
                mean_copies.append(copy)
            mean_out[mine, :] = tile
        steps = [ex.gather_steps(q) for q in range(2)]
        for k in range(len(steps[0])):
            for q in range(2):
                r = steps[q][k]
                copies[(q, r)].wait_recv()
                for _, copy, beyond in forward(q, r):
                    copy.start()
                    copies[(q, beyond)] = copy
        for copy in mean_copies:
            copy.wait()
        local.wait()
        for copy in copies.values():
            copy.wait_send()
    for copy in pending:
        copy.wait_send()


def comm_call(name, collective, ex, middle, part=None, psq=None, ins=(), outs=(), gather=None, means=False):
    n = ex.size
    spec = dict(reduce=part is not None, squares=psq is not None, gather=gather is not None, means=means, n_in=len(ins), n_out=len(outs))
    vm = pl.BlockSpec(memory_space=pltpu.VMEM)
    anywhere = pl.BlockSpec(memory_space=pl.ANY)
    operands, in_specs, out_shape, out_specs, scratch = [], [], [], [], []
    if part is not None:
        rows, depth = part.shape[0] // n, part.shape[1]
        operands.append(part)
        in_specs.append(anywhere)
    else:
        rows, depth = ins[0].shape
    if psq is not None:
        operands.append(psq)
        in_specs.append(vm)
    operands.extend(ins)
    in_specs.extend([vm] * len(ins))
    half = rows // 2
    dma = pltpu.SemaphoreType.DMA
    if part is not None:
        slots = n // 2
        scratch += [
            pltpu.VMEM((slots, rows, depth), BF), pltpu.VMEM((slots, rows, depth), BF),
            pltpu.VMEM((2 * slots, half, depth), BF), pltpu.VMEM((2 * (slots - 1), half, depth), BF),
            dma((slots,)), dma((slots,)), dma((slots,)), dma((2 * slots,)), dma((2 * (slots - 1),)),
        ]
        if psq is not None:
            scratch += [pltpu.VMEM((n, 8, rows), F32), dma((n,)), dma((n,))]
    if gather is not None:
        out_shape.append(jax.ShapeDtypeStruct((n * rows, gather), BF))
        out_specs.append(anywhere)
        if means:
            out_shape.append(jax.ShapeDtypeStruct((n * 8, rows), F32))
            out_specs.append(vm)
        scratch += [pltpu.VMEM((rows, gather), BF), dma, dma((2, n)), dma((2, n))]
        if means:
            scratch += [pltpu.VMEM((8, rows), F32), dma((n,)), dma((n,))]
    out_shape.extend(outs)
    out_specs.extend([vm] * len(outs))
    return pl.pallas_call(
        functools.partial(comm_kernel, ex, rows, spec, middle),
        out_shape=tuple(out_shape),
        in_specs=in_specs,
        out_specs=tuple(out_specs),
        scratch_shapes=scratch,
        compiler_params=pltpu.CompilerParams(collective_id=collective, has_side_effects=True, vmem_limit_bytes=VM),
        name=name,
    )(*operands)


LAYERS = 2
SIZE = 128
NAMES = (
    "norm_gain", "inner_weight", "state_weight", "step_weight", "step_bias", "decay_log", "skip_gain",
    "conv_weight", "conv_bias", "state_conv_weight", "state_conv_bias", "gate_gain", "out_weight",
)


def shape_of(rows, depth):
    return jax.ShapeDtypeStruct((rows, depth), F32)


def row_scale_of(resid):
    return lax.rsqrt(jnp.mean(resid * resid, axis=1, keepdims=True) + EPS)


def retile(tiles, count):
    width = tiles.shape[1]
    if tiles.shape[0] == count * 8:
        return tiles
    flat = tiles.reshape(-1, 8, width)[:, 0, :].reshape(count, 1, -1)
    return jnp.broadcast_to(flat, (count, 8, flat.shape[2])).reshape(count * 8, -1)


def gate_of(square, inner_all):
    return lax.rsqrt(square / inner_all + EPS)


def start_middle(layer, total, square, ins, outs):
    resid, gain = ins[0][...], ins[1][layer : layer + 1, :]
    return (resid * row_scale_of(resid) * gain).astype(BF), None


def between_middle(layer, inner_all, total, square, ins, outs):
    gate = gate_of(square, inner_all)
    mixed = gate * total
    hidden = ins[0][...] + mixed
    outs[0][...] = hidden
    outs[1][...] = mixed
    outs[2][...] = gate
    return (hidden * row_scale_of(hidden) * ins[1][layer : layer + 1, :]).astype(BF), None


def turn_middle(inner_all, total, square, ins, outs):
    gate = gate_of(square, inner_all)
    mixed = gate * total
    grad = ins[1][...]
    outs[0][...] = ins[0][...] + mixed
    mean = -0.5 * gate * gate * jnp.sum(mixed * grad, axis=1, keepdims=True)
    return (gate * grad).astype(BF), mean


def norm_backward(layer, total, resid, grad, gain):
    scale = row_scale_of(resid)
    weighted = total * gain
    inner = jnp.sum(weighted * resid, axis=1, keepdims=True)
    gain_grad = jnp.sum(total * resid * scale, axis=0, keepdims=True)
    fresh = grad + scale * weighted - resid * (scale * scale * scale * inner / resid.shape[1])
    return fresh, gain_grad


def back_middle(layer, total, square, ins, outs):
    fresh, gain_grad = norm_backward(layer, total, ins[0][...], ins[1][...], ins[2][layer : layer + 1, :])
    outs[0][...] = fresh
    outs[1][...] = gain_grad
    mixed, gate = ins[3][...], ins[4][...]
    mean = -0.5 * gate * gate * jnp.sum(mixed * fresh, axis=1, keepdims=True)
    return (gate * fresh).astype(BF), mean


def end_middle(layer, total, square, ins, outs):
    fresh, gain_grad = norm_backward(layer, total, ins[0][...], ins[1][...], ins[2][layer : layer + 1, :])
    outs[0][...] = fresh
    outs[1][...] = gain_grad
    return None


def shards(ex, residual, cotangent, segments, *weights):
    w = dict(zip(NAMES, weights))
    rows, depth = residual.shape
    tokens = segments.shape[1]
    inner = w["inner_weight"].shape[3]
    heads = w["step_weight"].shape[2]
    inner_all = inner * ex.size
    count = tokens // SIZE
    gain = w["norm_gain"]
    meta, segrow = token_meta(segments[0], SIZE)
    ids = iter(range(100))
    resids, mixeds, gates, normeds, saved = [residual], [], [], [], []
    (normed,) = comm_call(
        "rows_start", next(ids), ex, functools.partial(start_middle, 0), ins=(residual, gain), gather=depth
    )
    hidden = residual
    for layer in range(LAYERS):
        normeds.append(normed)
        made = forward_compute(layer, SIZE, normed, meta, segrow, w)
        saved.append(made[:8])
        part, squares = made[8:]
        squares = retile(squares, ex.size)
        if layer + 1 < LAYERS:
            normed, hidden, mixed, gate = comm_call(
                "rows_between", next(ids), ex, functools.partial(between_middle, layer + 1, inner_all),
                part=part, psq=squares, ins=(hidden, gain),
                outs=(shape_of(rows, depth), shape_of(rows, depth), shape_of(rows, 1)), gather=depth,
            )
            resids.append(hidden)
            mixeds.append(mixed)
            gates.append(gate)
        else:
            sent, mean, block_output = comm_call(
                "rows_turn", next(ids), ex, functools.partial(turn_middle, inner_all),
                part=part, psq=squares, ins=(hidden, cotangent), outs=(shape_of(rows, depth),), gather=depth, means=True,
            )
    grad = cotangent
    big, small = [None] * LAYERS, [None] * LAYERS
    for layer in range(LAYERS - 1, -1, -1):
        made = backward_compute(layer, SIZE, inner_all, sent, retile(mean, count), meta, segrow, saved[layer], w)
        rg, rv, rs, rd, sc, part = made[:6]
        g_inner, g_state, g_step, g_out = weight_compute(normeds[layer], sent, sc, rg, rv, rs, rd)
        scatter = lambda v, dim: lax.psum_scatter(v, "dp", scatter_dimension=dim, tiled=True).astype(F32)
        big[layer] = (
            scatter(g_inner, 1),
            lax.psum_scatter(g_state, ("dp", "tensor"), scatter_dimension=0, tiled=True).astype(F32),
            scatter(g_step, 0),
            scatter(g_out, 1),
        )
        if layer:
            sent, mean, grad, g_gain = comm_call(
                "rows_back", next(ids), ex, functools.partial(back_middle, layer), part=part,
                ins=(resids[layer], grad, gain, mixeds[layer - 1], gates[layer - 1]),
                outs=(shape_of(rows, depth), shape_of(1, depth)), gather=depth, means=True,
            )
        else:
            grad, g_gain = comm_call(
                "rows_end", next(ids), ex, functools.partial(end_middle, layer), part=part,
                ins=(resids[layer], grad, gain), outs=(shape_of(rows, depth), shape_of(1, depth)),
            )
        small[layer] = (made[6:], g_gain)
    per_dp = lax.psum(
        jnp.stack([jnp.concatenate([m[0], m[1], m[4], m[5]], axis=0) for m, _ in small]), "dp"
    )
    per_head = lax.psum(jnp.stack([jnp.concatenate([m[6], m[7]], axis=0) for m, _ in small]), "dp")
    everywhere = lax.psum(jnp.stack([jnp.concatenate([m[2], m[3]], axis=0) for m, _ in small]), ("dp", "tensor"))
    g_norm = lax.psum_scatter(
        jnp.concatenate([g for _, g in small], axis=0), ("dp", "tensor"), scatter_dimension=1, tiled=True
    )
    taps = w["conv_weight"].shape[1]
    stack = lambda k: jnp.stack([big[layer][k] for layer in range(LAYERS)])
    return (
        block_output,
        grad,
        g_norm,
        stack(0),
        stack(1),
        stack(2),
        per_head[:, 0],
        per_head[:, 1],
        per_dp[:, taps + 2].reshape(LAYERS, heads, -1).sum(2),
        per_dp[:, :taps],
        per_dp[:, taps],
        everywhere[:, :taps],
        everywhere[:, taps],
        per_dp[:, taps + 1],
        stack(3),
    )


def solution(mesh):
    ex = Exchange(mesh.shape["tensor"])
    return jax.shard_map(
        functools.partial(shards, ex),
        mesh=mesh,
        in_specs=(
            P(("dp", "tensor"), None),
            P(("dp", "tensor"), None),
            P("dp", None),
            P(),
            P(None, None, None, "tensor"),
            P(),
            P(None, None, "tensor"),
            P(None, "tensor"),
            P(None, "tensor"),
            P(None, "tensor"),
            P(None, None, "tensor"),
            P(None, "tensor"),
            P(),
            P(),
            P(None, "tensor"),
            P(None, "tensor", None),
        ),
        out_specs=(
            P(("dp", "tensor"), None),
            P(("dp", "tensor"), None),
            P(None, ("dp", "tensor")),
            P(None, None, "dp", "tensor"),
            P(None, ("dp", "tensor"), None),
            P(None, "dp", "tensor"),
            P(None, "tensor"),
            P(None, "tensor"),
            P(None, "tensor"),
            P(None, None, "tensor"),
            P(None, "tensor"),
            P(),
            P(),
            P(None, "tensor"),
            P(None, "tensor", "dp"),
        ),
        check_vma=False,
    )
```

time: 1170 us -> 794 us (0.68); the launches traced: 1150 us -> 792 us
  Pallas kernels: 0 us -> 288 us
  matrix products: 244 us -> 0 us
  other arithmetic: 186 us -> 9.16 us
  local copies, waits for them, and re-layouts: 116 us -> 19.5 us
  waiting for transfers between devices: 484 us -> 404 us
  blocking collectives: 104 us -> 57.4 us
    pallas_call x0 -> x11, Pallas kernels: none -> 288 us  [the longest x5 156 us: comm_call(): pl.pallas_call(functools.partial(comm_kernel, ex, rows, spec, middle), ou...]
    dot_general x60 -> x0, matrix products: 244 us -> none  [the longest x8 68 us: state_scan(): jnp.einsum('chts,cshp->cthp', decay_mat * scores[:, None], weighted, prec...]
    another operation x31 -> x14, other arithmetic: 87 us -> 6.18 us  [the longest x4 6.03 us: shards(): stack = lambda k: jnp.stack([big[layer][k] for layer in range(LAYERS)])]
    all_gather x4 -> x0, waiting for transfers between devices: 59.3 us -> none  [the longest x2 59.3 us: forward_layer(): normed = lax.all_gather(normed_rows, 'tensor', axis=0, tiled=True)]
    unnamed x526 -> x59, local copies, waits for them, and re-layouts: 47 us -> 14.1 us
    reduce_sum x30 -> x1, other arithmetic: 32.2 us -> 0.65 us  [shards(): per_dp[:, taps + 2].reshape(LAYERS, heads, -1).sum(2)]
    psum x4 -> x2, blocking collectives: 86.8 us -> 57.4 us  [the longest x1 39.7 us: shards(): lax.psum(jnp.stack([jnp.concatenate([m[2], m[3]], axis=0) for m, _ in sma...]
    reshape x22 -> x0, local copies, waits for them, and re-layouts: 24.4 us -> none  [the longest x6 17.9 us: state_scan(): return result.reshape(length, heads * width)]
  transfers between devices with their start and end apart: 15 -> 9, of which waited for: 9 -> 9; matrix products, arithmetic and copies ran while one was open for 23% -> 2% of each run, Pallas kernels for 0% -> 3%
where the time goes in v1:
time: 794 us; the launch traced here: 792 us
  waiting for transfers between devices  404 us (51%)
  Pallas kernels  288 us (36%)
  blocking collectives  57.4 us (7%)
  local copies, waits for them, and re-layouts  19.5 us (2%)
  between operations  14.3 us (2%)
  other arithmetic  9.16 us (1%)
    reduce_scatter x2, waiting for transfers between devices, shards(): lax.psum_scatter(g_state, ('dp', 'tensor'), scatter_dimension=0, tiled=True)  199 us
    pallas_call x5, Pallas kernels, comm_call(): pl.pallas_call(functools.partial(comm_kernel, ex, rows, spec, middle), ou...  156 us
    reduce_scatter x4, waiting for transfers between devices, shards(): lax.psum_scatter(v, 'dp', scatter_dimension=dim, tiled=True).astype(F32)  138 us
    pallas_call x2, Pallas kernels, backward_compute(): pl.pallas_call(kernel, grid=(count,), out_shape=(out(inner, BF), out(inne...  69.8 us
    unnamed x12, waiting for transfers between devices  67.7 us
    pallas_call x2, Pallas kernels, forward_compute(): pl.pallas_call(kernel, grid=(count,), out_shape=(out(inner, F32), out(inn...  39.8 us
    psum x1, blocking collectives, shards(): lax.psum(jnp.stack([jnp.concatenate([m[2], m[3]], axis=0) for m, _ in sma...  39.7 us
    pallas_call x2, Pallas kernels, weight_compute(): pl.pallas_call(weight_kernel, grid=(depth // step,), out_shape=(jax.Shape...  22.4 us
  transfers between devices with their start and end apart: 9, of which 9 were waited for; matrix products, arithmetic and copies ran while one was open for 2% of the time, Pallas kernels for 3%

profile of v1, /device:TPU:0, one launch (start us, length us, event | category | flops | bytes accessed | tf_op | source)
XLA Modules:
  0.0 792.5 jit_solution(9206820169725777725)
XLA Ops:
  7.2 0.7 convert_element_type.45
  8.8 0.8 compare_convert_fusion
  9.7 1.0 copy.58.meta_ref
  10.7 2.0 copy.59.wstep_ref
  12.7 20.9 %rows_start.1.nb_ref.normed_ref = bf16[1024,1536]{1,0:T(8,128)(2,1)} custom-call(f32[128,1536]{1,0:T(8,128)} %refs_1_.3, f32[2,1536]{1,0:T(2,128)} %refs_3_.7), custom_call_target="tpu_custom_call" | custom-call | tf_op jit(solution)/shard_map/rows_start/pallas_call | solution.py:770
  33.6 19.9 %forward_mix.2 = (f32[1024,384]{1,0:T(8,128)}, bf16[1024,384]{1,0:T(8,128)(2,1)}, f32[1024,384]{1,0:T(8,128)}, bf16[1024,256]{1,0:T(8,128)(2,1)}, f32[1024,256]{...) custom-call(bf16[1024,1536]{1,0:T(8,128)(2,1)} %rows_start.1.nb_ref., ...), custom_call_target="tpu_custom_call" | custom-call | tf_op jit(solution)/shard_map/forward_mix/pallas_call | solution.py:218
  53.5 37.8 %rows_between.1 = (bf16[1024,1536]{1,0:T(8,128)(2,1)}, f32[128,1536]{1,0:T(8,128)}, f32[128,1536]{1,0:T(8,128)}, f32[128,1]{1,0:T(8,128)}) custom-call(bf16[1024,1536]{1,0:T(8,128)(2,1)} %get-tuple-element.84.refs_0_, f32[64,128]{1,0:T(8,128)} %get-tuple-element.85.refs_1_, f32[128,1536]{1,0:T(8,128)} %refs_1_.3, f32[2,1536]{1,0:T(2,128)} %refs_3_.7), custom_call_target="tpu_custom_call" | custom-call | tf_op jit(solution)/shard_map/rows_between/pallas_call | solution.py:770
  91.2 19.9 %forward_mix.3 = (f32[1024,384]{1,0:T(8,128)}, bf16[1024,384]{1,0:T(8,128)(2,1)}, f32[1024,384]{1,0:T(8,128)}, bf16[1024,256]{1,0:T(8,128)(2,1)}, f32[1024,256]{...) custom-call(bf16[1024,1536]{1,0:T(8,128)(2,1)} %get-tuple-element.86, ...), custom_call_target="tpu_custom_call" | custom-call | tf_op jit(solution)/shard_map/forward_mix/pallas_call | solution.py:218
  111.2 38.1 %rows_turn.1 = (bf16[1024,1536]{1,0:T(8,128)(2,1)}, f32[64,128]{1,0:T(8,128)}, f32[128,1536]{1,0:T(8,128)}) custom-call(bf16[1024,1536]{1,0:T(8,128)(2,1)} %get-tuple-element.87.refs_0_, f32[64,128]{1,0:T(8,128)} %get-tuple-element.88.refs_1_, f32[128,1536]{1,0:T(8,128)} %get-tuple-element.89.refs_2_.refs_1_, f32[128,1536]{1,0:T(8,128)} %refs_2_.3), custom_call_target="tpu_custom_call" | custom-call | tf_op jit(solution)/shard_map/rows_turn/pallas_call | solution.py:770
  149.3 34.8 %backward_mix.2 = (bf16[1024,384]{1,0:T(8,128)(2,1)}, bf16[1024,384]{1,0:T(8,128)(2,1)}, bf16[1024,256]{1,0:T(8,128)(2,1)}, bf16[1024,6]{1,0:T(8,128)(2,1)}, bf1...) custom-call(bf16[1024,1536]{1,0:T(8,128)(2,1)} %get-tuple-element.91, ...), custom_call_target="tpu_custom_call" | custom-call | tf_op jit(solution)/shard_map/backward_mix/pallas_call | solution.py:452
  184.1 38.6 %rows_back.1 = (bf16[1024,1536]{1,0:T(8,128)(2,1)}, f32[64,128]{1,0:T(8,128)}, f32[128,1536]{1,0:T(8,128)}, f32[1,1536]{1,0:T(1,128)}) custom-call(bf16[1024,1536]{1,0:T(8,128)(2,1)} %get-tuple-element.101.refs_0_, f32[128,1536]{1,0:T(8,128)} %get-tuple-element.89.refs_2_.refs_1_, f32[128,1536]{1,0:T(8,128)} %refs_2_.3, f32[2,1536]{1,0:T(2,128)} %refs_3_.7, ...), custom_call_target="tpu_custom_call" | custom-call | tf_op jit(solution)/shard_map/rows_back/pallas_call | solution.py:770
  222.7 35.0 %backward_mix.3 = (bf16[1024,384]{1,0:T(8,128)(2,1)}, bf16[1024,384]{1,0:T(8,128)(2,1)}, bf16[1024,256]{1,0:T(8,128)(2,1)}, bf16[1024,6]{1,0:T(8,128)(2,1)}, bf1...) custom-call(bf16[1024,1536]{1,0:T(8,128)(2,1)} %get-tuple-element.10, ...), custom_call_target="tpu_custom_call" | custom-call | tf_op jit(solution)/shard_map/backward_mix/pallas_call | solution.py:452
  257.6 20.6 %rows_end.1 = (f32[128,1536]{1,0:T(8,128)}, f32[1,1536]{1,0:T(1,128)}) custom-call(bf16[1024,1536]{1,0:T(8,128)(2,1)} %get-tuple-element.114.refs_0_, f32[128,1536]{1,0:T(8,128)} %refs_1_.3, f32[128,1536]{1,0:T(8,128)} %get-tuple-element.115.refs_2_, f32[2,1536]{1,0:T(2,128)} %refs_3_.7), custom_call_target="tpu_custom_call" | custom-call | tf_op jit(solution)/shard_map/rows_end/pallas_call | solution.py:770
  278.3 0.7 pad_maximum_fusion.2
  279.0 1.2 copy.68
  280.2 11.2 %weight_grads.3 = (bf16[2,1536,384]{2,1,0:T(8,128)(2,1)}, bf16[1536,256]{1,0:T(8,128)(2,1)}, bf16[1536,6]{1,0:T(8,128)(2,1)}, bf16[384,1536]{1,0:T(8,128)(2,1)}) custom-call(bf16[1024,1536]{1,0:T(8,128)(2,1)} %get-tuple-element.86.nb_ref.normed_ref, bf16[1024,1536]{1,0:T(8,128)(2,1)} %get-tuple-element.91.sent_ref, ...), custom_call_target="tpu_custom_call" | custom-call | tf_op jit(solution)/shard_map/weight_grads/pallas_call | solution.py:509
  291.5 11.3 %weight_grads.2 = (bf16[2,1536,384]{2,1,0:T(8,128)(2,1)}, bf16[1536,256]{1,0:T(8,128)(2,1)}, bf16[1536,6]{1,0:T(8,128)(2,1)}, bf16[384,1536]{1,0:T(8,128)(2,1)}) custom-call(bf16[1024,1536]{1,0:T(8,128)(2,1)} %rows_start.1.nb_ref.normed_ref, bf16[1024,1536]{1,0:T(8,128)(2,1)} %get-tuple-element.104.sent_ref, bf16[1024,384]{1,0:T(8,128)(2,1)} %get-tuple-element.119.sc_ref, ...), custom_call_target="tpu_custom_call" | custom-call | tf_op jit(solution)/shard_map/weight_grads/pallas_call | solution.py:509
  304.0 1.4 copy.72
  305.5 1.4 copy.70
  307.0 0.7 reduce-scatter.18.cloned.1.call-update
  307.9 0.7 reduce-scatter.16.cloned.1.call-update
  308.7 39.7 %psum.23 = f32[2,5,256]{2,1,0:T(8,128)S(1)} all-reduce(f32[2,5,256]{2,1,0:T(8,128)S(1)} %pad_maximum_fusion.1), channel_id=1, replica_groups=mesh['dp'=4,'tensor'=8] {'dp','tensor'}, use_global_device_ids=true, to_apply=%region_10.0 | all-reduce | flops 2560 | bytes 20480 | tf_op jit(solution)/shard_map/psum | solution.py:923
  348.4 0.6 slice.73
  349.8 17.7 %all-reduce.2 = (f32[2,2,6]{2,1,0:T(2,128)S(1)}, f32[2,7,384]{2,1,0:T(8,128)S(1)}) all-reduce(f32[2,2,6]{2,1,0:T(2,128)S(1)} %pad_maximum_fusion.3, f32[2,7,384]{2,1,0:T(8,128)S(1)} %pad_maximum_fusion), channel_id=1, replica_groups=mesh['dp'=4,'tensor'=8] {'dp'}, use_global_device_ids=true, to_apply=%region_7.0 | all-reduce | flops 5400 | bytes 43200 | tf_op jit(solution)/shard_map/psum | solution.py:922
  367.5 0.6 slice.71
  368.1 0.6 copy.83
  368.7 0.6 copy.84
  369.4 0.7 reduce_sum.9
  370.6 6.3 reduce-scatter.28.cloned.1.call-done
  376.9 1.4 copy.69
  378.3 20.8 %reduce-scatter.26.cloned.1.call-done = bf16[384,6]{1,0:T(8,128)(2,1)} async-done(((bf16[1536,6]{1,0:T(8,128)(2,1)}), bf16[384,6]{1,0:T(8,128)(2,1)}) %reduce-scatter.26.cloned.1.call-update) | async-done | bytes 4624 | tf_op jit(solution)/shard_map/reduce_scatter | solution.py:900
  399.1 1.0 copy.67
  400.1 20.3 %reduce-scatter.24.cloned.1.call-done = bf16[384,6]{1,0:T(8,128)(2,1)} async-done(((bf16[1536,6]{1,0:T(8,128)(2,1)}), bf16[384,6]{1,0:T(8,128)(2,1)}) %reduce-scatter.24.cloned.1.call-update) | async-done | bytes 4624 | tf_op jit(solution)/shard_map/reduce_scatter | solution.py:900
  420.5 1.0 copy.66
  421.5 0.7 maximum_convert_fusion.3
  422.1 98.3 %reduce-scatter.22.cloned.1.call-done = bf16[48,256]{1,0:T(8,128)(2,1)} async-done(((bf16[1536,256]{1,0:T(8,128)(2,1)}), bf16[48,256]{1,0:T(8,128)(2,1)}) %reduce-scatter.22.cloned.1.call-update) | async-done | bytes 24592 | tf_op jit(solution)/shard_map/reduce_scatter | solution.py:903
  520.5 100.3 %reduce-scatter.20.cloned.1.call-done = bf16[48,256]{1,0:T(8,128)(2,1)} async-done(((bf16[1536,256]{1,0:T(8,128)(2,1)}), bf16[48,256]{1,0:T(8,128)(2,1)}) %reduce-scatter.20.cloned.1.call-update) | async-done | bytes 24592 | tf_op jit(solution)/shard_map/reduce_scatter | solution.py:903
  620.7 1.4 maximum_convert_fusion.2
  622.1 29.8 %reduce-scatter.32.cloned.1.call-done = bf16[384,384]{1,0:T(8,128)(2,1)} async-done(((bf16[1536,384]{1,0:T(8,128)(2,1)}), bf16[384,384]{1,0:T(8,128)(2,1)}) %reduce-scatter.32.cloned.1.call-update) | async-done | bytes 294928
  651.9 1.2 copy.73
  653.1 29.1 %reduce-scatter.30.cloned.1.call-done = bf16[384,384]{1,0:T(8,128)(2,1)} async-done(((bf16[1536,384]{1,0:T(8,128)(2,1)}), bf16[384,384]{1,0:T(8,128)(2,1)}) %reduce-scatter.30.cloned.1.call-update) | async-done | bytes 294928
  682.1 1.2 copy.71
  683.3 1.1 maximum_convert_fusion.1
  684.4 46.9 %reduce-scatter.18.cloned.1.call-done = bf16[2,384,384]{2,1,0:T(8,128)(2,1)} async-done(((bf16[2,1536,384]{2,1,0:T(8,128)(2,1)}), bf16[2,384,384]{2,1,0:T(8,128)(2,1)}) %reduce-scatter.18.cloned.1.call-update) | async-done | bytes 589840 | tf_op jit(solution)/shard_map/reduce_scatter | solution.py:900
  731.3 49.4 %reduce-scatter.16.cloned.1.call-done = bf16[2,384,384]{2,1,0:T(8,128)(2,1)} async-done(((bf16[2,1536,384]{2,1,0:T(8,128)(2,1)}), bf16[2,384,384]{2,1,0:T(8,128)(2,1)}) %reduce-scatter.16.cloned.1.call-update) | async-done | bytes 589840 | tf_op jit(solution)/shard_map/reduce_scatter | solution.py:900
  780.8 2.9 maximum_convert_fusion
  783.7 0.9 copy.88
  785.1 0.9 copy.89
  (87 shorter events, 4.5 us)
Async XLA Ops:
  7.2 369.8 %reduce-scatter.28.cloned.1.call-start = ((), (), s32[]{:S(2)}) async-start(), calls=%async_computation.15 | async-start | bytes 811008
  9.7 23.9 %copy-start = (f32[8,1024]{1,0:T(8,128)}, f32[8,1024]{1,0:T(8,128)S(1)}, u32[]{:S(2)}) copy-start(f32[8,1024]{1,0:T(8,128)S(1)} %stack.104.segrow_ref) | copy-start | bytes 98308
  257.6 20.6 %copy-start.7 = (f32[1,1536]{1,0:T(1,128)S(1)}, f32[1,1536]{1,0:T(1,128)}, u32[]{:S(2)}) copy-start(f32[1,1536]{1,0:T(1,128)} %get-tuple-element.118) | copy-start | bytes 18436
  280.2 118.9 %reduce-scatter.26.cloned.1.call-start = ((), (), s32[]{:S(2)}) async-start(), calls=%async_computation.14 | async-start | bytes 491520 | tf_op jit(solution)/shard_map/reduce_scatter | solution.py:900
  291.4 129.0 %reduce-scatter.24.cloned.1.call-start = ((), (), s32[]{:S(2)}) async-start(), calls=%async_computation.13 | async-start | bytes 491520 | tf_op jit(solution)/shard_map/reduce_scatter | solution.py:900
  302.7 1.3 copy-start.1
  302.8 217.7 %reduce-scatter.22.cloned.1.call-start = ((), (), s32[]{:S(2)}) async-start(), calls=%async_computation.12 | async-start | bytes 811008 | tf_op jit(solution)/shard_map/reduce_scatter | solution.py:903
  303.3 317.4 %reduce-scatter.20.cloned.1.call-start = ((), (), s32[]{:S(2)}) async-start(), calls=%async_computation.11 | async-start | bytes 811008 | tf_op jit(solution)/shard_map/reduce_scatter | solution.py:903
  303.9 348.0 %reduce-scatter.32.cloned.1.call-start = ((), (), s32[]{:S(2)}) async-start(), calls=%async_computation.17 | async-start | bytes 1474560
  304.0 1.5 copy-start.2
  305.4 376.7 %reduce-scatter.30.cloned.1.call-start = ((), (), s32[]{:S(2)}) async-start(), calls=%async_computation.16 | async-start | bytes 1474560
  306.9 424.4 %reduce-scatter.18.cloned.1.call-start = ((), (), s32[]{:S(2)}) async-start(), calls=%async_computation.10 | async-start | bytes 2949120 | tf_op jit(solution)/shard_map/reduce_scatter | solution.py:900
  307.7 0.9 copy-start.9
  307.7 0.9 copy-start.17
  307.7 0.9 copy-start.8
  307.7 0.9 copy-start.16
  307.7 41.9 %copy-start.20 = (f32[1,6]{1,0:T(1,128)S(1)}, f32[1,6]{1,0:T(1,128)}, u32[]{:S(2)}) copy-start(f32[1,6]{1,0:T(1,128)} %get-tuple-element.135) | copy-start | bytes 76
  307.7 41.9 %copy-start.21 = (f32[1,6]{1,0:T(1,128)S(1)}, f32[1,6]{1,0:T(1,128)}, u32[]{:S(2)}) copy-start(f32[1,6]{1,0:T(1,128)} %get-tuple-element.136) | copy-start | bytes 76
  307.7 41.9 %copy-start.18 = (f32[1,6]{1,0:T(1,128)S(1)}, f32[1,6]{1,0:T(1,128)}, u32[]{:S(2)}) copy-start(f32[1,6]{1,0:T(1,128)} %get-tuple-element.137) | copy-start | bytes 76
  307.8 41.9 %copy-start.19 = (f32[1,6]{1,0:T(1,128)S(1)}, f32[1,6]{1,0:T(1,128)}, u32[]{:S(2)}) copy-start(f32[1,6]{1,0:T(1,128)} %get-tuple-element.138) | copy-start | bytes 76
  307.8 41.9 %copy-start.6 = (f32[4,384]{1,0:T(4,128)S(1)}, f32[4,384]{1,0:T(4,128)}, u32[]{:S(2)}) copy-start(f32[4,384]{1,0:T(4,128)} %get-tuple-element.139) | copy-start | bytes 18436
  307.8 41.9 %copy-start.13 = (f32[1,384]{1,0:T(1,128)S(1)}, f32[1,384]{1,0:T(1,128)}, u32[]{:S(2)}) copy-start(f32[1,384]{1,0:T(1,128)} %get-tuple-element.140) | copy-start | bytes 4612
  307.8 41.9 %copy-start.14 = (f32[1,384]{1,0:T(1,128)S(1)}, f32[1,384]{1,0:T(1,128)}, u32[]{:S(2)}) copy-start(f32[1,384]{1,0:T(1,128)} %get-tuple-element.141) | copy-start | bytes 4612
  307.8 41.9 %copy-start.15 = (f32[1,384]{1,0:T(1,128)S(1)}, f32[1,384]{1,0:T(1,128)}, u32[]{:S(2)}) copy-start(f32[1,384]{1,0:T(1,128)} %get-tuple-element.142) | copy-start | bytes 4612
  307.8 41.9 %copy-start.5 = (f32[4,384]{1,0:T(4,128)S(1)}, f32[4,384]{1,0:T(4,128)}, u32[]{:S(2)}) copy-start(f32[4,384]{1,0:T(4,128)} %get-tuple-element.143) | copy-start | bytes 18436
  307.8 41.9 %copy-start.10 = (f32[1,384]{1,0:T(1,128)S(1)}, f32[1,384]{1,0:T(1,128)}, u32[]{:S(2)}) copy-start(f32[1,384]{1,0:T(1,128)} %get-tuple-element.144) | copy-start | bytes 4612
  307.8 41.9 %copy-start.11 = (f32[1,384]{1,0:T(1,128)S(1)}, f32[1,384]{1,0:T(1,128)}, u32[]{:S(2)}) copy-start(f32[1,384]{1,0:T(1,128)} %get-tuple-element.145) | copy-start | bytes 4612
  307.8 41.9 %copy-start.12 = (f32[1,384]{1,0:T(1,128)S(1)}, f32[1,384]{1,0:T(1,128)}, u32[]{:S(2)}) copy-start(f32[1,384]{1,0:T(1,128)} %get-tuple-element.146) | copy-start | bytes 4612
  307.9 472.9 %reduce-scatter.16.cloned.1.call-start = ((), (), s32[]{:S(2)}) async-start(), calls=%async_computation.9 | async-start | bytes 2949120 | tf_op jit(solution)/shard_map/reduce_scatter | solution.py:900
  780.8 2.9 copy-start.3
  783.7 1.4 copy-start.4
Sparse Core Ops, SparseCore 0:
  280.3 96.5 reduce-scatter.27
  379.2 19.8 reduce-scatter.25
  401.4 19.0 reduce-scatter.23
  426.0 94.4 reduce-scatter.21
  525.4 95.2 reduce-scatter.19
  623.5 28.3 reduce-scatter.31
  654.2 27.8 reduce-scatter.29
  685.0 46.2 reduce-scatter.17
  733.7 47.0 reduce-scatter.15

commit v2 on v1

--- a/solution.py
+++ b/solution.py
@@ -1,4 +1,5 @@
 import functools
+from typing import Any, NamedTuple
 import jax
 import jax.numpy as jnp
 from jax import lax
@@ -12,6 +13,26 @@
 F32 = jnp.float32
 BF = jnp.bfloat16
 VM = 60 * 1024 * 1024
+
+
+def cost_of(flops, moved=1 << 24):
+    return pl.CostEstimate(flops=flops, bytes_accessed=moved, transcendentals=0)
+
+
+class Weights(NamedTuple):
+    norm_gain: jax.Array
+    inner_weight: jax.Array
+    state_weight: jax.Array
+    step_weight: jax.Array
+    step_bias: jax.Array
+    decay_log: jax.Array
+    skip_gain: jax.Array
+    conv_weight: jax.Array
+    conv_bias: jax.Array
+    state_conv_weight: jax.Array
+    state_conv_bias: jax.Array
+    gate_gain: jax.Array
+    out_weight: jax.Array
 
 
 def dot(a, b):
@@ -206,10 +227,10 @@
 
 def forward_compute(layer, size, normed, meta, segrow, w):
     tokens, depth = normed.shape
-    inner = w["inner_weight"].shape[3]
-    heads = w["step_weight"].shape[2]
+    inner = w.inner_weight.shape[3]
+    heads = w.step_weight.shape[2]
     width = inner // heads
-    both = w["state_weight"].shape[2]
+    both = w.state_weight.shape[2]
     half = both // 2
     count = tokens // size
     rows = lambda wide: pl.BlockSpec((size, wide), lambda c: (c, 0))
@@ -227,18 +248,18 @@
         ),
         in_specs=[
             rows(depth), rows(8), pl.BlockSpec((8, size), lambda c: (0, c)),
-            layer_block(w["inner_weight"].shape, layer),
-            layer_block(w["state_weight"].shape, layer),
-            layer_block(w["step_weight"].shape, layer),
-            layer_block(w["out_weight"].shape, layer),
-            layer_block(w["conv_weight"].shape, layer),
-            whole_block(w["conv_bias"].shape),
-            layer_block(w["state_conv_weight"].shape, layer),
-            whole_block(w["state_conv_bias"].shape),
-            whole_block(w["step_bias"].shape),
-            whole_block(w["decay_log"].shape),
-            whole_block(w["skip_gain"].shape),
-            whole_block(w["gate_gain"].shape),
+            layer_block(w.inner_weight.shape, layer),
+            layer_block(w.state_weight.shape, layer),
+            layer_block(w.step_weight.shape, layer),
+            layer_block(w.out_weight.shape, layer),
+            layer_block(w.conv_weight.shape, layer),
+            whole_block(w.conv_bias.shape),
+            layer_block(w.state_conv_weight.shape, layer),
+            whole_block(w.state_conv_bias.shape),
+            whole_block(w.step_bias.shape),
+            whole_block(w.decay_log.shape),
+            whole_block(w.skip_gain.shape),
+            whole_block(w.gate_gain.shape),
         ],
         out_specs=(
             rows(inner), rows(inner), rows(inner), rows(both), rows(both), rows(heads), rows(inner),
@@ -252,11 +273,12 @@
             pltpu.VMEM((size + 8, both), F32),
         ],
         compiler_params=pltpu.CompilerParams(vmem_limit_bytes=VM),
-        name="forward_mix",
+        cost_estimate=cost_of(10 * tokens * depth * inner),
+        name="forward",
     )(
-        normed, meta, segrow, w["inner_weight"], w["state_weight"], w["step_weight"], w["out_weight"],
-        w["conv_weight"], w["conv_bias"], w["state_conv_weight"], w["state_conv_bias"],
-        w["step_bias"], w["decay_log"], w["skip_gain"], w["gate_gain"],
+        normed, meta, segrow, w.inner_weight, w.state_weight, w.step_weight, w.out_weight,
+        w.conv_weight, w.conv_bias, w.state_conv_weight, w.state_conv_bias,
+        w.step_bias, w.decay_log, w.skip_gain, w.gate_gain,
     )
 
 
@@ -438,12 +460,12 @@
 def backward_compute(layer, size, inner_all, sent, mean, meta, segrow, saved, w):
     g, v, pv, s, ps, d, y, sp = saved
     tokens, depth = sent.shape
-    inner = w["inner_weight"].shape[3]
-    heads = w["step_weight"].shape[2]
+    inner = w.inner_weight.shape[3]
+    heads = w.step_weight.shape[2]
     width = inner // heads
-    both = w["state_weight"].shape[2]
+    both = w.state_weight.shape[2]
     half = both // 2
-    taps = w["conv_weight"].shape[1]
+    taps = w.conv_weight.shape[1]
     count = tokens // size
     rows = lambda wide: pl.BlockSpec((size, wide), lambda c: (count - 1 - c, 0))
     kernel = functools.partial(backward_kernel, layer, heads, width, inner_all)
@@ -461,16 +483,16 @@
             pl.BlockSpec((8, size), lambda c: (0, count - 1 - c)),
             rows(inner), rows(inner), rows(inner), rows(both), rows(both), rows(heads), rows(inner),
             pl.BlockSpec((None, half, inner), lambda c: (count - 1 - c, 0, 0)),
-            layer_block(w["inner_weight"].shape, layer),
-            layer_block(w["state_weight"].shape, layer),
-            layer_block(w["step_weight"].shape, layer),
-            layer_block(w["out_weight"].shape, layer),
-            layer_block(w["conv_weight"].shape, layer),
-            layer_block(w["state_conv_weight"].shape, layer),
-            whole_block(w["step_bias"].shape),
-            whole_block(w["decay_log"].shape),
-            whole_block(w["skip_gain"].shape),
-            whole_block(w["gate_gain"].shape),
+            layer_block(w.inner_weight.shape, layer),
+            layer_block(w.state_weight.shape, layer),
+            layer_block(w.step_weight.shape, layer),
+            layer_block(w.out_weight.shape, layer),
+            layer_block(w.conv_weight.shape, layer),
+            layer_block(w.state_conv_weight.shape, layer),
+            whole_block(w.step_bias.shape),
+            whole_block(w.decay_log.shape),
+            whole_block(w.skip_gain.shape),
+            whole_block(w.gate_gain.shape),
         ],
         out_specs=(
             rows(inner), rows(inner), rows(both), rows(heads), rows(inner), rows(depth),
@@ -482,52 +504,61 @@
             pltpu.VMEM((taps - 1, size + 8, both), F32),
         ],
         compiler_params=pltpu.CompilerParams(vmem_limit_bytes=VM),
-        name="backward_mix",
+        cost_estimate=cost_of(20 * tokens * depth * inner),
+        name="backward",
     )(
         sent, mean, meta, segrow, g, v, pv, s, ps, d, y, sp,
-        w["inner_weight"], w["state_weight"], w["step_weight"], w["out_weight"],
-        w["conv_weight"], w["state_conv_weight"],
-        w["step_bias"], w["decay_log"], w["skip_gain"], w["gate_gain"],
+        w.inner_weight, w.state_weight, w.step_weight, w.out_weight,
+        w.conv_weight, w.state_conv_weight,
+        w.step_bias, w.decay_log, w.skip_gain, w.gate_gain,
     )
 
 
-def weight_kernel(normed_ref, sent_ref, sc_ref, rg_ref, rv_ref, rs_ref, rd_ref, gin_ref, gst_ref, gsd_ref, gout_ref):
-    nb = normed_ref[...]
-    gin_ref[0] = t_dot(nb, rg_ref[...]).astype(BF)
-    gin_ref[1] = t_dot(nb, rv_ref[...]).astype(BF)
-    gst_ref[...] = t_dot(nb, rs_ref[...]).astype(BF)
-    gsd_ref[...] = t_dot(nb, rd_ref[...]).astype(BF)
-    gout_ref[...] = t_dot(sc_ref[...], sent_ref[...]).astype(BF)
-
-
-def weight_compute(normed, sent, sc, rg, rv, rs, rd):
+def weight_kernel(steps, normed_ref, sent_ref, sc_ref, rg_ref, rv_ref, rs_ref, rd_ref, gin_ref, gst_ref, gsd_ref, gout_ref):
+    cols = normed_ref.shape[1] // steps
+    for i in range(steps):
+        here = slice(i * cols, (i + 1) * cols)
+        nb = normed_ref[:, here]
+        turned_nb = jnp.transpose(nb)
+        gin_ref[i, 0] = dot(turned_nb, rg_ref[...]).astype(BF)
+        gin_ref[i, 1] = dot(turned_nb, rv_ref[...]).astype(BF)
+        gst_ref[here, :] = dot(turned_nb, rs_ref[...]).astype(BF)
+        gsd_ref[:, here] = t_dot(rd_ref[...], nb)
+        gout_ref[i] = t_dot(sc_ref[...], sent_ref[:, here]).astype(BF)
+
+
+def weight_compute(across, normed, sent, sc, rg, rv, rs, rd):
     tokens, depth = normed.shape
     inner, both, heads = rg.shape[1], rs.shape[1], rd.shape[1]
-    step = 256
+    share = depth // across
+    steps = 1 if share % 128 == 0 else across
+    wide = share * steps
     whole = lambda wide: pl.BlockSpec((tokens, wide), lambda i: (0, 0), pipeline_mode=pl.Buffered(1))
-    cols = pl.BlockSpec((tokens, step), lambda i: (0, i))
+    cols = pl.BlockSpec((tokens, wide), lambda i: (0, i))
     return pl.pallas_call(
-        weight_kernel,
-        grid=(depth // step,),
+        functools.partial(weight_kernel, steps),
+        grid=(depth // wide,),
         out_shape=(
-            jax.ShapeDtypeStruct((2, depth, inner), BF),
+            jax.ShapeDtypeStruct((across, 2, share, inner), BF),
             jax.ShapeDtypeStruct((depth, both), BF),
-            jax.ShapeDtypeStruct((depth, heads), BF),
-            jax.ShapeDtypeStruct((inner, depth), BF),
+            jax.ShapeDtypeStruct((heads, depth), F32),
+            jax.ShapeDtypeStruct((across, inner, share), BF),
         ),
         in_specs=[cols, cols, whole(inner), whole(inner), whole(inner), whole(both), whole(heads)],
         out_specs=(
-            pl.BlockSpec((2, step, inner), lambda i: (0, i, 0)),
-            pl.BlockSpec((step, both), lambda i: (i, 0)),
-            pl.BlockSpec((step, heads), lambda i: (i, 0)),
-            pl.BlockSpec((inner, step), lambda i: (0, i)),
+            pl.BlockSpec((steps, 2, share, inner), lambda i: (i, 0, 0, 0)),
+            pl.BlockSpec((wide, both), lambda i: (i, 0)),
+            pl.BlockSpec((heads, wide), lambda i: (0, i)),
+            pl.BlockSpec((steps, inner, share), lambda i: (i, 0, 0)),
         ),
         compiler_params=pltpu.CompilerParams(vmem_limit_bytes=VM),
-        name="weight_grads",
+        cost_estimate=cost_of(2 * tokens * depth * (3 * inner + both)),
+        name="weights",
     )(normed, sent, sc, rg, rv, rs, rd)
 
 
 AXIS = "tensor"
+DATA = "dp"
 
 
 def span_of(dims):
@@ -566,65 +597,122 @@
         return sorted(found, key=lambda r: (self.gather_last(q, r), r & (r - 1) != 0))
 
 
-def remote(src, dst, send, recv, target):
+def remote(src, dst, send, recv, target, axis=AXIS):
     return pltpu.make_async_remote_copy(
         src_ref=src, dst_ref=dst, send_sem=send, recv_sem=recv,
-        device_id={AXIS: target}, device_id_type=pl.DeviceIdType.MESH,
+        device_id={axis: target}, device_id_type=pl.DeviceIdType.MESH,
     )
 
 
-def greet(targets):
+def greet(targets, across=()):
     barrier = pltpu.get_barrier_semaphore()
-    for target in targets:
-        pl.semaphore_signal(barrier, inc=1, device_id={AXIS: target}, device_id_type=pl.DeviceIdType.MESH)
-    pl.semaphore_wait(barrier, len(targets))
+    for axis, group in ((AXIS, targets), (DATA, across)):
+        for target in group:
+            pl.semaphore_signal(barrier, inc=1, device_id={axis: target}, device_id_type=pl.DeviceIdType.MESH)
+    pl.semaphore_wait(barrier, len(targets) + len(across))
 
 
 def block_rows(block, rows, half, q):
     return pl.ds(pl.multiple_of(block * rows + q * half, half), half)
+
+
+class Spec(NamedTuple):
+    reduce: bool
+    squares: bool
+    gather: bool
+    means: bool
+    n_in: int
+    n_out: int
+
+
+def reduce_scratch(ex, rows, depth):
+    slots, half = ex.size // 2, rows // 2
+    dma = pltpu.SemaphoreType.DMA
+    return [
+        pltpu.VMEM((slots, rows, depth), BF), pltpu.VMEM((slots, rows, depth), BF),
+        pltpu.VMEM((2 * slots, half, depth), BF), pltpu.VMEM((2 * (slots - 1), half, depth), BF),
+        dma((slots,)), dma((slots,)), dma((slots,)), dma((2 * slots,)), dma((2 * (slots - 1),)),
+    ]
+
+
+def reduce_start(ex, part_ref, rows, bufs):
+    own, pair, _, _, load_sem, pair_send, pair_recv, _, _ = bufs
+    me = lax.axis_index(AXIS)
+    block = lambda b: part_ref.at[pl.ds(pl.multiple_of(b * rows, rows), rows), :]
+    loads, pairs = {}, {}
+    for i, r in enumerate(ex.offsets):
+        loads[r] = pltpu.make_async_copy(block(me ^ r), own.at[i], load_sem.at[i])
+        loads[r].start()
+    for i, r in enumerate(ex.offsets):
+        pairs[r] = remote(block(me ^ r ^ 1), pair.at[i], pair_send.at[i], pair_recv.at[i], me ^ 1)
+        pairs[r].start()
+    return loads, pairs
+
+
+def reduce_finish(ex, rows, bufs, loads, pairs, pending):
+    own, pair, stage, got, _, _, _, link_send, link_recv = bufs
+    me = lax.axis_index(AXIS)
+    n, half = ex.size, rows // 2
+    slot_of = {r: i for i, r in enumerate(ex.offsets)}
+    steps = [ex.reduce_steps(q) for q in range(2)]
+    index = {}
+    for q in range(2):
+        for i, r in steps[q]:
+            for j in range(i):
+                index[(q, j, r)] = len(index)
+    ready, arrivals, final = set(), {}, [None, None]
+    for k in range(len(steps[0])):
+        for q in range(2):
+            i, r = steps[q][k]
+            if r not in ready:
+                loads[r].wait()
+                pairs[r].wait_recv()
+                ready.add(r)
+            piece = pl.ds(q * half, half)
+            value = own[slot_of[r], piece, :].astype(F32) + pair[slot_of[r], piece, :].astype(F32)
+            for j in range(i):
+                arrivals[(q, j, r)].wait_recv()
+                value = value + got[index[(q, j, r)]].astype(F32)
+            if r == 0:
+                final[q] = value
+                continue
+            d = ex.orders[q][i]
+            s = q * (n // 2) + slot_of[r]
+            stage[s] = value.astype(BF)
+            at = index[(q, i, r ^ d)]
+            copy = remote(stage.at[s], got.at[at], link_send.at[s], link_recv.at[at], me ^ d)
+            copy.start()
+            arrivals[(q, i, r ^ d)] = copy
+            pending.append(copy)
+    pending.extend(pairs.values())
+    return jnp.concatenate(final, axis=0)
 
 
 def comm_kernel(ex, rows, spec, middle, *refs):
     refs = list(refs)
     take = lambda k: [refs.pop(0) for _ in range(k)]
-    part_ref = take(1)[0] if spec["reduce"] else None
-    psq_ref = take(1)[0] if spec["squares"] else None
-    ins = take(spec["n_in"])
-    out_ref = take(1)[0] if spec["gather"] else None
-    mean_out = take(1)[0] if spec["means"] else None
-    outs = take(spec["n_out"])
+    part_ref = take(1)[0] if spec.reduce else None
+    psq_ref = take(1)[0] if spec.squares else None
+    ins = take(spec.n_in)
+    out_ref = take(1)[0] if spec.gather else None
+    mean_out = take(1)[0] if spec.means else None
+    outs = take(spec.n_out)
     me = lax.axis_index(AXIS)
     n = ex.size
     half = rows // 2
     peers = [me ^ r for r in range(1, n)]
-    partners = peers if (spec["squares"] or spec["means"]) else [me ^ d for d in ex.links + [1]]
+    partners = peers if (spec.squares or spec.means) else [me ^ d for d in ex.links + [1]]
     greet(partners)
     pending = []
 
     total = None
-    if spec["reduce"]:
-        own, pair, stage, got = take(4)
-        load_sem, pair_send, pair_recv, link_send, link_recv = take(5)
-        if spec["squares"]:
+    square = None
+    if spec.reduce:
+        bufs = take(9)
+        loads, pairs = reduce_start(ex, part_ref, rows, bufs)
+        squares = []
+        if spec.squares:
             sq_buf, sq_send, sq_recv = take(3)
-        slot_of = {r: i for i, r in enumerate(ex.offsets)}
-        loads = {}
-        for r in ex.offsets:
-            i = slot_of[r]
-            loads[r] = pltpu.make_async_copy(
-                part_ref.at[pl.ds(pl.multiple_of((me ^ r) * rows, rows), rows), :], own.at[i], load_sem.at[i]
-            )
-            loads[r].start()
-        pairs = {}
-        for r in ex.offsets:
-            i = slot_of[r]
-            pairs[r] = remote(
-                part_ref.at[pl.ds(pl.multiple_of((me ^ r ^ 1) * rows, rows), rows), :], pair.at[i],
-                pair_send.at[i], pair_recv.at[i], me ^ 1,
-            )
-            pairs[r].start()
-        squares = []
-        if spec["squares"]:
             for r in range(1, n):
                 copy = remote(
                     psq_ref.at[pl.ds(pl.multiple_of((me ^ r) * 8, 8), 8), :], sq_buf.at[r],
@@ -632,49 +720,16 @@
                 )
                 copy.start()
                 squares.append(copy)
-        ready = set()
-        index = {}
-        for q in range(2):
-            for i, r in ex.reduce_steps(q):
-                for j in range(i):
-                    index[(q, j, r)] = len(index)
-        arrivals = {}
-        steps = [ex.reduce_steps(q) for q in range(2)]
-        final = [None, None]
-        for k in range(len(steps[0])):
-            for q in range(2):
-                i, r = steps[q][k]
-                if r not in ready:
-                    loads[r].wait()
-                    pairs[r].wait_recv()
-                    ready.add(r)
-                piece = pl.ds(q * half, half)
-                value = own[slot_of[r], piece, :].astype(F32) + pair[slot_of[r], piece, :].astype(F32)
-                for j in range(i):
-                    arrivals[(q, j, r)].wait_recv()
-                    value = value + got[index[(q, j, r)]].astype(F32)
-                if r == 0:
-                    final[q] = value
-                    continue
-                d = ex.orders[q][i]
-                s = q * (n // 2) + slot_of[r]
-                stage[s] = value.astype(BF)
-                at = index[(q, i, r ^ d)]
-                copy = remote(stage.at[s], got.at[at], link_send.at[s], link_recv.at[at], me ^ d)
-                copy.start()
-                arrivals[(q, i, r ^ d)] = copy
-                pending.append(copy)
-        total = jnp.concatenate(final, axis=0)
-        pending.extend(pairs.values())
-        square = None
-        if spec["squares"]:
+        total = reduce_finish(ex, rows, bufs, loads, pairs, pending)
+        if spec.squares:
             square = psq_ref[pl.ds(pl.multiple_of(me * 8, 8), 8), :]
             for r, copy in enumerate(squares, 1):
                 copy.wait_recv()
                 square = square + sq_buf[r]
+            square = column_of(square)
             pending.extend(squares)
-    result = middle(total, column_of(square) if spec["squares"] else None, ins, outs)
-    if spec["gather"]:
+    result = middle(total, square, ins, outs)
+    if spec.gather:
         row_buf, own_sem, send_sem, recv_sem = take(4)
         sent_rows, mean = result
         row_buf[...] = sent_rows
@@ -701,7 +756,7 @@
         )
         local.start()
         mean_copies = []
-        if spec["means"]:
+        if spec.means:
             mean_buf, mean_send, mean_recv = take(3)
             tile = tile_of(mean)
             mean_buf[...] = tile
@@ -730,7 +785,7 @@
 
 def comm_call(name, collective, ex, middle, part=None, psq=None, ins=(), outs=(), gather=None, means=False):
     n = ex.size
-    spec = dict(reduce=part is not None, squares=psq is not None, gather=gather is not None, means=means, n_in=len(ins), n_out=len(outs))
+    spec = Spec(part is not None, psq is not None, gather is not None, means, len(ins), len(outs))
     vm = pl.BlockSpec(memory_space=pltpu.VMEM)
     anywhere = pl.BlockSpec(memory_space=pl.ANY)
     operands, in_specs, out_shape, out_specs, scratch = [], [], [], [], []
@@ -748,12 +803,7 @@
     half = rows // 2
     dma = pltpu.SemaphoreType.DMA
     if part is not None:
-        slots = n // 2
-        scratch += [
-            pltpu.VMEM((slots, rows, depth), BF), pltpu.VMEM((slots, rows, depth), BF),
-            pltpu.VMEM((2 * slots, half, depth), BF), pltpu.VMEM((2 * (slots - 1), half, depth), BF),
-            dma((slots,)), dma((slots,)), dma((slots,)), dma((2 * slots,)), dma((2 * (slots - 1),)),
-        ]
+        scratch += reduce_scratch(ex, rows, depth)
         if psq is not None:
             scratch += [pltpu.VMEM((n, 8, rows), F32), dma((n,)), dma((n,))]
     if gather is not None:
@@ -774,17 +824,98 @@
         out_specs=tuple(out_specs),
         scratch_shapes=scratch,
         compiler_params=pltpu.CompilerParams(collective_id=collective, has_side_effects=True, vmem_limit_bytes=VM),
+        cost_estimate=cost_of(1 << 33),
         name=name,
     )(*operands)
 
 
+def sums_kernel(ex, across, state_ref, small_ref, wide_ref, state_out, small_out, wide_out, *refs):
+    refs = list(refs)
+    take = lambda k: [refs.pop(0) for _ in range(k)]
+    bufs = take(9)
+    small_buf, wide_buf, mid_buf, all_buf, cell_buf, cell_got = take(6)
+    small_send, small_recv, wide_send, wide_recv, all_send, all_recv, cell_send, cell_recv = take(8)
+    me, row = lax.axis_index(AXIS), lax.axis_index(DATA)
+    n = ex.size
+    layers, cells = state_out.shape[0], state_out.shape[1]
+    rows = state_ref.shape[0] // n
+    greet([me ^ r for r in range(1, n)], [row ^ r for r in range(1, across)])
+    pending, small_copies, wide_copies = [], [], []
+    for r in range(1, across):
+        small_copies.append(remote(small_ref, small_buf.at[r], small_send.at[r], small_recv.at[r], row ^ r, DATA))
+        wide_copies.append(remote(wide_ref, wide_buf.at[r], wide_send.at[r], wide_recv.at[r], row ^ r, DATA))
+        small_copies[-1].start()
+        wide_copies[-1].start()
+    loads, pairs = reduce_start(ex, state_ref, rows, bufs)
+    total, wide = small_ref[...], wide_ref[...]
+    for r in range(1, across):
+        small_copies[r - 1].wait_recv()
+        total = total + small_buf[r]
+        wide_copies[r - 1].wait_recv()
+        wide = wide + wide_buf[r]
+    small_out[...] = total
+    mid_buf[...] = wide
+    all_copies = []
+    for r in range(1, n):
+        all_copies.append(remote(mid_buf, all_buf.at[r], all_send.at[r], all_recv.at[r], me ^ r))
+        all_copies[-1].start()
+    state = reduce_finish(ex, rows, bufs, loads, pairs, pending)
+    for k in range(layers * across):
+        cell_buf[k] = state[k * cells : (k + 1) * cells, :]
+    cell_copies = {}
+    for r in range(1, across):
+        for layer in range(layers):
+            k = r * layers + layer
+            cell_copies[k] = remote(
+                cell_buf.at[layer * across + (row ^ r)], cell_got.at[k], cell_send.at[k], cell_recv.at[k], row ^ r, DATA
+            )
+            cell_copies[k].start()
+    wide_out[0] = wide
+    total = wide
+    for r in range(1, n):
+        all_copies[r - 1].wait_recv()
+        total = total + all_buf[r]
+    wide_out[1] = total
+    for layer in range(layers):
+        value = cell_buf[layer * across + row]
+        for r in range(1, across):
+            cell_copies[r * layers + layer].wait_recv()
+            value = value + cell_got[r * layers + layer]
+        state_out[layer] = value
+    for copy in pending + small_copies + wide_copies + all_copies + list(cell_copies.values()):
+        copy.wait_send()
+
+
+def sums_call(collective, ex, across, layers, state, small, wide):
+    rows, both = state.shape[0] // ex.size, state.shape[1]
+    cells = rows // (layers * across)
+    vm = pl.BlockSpec(memory_space=pltpu.VMEM)
+    dma = pltpu.SemaphoreType.DMA
+    n = ex.size
+    return pl.pallas_call(
+        functools.partial(sums_kernel, ex, across),
+        out_shape=(
+            jax.ShapeDtypeStruct((layers, cells, both), F32),
+            jax.ShapeDtypeStruct(small.shape, F32),
+            jax.ShapeDtypeStruct((2,) + wide.shape, F32),
+        ),
+        in_specs=[pl.BlockSpec(memory_space=pl.ANY), vm, vm],
+        out_specs=(vm, vm, vm),
+        scratch_shapes=reduce_scratch(ex, rows, both) + [
+            pltpu.VMEM((across,) + small.shape, F32), pltpu.VMEM((across,) + wide.shape, F32),
+            pltpu.VMEM(wide.shape, F32), pltpu.VMEM((n,) + wide.shape, F32),
+            pltpu.VMEM((layers * across, cells, both), F32), pltpu.VMEM((layers * across, cells, both), F32),
+            dma((across,)), dma((across,)), dma((across,)), dma((across,)), dma((n,)), dma((n,)),
+            dma((layers * across,)), dma((layers * across,)),
+        ],
+        compiler_params=pltpu.CompilerParams(collective_id=collective, has_side_effects=True, vmem_limit_bytes=VM),
+        cost_estimate=cost_of(1 << 33),
+        name="sums",
+    )(state, small, wide)
+
+
 LAYERS = 2
 SIZE = 128
-NAMES = (
-    "norm_gain", "inner_weight", "state_weight", "step_weight", "step_bias", "decay_log", "skip_gain",
-    "conv_weight", "conv_bias", "state_conv_weight", "state_conv_bias", "gate_gain", "out_weight",
-)
-
 
 def shape_of(rows, depth):
     return jax.ShapeDtypeStruct((rows, depth), F32)
@@ -800,6 +931,15 @@
         return tiles
     flat = tiles.reshape(-1, 8, width)[:, 0, :].reshape(count, 1, -1)
     return jnp.broadcast_to(flat, (count, 8, flat.shape[2])).reshape(count * 8, -1)
+
+
+def scatter_all(*arrays):
+    flat = [a.reshape(a.shape[0], -1, a.shape[-1]) for a in arrays]
+    if len({f.shape[2] for f in flat}) > 1:
+        return [lax.psum_scatter(a, DATA, scatter_dimension=0, tiled=True)[0].astype(F32) for a in arrays]
+    both = lax.psum_scatter(jnp.concatenate(flat, axis=1), DATA, scatter_dimension=0, tiled=True)[0].astype(F32)
+    ends = [sum(f.shape[1] for f in flat[:i]) for i in range(len(flat) + 1)]
+    return [both[ends[i] : ends[i + 1]].reshape(a.shape[1:]) for i, a in enumerate(arrays)]
 
 
 def gate_of(square, inner_all):
@@ -855,20 +995,20 @@
     return None
 
 
-def shards(ex, residual, cotangent, segments, *weights):
-    w = dict(zip(NAMES, weights))
+def shards(ex, across, residual, cotangent, segments, *weights):
+    w = Weights(*weights)
     rows, depth = residual.shape
     tokens = segments.shape[1]
-    inner = w["inner_weight"].shape[3]
-    heads = w["step_weight"].shape[2]
+    inner = w.inner_weight.shape[3]
+    heads = w.step_weight.shape[2]
     inner_all = inner * ex.size
     count = tokens // SIZE
-    gain = w["norm_gain"]
+    gain = w.norm_gain
     meta, segrow = token_meta(segments[0], SIZE)
     ids = iter(range(100))
     resids, mixeds, gates, normeds, saved = [residual], [], [], [], []
     (normed,) = comm_call(
-        "rows_start", next(ids), ex, functools.partial(start_middle, 0), ins=(residual, gain), gather=depth
+        "start", next(ids), ex, functools.partial(start_middle, 0), ins=(residual, gain), gather=depth
     )
     hidden = residual
     for layer in range(LAYERS):
@@ -879,7 +1019,7 @@
         squares = retile(squares, ex.size)
         if layer + 1 < LAYERS:
             normed, hidden, mixed, gate = comm_call(
-                "rows_between", next(ids), ex, functools.partial(between_middle, layer + 1, inner_all),
+                "between", next(ids), ex, functools.partial(between_middle, layer + 1, inner_all),
                 part=part, psq=squares, ins=(hidden, gain),
                 outs=(shape_of(rows, depth), shape_of(rows, depth), shape_of(rows, 1)), gather=depth,
             )
@@ -888,7 +1028,7 @@
             gates.append(gate)
         else:
             sent, mean, block_output = comm_call(
-                "rows_turn", next(ids), ex, functools.partial(turn_middle, inner_all),
+                "turn", next(ids), ex, functools.partial(turn_middle, inner_all),
                 part=part, psq=squares, ins=(hidden, cotangent), outs=(shape_of(rows, depth),), gather=depth, means=True,
             )
     grad = cotangent
@@ -896,94 +1036,110 @@
     for layer in range(LAYERS - 1, -1, -1):
         made = backward_compute(layer, SIZE, inner_all, sent, retile(mean, count), meta, segrow, saved[layer], w)
         rg, rv, rs, rd, sc, part = made[:6]
-        g_inner, g_state, g_step, g_out = weight_compute(normeds[layer], sent, sc, rg, rv, rs, rd)
-        scatter = lambda v, dim: lax.psum_scatter(v, "dp", scatter_dimension=dim, tiled=True).astype(F32)
-        big[layer] = (
-            scatter(g_inner, 1),
-            lax.psum_scatter(g_state, ("dp", "tensor"), scatter_dimension=0, tiled=True).astype(F32),
-            scatter(g_step, 0),
-            scatter(g_out, 1),
-        )
+        g_inner, g_state, g_step, g_out = weight_compute(across, normeds[layer], sent, sc, rg, rv, rs, rd)
+        part, g_inner, g_out = lax.optimization_barrier((part, g_inner, g_out))
+        big[layer] = scatter_all(g_inner, g_out)
         if layer:
             sent, mean, grad, g_gain = comm_call(
-                "rows_back", next(ids), ex, functools.partial(back_middle, layer), part=part,
+                "back", next(ids), ex, functools.partial(back_middle, layer), part=part,
                 ins=(resids[layer], grad, gain, mixeds[layer - 1], gates[layer - 1]),
                 outs=(shape_of(rows, depth), shape_of(1, depth)), gather=depth, means=True,
             )
         else:
             grad, g_gain = comm_call(
-                "rows_end", next(ids), ex, functools.partial(end_middle, layer), part=part,
+                "end", next(ids), ex, functools.partial(end_middle, layer), part=part,
                 ins=(resids[layer], grad, gain), outs=(shape_of(rows, depth), shape_of(1, depth)),
             )
-        small[layer] = (made[6:], g_gain)
-    per_dp = lax.psum(
-        jnp.stack([jnp.concatenate([m[0], m[1], m[4], m[5]], axis=0) for m, _ in small]), "dp"
+        small[layer] = (made[6:], g_gain, g_state, g_step)
+    taps = w.conv_weight.shape[1]
+    both = w.state_weight.shape[2]
+    cells = depth // (ex.size * across)
+
+    def narrow(m):
+        pad = jnp.zeros((1, inner - heads), F32)
+        return jnp.concatenate(
+            [m[0], m[1], m[4], m[5], jnp.concatenate([m[6], pad], axis=1), jnp.concatenate([m[7], pad], axis=1)], axis=0
+        )
+
+    def wide(item):
+        m, g_gain, _, g_step = item
+        pad = jnp.zeros((taps, depth - both), F32)
+        return jnp.concatenate(
+            [g_step, g_gain, jnp.concatenate([m[2], pad], axis=1), jnp.concatenate([m[3], pad[:1]], axis=1)], axis=0
+        )
+
+    state = jnp.stack([item[2].reshape(across, ex.size, cells, both) for item in small])
+    state = jnp.transpose(state, (2, 0, 1, 3, 4)).reshape(-1, both)
+    g_state, narrow_sum, wide_sum = sums_call(
+        next(ids), ex, across, LAYERS, state,
+        jnp.stack([narrow(item[0]) for item in small]), jnp.stack([wide(item) for item in small]),
     )
-    per_head = lax.psum(jnp.stack([jnp.concatenate([m[6], m[7]], axis=0) for m, _ in small]), "dp")
-    everywhere = lax.psum(jnp.stack([jnp.concatenate([m[2], m[3]], axis=0) for m, _ in small]), ("dp", "tensor"))
-    g_norm = lax.psum_scatter(
-        jnp.concatenate([g for _, g in small], axis=0), ("dp", "tensor"), scatter_dimension=1, tiled=True
-    )
-    taps = w["conv_weight"].shape[1]
-    stack = lambda k: jnp.stack([big[layer][k] for layer in range(LAYERS)])
+    per_dp = wide_sum[0, :, :heads]
+    everywhere = wide_sum[1, :, heads:]
+    own = lax.axis_index(DATA)
+    step_cols = depth // across
+    g_step = jnp.transpose(lax.dynamic_slice_in_dim(per_dp, own * step_cols, step_cols, 2), (0, 2, 1))
+    device = own * ex.size + lax.axis_index(AXIS)
+    g_norm = lax.dynamic_slice_in_dim(everywhere[:, 0], device * cells, cells, 1)
     return (
         block_output,
         grad,
         g_norm,
-        stack(0),
-        stack(1),
-        stack(2),
-        per_head[:, 0],
-        per_head[:, 1],
-        per_dp[:, taps + 2].reshape(LAYERS, heads, -1).sum(2),
-        per_dp[:, :taps],
-        per_dp[:, taps],
-        everywhere[:, :taps],
-        everywhere[:, taps],
-        per_dp[:, taps + 1],
-        stack(3),
+        jnp.stack([item[0] for item in big]),
+        g_state,
+        g_step,
+        narrow_sum[:, taps + 3, :heads],
+        narrow_sum[:, taps + 4, :heads],
+        narrow_sum[:, taps + 2].reshape(LAYERS, heads, -1).sum(2),
+        narrow_sum[:, :taps],
+        narrow_sum[:, taps],
+        everywhere[:, 1 : taps + 1, :both],
+        everywhere[:, taps + 1, :both],
+        narrow_sum[:, taps + 1],
+        jnp.stack([item[1] for item in big]),
     )
 
 
 def solution(mesh):
-    ex = Exchange(mesh.shape["tensor"])
+    ex = Exchange(mesh.shape[AXIS])
+    both, rest = (DATA, AXIS), None
     return jax.shard_map(
-        functools.partial(shards, ex),
+        functools.partial(shards, ex, mesh.shape[DATA]),
         mesh=mesh,
         in_specs=(
-            P(("dp", "tensor"), None),
-            P(("dp", "tensor"), None),
-            P("dp", None),
+            P(both, rest),
+            P(both, rest),
+            P(DATA, rest),
             P(),
-            P(None, None, None, "tensor"),
+            P(rest, rest, rest, AXIS),
             P(),
-            P(None, None, "tensor"),
-            P(None, "tensor"),
-            P(None, "tensor"),
-            P(None, "tensor"),
-            P(None, None, "tensor"),
-            P(None, "tensor"),
+            P(rest, rest, AXIS),
+            P(rest, AXIS),
+            P(rest, AXIS),
+            P(rest, AXIS),
+            P(rest, rest, AXIS),
+            P(rest, AXIS),
             P(),
             P(),
-            P(None, "tensor"),
-            P(None, "tensor", None),
+            P(rest, AXIS),
+            P(rest, AXIS, rest),
         ),
         out_specs=(
-            P(("dp", "tensor"), None),
-            P(("dp", "tensor"), None),
-            P(None, ("dp", "tensor")),
-            P(None, None, "dp", "tensor"),
-            P(None, ("dp", "tensor"), None),
-            P(None, "dp", "tensor"),
-            P(None, "tensor"),
-            P(None, "tensor"),
-            P(None, "tensor"),
-            P(None, None, "tensor"),
-            P(None, "tensor"),
+            P(both, rest),
+            P(both, rest),
+            P(rest, both),
+            P(rest, rest, DATA, AXIS),
+            P(rest, both, rest),
+            P(rest, DATA, AXIS),
+            P(rest, AXIS),
+            P(rest, AXIS),
+            P(rest, AXIS),
+            P(rest, rest, AXIS),
+            P(rest, AXIS),
             P(),
             P(),
-            P(None, "tensor"),
-            P(None, "tensor", "dp"),
+            P(rest, AXIS),
+            P(rest, AXIS, DATA),
         ),
         check_vma=False,
     )

time: 794 us -> 421 us (0.53)
  waiting for transfers between devices: 404 us -> 0.06 us
  Pallas kernels: 288 us -> 370 us
  blocking collectives: 57.4 us -> 0 us
    reduce_scatter x6 -> x2, waiting for transfers between devices: 336 us -> 0.02 us  [scatter_all(): lax.psum_scatter(jnp.concatenate(flat, axis=1), DATA, scatter_dimension=0...]
    pallas_call x2 -> x3, Pallas kernels: 22.4 us -> 104 us  [the longest x1 84.1 us: sums_call(): pl.pallas_call(functools.partial(sums_kernel, ex, across), out_shape=(jax...]
    unnamed x12 -> x2, waiting for transfers between devices: 67.7 us -> 0.03 us
    psum x2 -> x0, blocking collectives: 57.4 us -> none  [the longest x1 39.7 us: shards(): lax.psum(jnp.stack([jnp.concatenate([m[2], m[3]], axis=0) for m, _ in sma...]
  transfers between devices with their start and end apart: 9 -> 2, of which waited for: 9 -> 0; matrix products, arithmetic and copies ran while one was open for 2% -> 4% of each run, Pallas kernels for 3% -> 45%
where the time goes in v2:
time: 421 us; the launch traced here: 420 us
  Pallas kernels  370 us (88%)
  local copies, waits for them, and re-layouts  20.1 us (5%)
  other arithmetic  15.5 us (4%)
  between operations  14.5 us (3%)
    pallas_call x5, Pallas kernels, comm_call(): pl.pallas_call(functools.partial(comm_kernel, ex, rows, spec, middle), ou...  156 us
    pallas_call x1, Pallas kernels, sums_call(): pl.pallas_call(functools.partial(sums_kernel, ex, across), out_shape=(jax...  84.1 us
    pallas_call x2, Pallas kernels, backward_compute(): pl.pallas_call(kernel, grid=(count,), out_shape=(out(inner, BF), out(inne...  69.7 us
    pallas_call x2, Pallas kernels, forward_compute(): pl.pallas_call(kernel, grid=(count,), out_shape=(out(inner, F32), out(inn...  39.7 us
    pallas_call x2, Pallas kernels, weight_compute(): pl.pallas_call(functools.partial(weight_kernel, steps), grid=(depth // wi...  20.4 us
  transfers between devices with their start and end apart: 2, of which 0 were waited for; matrix products, arithmetic and copies ran while one was open for 4% of the time, Pallas kernels for 45%

profile of v2, /device:TPU:0, one launch (start us, length us, event | category | flops | bytes accessed | tf_op | source)
XLA Modules:
  0.0 420.3 jit_solution(808169124490426127)
XLA Ops:
  7.2 0.7 convert_element_type.45
  8.1 0.1 copy.62
  8.2 0.1 copy.64
  8.2 0.1 copy.63
  8.8 0.8 compare_convert_fusion
  9.7 1.0 copy.47.meta_ref
  10.7 2.0 copy.48.wstep_ref
  12.7 20.9 %start.1.nb_ref.normed_ref = bf16[1024,1536]{1,0:T(8,128)(2,1)} custom-call(f32[128,1536]{1,0:T(8,128)} %refs_1_.3, f32[2,1536]{1,0:T(2,128)} %refs_3_.7), custom_call_target="tpu_custom_call" | custom-call | flops 8589934592 | bytes 16777216 | tf_op jit(solution)/shard_map/start/pallas_call | solution.py:820
  33.6 19.8 %forward.2 = (f32[1024,384]{1,0:T(8,128)}, bf16[1024,384]{1,0:T(8,128)(2,1)}, f32[1024,384]{1,0:T(8,128)}, bf16[1024,256]{1,0:T(8,128)(2,1)}, f32[1024,256]{1,0:...) custom-call(bf16[1024,1536]{1,0:T(8,128)(2,1)} %start.1.nb_ref.norme, ...), custom_call_target="tpu_custom_call" | custom-call | flops 6039797760 | bytes 16777216 | tf_op jit(solution)/shard_map/forward/pallas_call | solution.py:239
  53.5 37.7 %between.1 = (bf16[1024,1536]{1,0:T(8,128)(2,1)}, f32[128,1536]{1,0:T(8,128)}, f32[128,1536]{1,0:T(8,128)}, f32[128,1]{1,0:T(8,128)}) custom-call(bf16[1024,1536]{1,0:T(8,128)(2,1)} %get-tuple-element.93.refs_0_, f32[64,128]{1,0:T(8,128)} %get-tuple-element.94.refs_1_, f32[128,1536]{1,0:T(8,128)} %refs_1_.3, f32[2,1536]{1,0:T(2,128)} %refs_3_.7), custom_call_target="tpu_custom_call" | custom-call | flops 8589934592 | bytes 16777216 | tf_op jit(solution)/shard_map/between/pallas_call | solution.py:820
  91.2 19.8 %forward.3 = (f32[1024,384]{1,0:T(8,128)}, bf16[1024,384]{1,0:T(8,128)(2,1)}, f32[1024,384]{1,0:T(8,128)}, bf16[1024,256]{1,0:T(8,128)(2,1)}, f32[1024,256]{1,0:...) custom-call(bf16[1024,1536]{1,0:T(8,128)(2,1)} %get-tuple-element.95, ...), custom_call_target="tpu_custom_call" | custom-call | flops 6039797760 | bytes 16777216 | tf_op jit(solution)/shard_map/forward/pallas_call | solution.py:239
  111.0 38.1 %turn.1 = (bf16[1024,1536]{1,0:T(8,128)(2,1)}, f32[64,128]{1,0:T(8,128)}, f32[128,1536]{1,0:T(8,128)}) custom-call(bf16[1024,1536]{1,0:T(8,128)(2,1)} %get-tuple-element.96.refs_0_, f32[64,128]{1,0:T(8,128)} %get-tuple-element.97.refs_1_, f32[128,1536]{1,0:T(8,128)} %get-tuple-element.98.refs_2_.refs_1_, f32[128,1536]{1,0:T(8,128)} %refs_2_.3), custom_call_target="tpu_custom_call" | custom-call | flops 8589934592 | bytes 16777216 | tf_op jit(solution)/shard_map/turn/pallas_call | solution.py:820
  149.2 34.8 %backward.2 = (bf16[1024,384]{1,0:T(8,128)(2,1)}, bf16[1024,384]{1,0:T(8,128)(2,1)}, bf16[1024,256]{1,0:T(8,128)(2,1)}, bf16[1024,6]{1,0:T(8,128)(2,1)}, bf16[10...) custom-call(bf16[1024,1536]{1,0:T(8,128)(2,1)} %get-tuple-element.10, ...), custom_call_target="tpu_custom_call" | custom-call | flops 12079595520 | bytes 16777216 | tf_op jit(solution)/shard_map/backward/pallas_call | solution.py:474
  184.0 10.2 %weights.2 = (bf16[4,2,384,384]{3,2,1,0:T(8,128)(2,1)}, bf16[1536,256]{1,0:T(8,128)(2,1)}, f32[6,1536]{1,0:T(8,128)}, bf16[4,384,384]{2,1,0:T(8,128)(2,1)}) custom-call(bf16[1024,1536]{1,0:T(8,128)(2,1)} %get-tuple-element.95.nb_ref.normed_ref, bf16[1024,1536]{1,0:T(8,128)(2,1)} %get-tuple-element.100.sent_ref, bf16[1024,384]{1,0:T(8,128)(2,1)} %get-tuple-element.111.sc_ref, ...), custom_call_target="tpu_custom_call" | custom-call | flops 4429185024 | bytes 16777216 | tf_op jit(solution)/shard_map/weights/pallas_call | solution.py:538
  194.2 4.1 pad_maximum_fusion.1
  198.3 0.2 reduce-scatter.3.cloned.1.call-start
  198.6 38.6 %back.1 = (bf16[1024,1536]{1,0:T(8,128)(2,1)}, f32[64,128]{1,0:T(8,128)}, f32[128,1536]{1,0:T(8,128)}, f32[1,1536]{1,0:T(1,128)}) custom-call(bf16[1024,1536]{1,0:T(8,128)(2,1)} %get-tuple-element.118.refs_0_, f32[128,1536]{1,0:T(8,128)} %get-tuple-element.98.refs_2_.refs_1_, f32[128,1536]{1,0:T(8,128)} %refs_2_.3, f32[2,1536]{1,0:T(2,128)} %refs_3_.7, ...), custom_call_target="tpu_custom_call" | custom-call | flops 8589934592 | bytes 16777216 | tf_op jit(solution)/shard_map/back/pallas_call | solution.py:820
  237.2 34.9 %backward.3 = (bf16[1024,384]{1,0:T(8,128)(2,1)}, bf16[1024,384]{1,0:T(8,128)(2,1)}, bf16[1024,256]{1,0:T(8,128)(2,1)}, bf16[1024,6]{1,0:T(8,128)(2,1)}, bf16[10...) custom-call(bf16[1024,1536]{1,0:T(8,128)(2,1)} %get-tuple-element.12, ...), custom_call_target="tpu_custom_call" | custom-call | flops 12079595520 | bytes 16777216 | tf_op jit(solution)/shard_map/backward/pallas_call | solution.py:474
  272.1 10.2 %weights.3 = (bf16[4,2,384,384]{3,2,1,0:T(8,128)(2,1)}, bf16[1536,256]{1,0:T(8,128)(2,1)}, f32[6,1536]{1,0:T(8,128)}, bf16[4,384,384]{2,1,0:T(8,128)(2,1)}) custom-call(bf16[1024,1536]{1,0:T(8,128)(2,1)} %start.1.nb_ref.normed_ref, bf16[1024,1536]{1,0:T(8,128)(2,1)} %get-tuple-element.121.sent_ref, bf16[1024,384]{1,0:T(8,128)(2,1)} %get-tuple-element.132.sc_ref, ...), custom_call_target="tpu_custom_call" | custom-call | flops 4429185024 | bytes 16777216 | tf_op jit(solution)/shard_map/weights/pallas_call | solution.py:538
  282.3 4.2 pad_maximum_fusion
  286.5 1.1 copy-done.4
  287.6 0.2 copy-done.5
  287.8 0.1 pad_maximum_fusion.3
  288.1 1.3 copy.58
  289.6 0.6 pad_maximum_fusion.6.small_ref
  290.4 20.6 %end.1 = (f32[128,1536]{1,0:T(8,128)}, f32[1,1536]{1,0:T(1,128)}) custom-call(bf16[1024,1536]{1,0:T(8,128)(2,1)} %get-tuple-element.139.refs_0_, f32[128,1536]{1,0:T(8,128)} %refs_1_.3, f32[128,1536]{1,0:T(8,128)} %get-tuple-element.140.refs_2_, f32[2,1536]{1,0:T(2,128)} %refs_3_.7), custom_call_target="tpu_custom_call" | custom-call | flops 8589934592 | bytes 16777216 | tf_op jit(solution)/shard_map/end/pallas_call | solution.py:820
  311.0 0.7 fusion.1
  311.7 0.7 pad_maximum_fusion.5.wide_ref
  312.4 84.1 %sums.1 = (f32[2,48,256]{2,1,0:T(8,128)}, f32[2,9,384]{2,1,0:T(8,128)}, f32[2,2,12,1536]{3,2,1,0:T(8,128)}) custom-call(bf16[3072,256]{1,0:T(8,128)(2,1)} %bitcast.56, f32[2,9,384]{2,1,0:T(8,128)} %pad_maximum_fusion.6.small_ref, f32[2,12,1536]{2,1,0:T(8,128)} %pad_maximum_fusion.5.wide_ref), custom_call_target="tpu_custom_call" | custom-call | flops 8589934592 | bytes 16777216 | tf_op jit(solution)/shard_map/sums/pallas_call | solution.py:895
  396.6 1.0 fusion.5
  397.6 0.6 slice.103
  398.2 0.6 copy.69
  398.8 1.3 slice.90
  400.1 0.9 fusion.6
  401.1 0.7 reduce_sum.9
  401.8 0.6 copy.71
  402.3 0.6 copy.72
  402.9 0.6 copy.70
  403.5 0.6 constant_dynamic-slice_fusion.1
  404.1 1.3 fusion.7
  405.4 1.1 slice.102
  406.6 1.1 slice.101
  407.8 1.6 pad_maximum_fusion.2
  409.4 0.5 copy-done.1
  410.0 1.1 pad_maximum_fusion.4
  411.1 0.9 copy.76
  412.0 0.9 copy.77
  412.8 0.6 copy.78
  (79 shorter events, 1.2 us)
Async XLA Ops:
  7.2 398.2 %reduce-scatter.5.cloned.1.call-start = ((), (), s32[]{:S(2)}) async-start(), calls=%async_computation.3 | async-start | bytes 4423680 | tf_op jit(solution)/shard_map/reduce_scatter | solution.py:940
  9.7 23.9 %copy-start.6 = (f32[8,1024]{1,0:T(8,128)}, f32[8,1024]{1,0:T(8,128)S(1)}, u32[]{:S(2)}) copy-start(f32[8,1024]{1,0:T(8,128)S(1)} %stack.50.segrow_ref) | copy-start | bytes 98308
  198.3 208.2 %reduce-scatter.3.cloned.1.call-start = ((), (), s32[]{:S(2)}) async-start(), calls=%async_computation.2 | async-start | bytes 4423680 | tf_op jit(solution)/shard_map/reduce_scatter | solution.py:940
  286.4 1.1 copy-start.4
  286.4 1.4 copy-start.5
  287.9 1.5 copy-start.24
  287.9 1.5 copy-start.23
  288.0 1.5 copy-start.26
  288.0 1.5 copy-start.25
  288.0 1.5 copy-start.11
  288.0 1.5 copy-start.15
  288.0 1.5 copy-start.16
  288.0 1.5 copy-start.17
  288.0 1.5 copy-start.12
  288.0 1.5 copy-start.18
  288.1 1.5 copy-start.19
  288.1 1.5 copy-start.20
  288.1 2.2 copy-start.8
  288.1 2.2 copy-start.10
  288.1 2.2 copy-start.13
  288.1 2.2 copy-start.21
  290.3 20.7 %copy-start.9 = (f32[6,1536]{1,0:T(8,128)S(1)}, f32[6,1536]{1,0:T(8,128)}, u32[]{:S(2)}) copy-start(f32[6,1536]{1,0:T(8,128)} %get-tuple-element.156) | copy-start | bytes 110596
  290.3 20.7 %copy-start.14 = (f32[4,256]{1,0:T(4,128)S(1)}, f32[4,256]{1,0:T(4,128)}, u32[]{:S(2)}) copy-start(f32[4,256]{1,0:T(4,128)} %get-tuple-element.158) | copy-start | bytes 12292
  290.3 20.7 %copy-start.22 = (f32[1,256]{1,0:T(1,128)S(1)}, f32[1,256]{1,0:T(1,128)}, u32[]{:S(2)}) copy-start(f32[1,256]{1,0:T(1,128)} %get-tuple-element.159) | copy-start | bytes 3076
  407.7 1.6 copy-start
  407.7 2.2 copy-start.1
  409.4 1.7 copy-start.2
  409.9 2.0 copy-start.3
  410.0 2.9 copy-start.7
Sparse Core Ops, SparseCore 0:
  198.5 66.8 reduce-scatter.4
  286.6 82.4 reduce-scatter.2

commit v3 on v0

v3 whole, which is shorter than its diff:
```python
import functools
from types import SimpleNamespace
from typing import NamedTuple

import jax
import jax.numpy as jnp
from jax import lax
from jax.experimental import pallas as pl
from jax.experimental.pallas import tpu as pltpu
from jax.sharding import PartitionSpec as P

LAYERS = 2
SIZE = 128
AXIS = "tensor"
DATA = "dp"
EPS = 1e-05
HIGH = lax.Precision.HIGHEST
F32 = jnp.float32
BF = jnp.bfloat16
VM = 67_000_000


def cost_of(flops, moved=1 << 24):
    return pl.CostEstimate(flops=flops, bytes_accessed=moved, transcendentals=0)


class Weights(NamedTuple):
    norm_gain: jax.Array
    inner_weight: jax.Array
    state_weight: jax.Array
    step_weight: jax.Array
    step_bias: jax.Array
    decay_log: jax.Array
    skip_gain: jax.Array
    conv_weight: jax.Array
    conv_bias: jax.Array
    state_conv_weight: jax.Array
    state_conv_bias: jax.Array
    gate_gain: jax.Array
    out_weight: jax.Array


def dot(a, b):
    return lax.dot_general(a, b, (((1,), (0,)), ((), ())), preferred_element_type=F32)


def dot_t(a, b):
    return lax.dot_general(a, b, (((1,), (1,)), ((), ())), preferred_element_type=F32)


def t_dot(a, b):
    return lax.dot_general(a, b, (((0,), (0,)), ((), ())), preferred_element_type=F32)


def exact(a, b):
    return lax.dot_general(
        a, b, (((1,), (0,)), ((), ())), preferred_element_type=F32, precision=HIGH
    )


def sigmoid(x):
    return 1.0 / (1.0 + jnp.exp(-x))


def softplus(x):
    return jnp.maximum(x, 0.0) + jnp.log1p(jnp.exp(-jnp.abs(x)))


def tiles_of(inner, width):
    return [
        (start, min(128, inner - start), start // width, min(128, inner - start) // width)
        for start in range(0, inner, 128)
    ]


def expand(cols, inner, width):
    rows = cols.shape[0]
    parts = []
    for _, wide, first, number in tiles_of(inner, width):
        lane = lax.broadcasted_iota(jnp.int32, (rows, wide), 1)
        value = jnp.broadcast_to(cols[:, first : first + 1], (rows, wide))
        for j in range(1, number):
            value = jnp.where(lane >= j * width, cols[:, first + j : first + j + 1], value)
        parts.append(value)
    return parts[0] if len(parts) == 1 else jnp.concatenate(parts, axis=1)


def head_sum_matrix(inner, heads, width):
    row = lax.broadcasted_iota(jnp.int32, (inner, heads), 0)
    col = lax.broadcasted_iota(jnp.int32, (inner, heads), 1)
    return ((row >= col * width) & (row < (col + 1) * width)).astype(BF)


def head_sum(value, inner, heads, width):
    ones = head_sum_matrix(inner, heads, width)
    high = value.astype(BF)
    low = (value - high.astype(F32)).astype(BF)
    return dot(high, ones) + dot(low, ones)


def head_split(tile, width, number):
    if number == 1:
        return tile
    lane = lax.broadcasted_iota(jnp.int32, tile.shape, 1)
    zero = jnp.zeros_like(tile)
    return jnp.concatenate(
        [
            jnp.where((lane >= j * width) & (lane < (j + 1) * width), tile, zero)
            for j in range(number)
        ],
        axis=0,
    )


def pair_mask(seg_col, seg_row):
    rows, cols = seg_col.shape[0], seg_row.shape[1]
    row = lax.broadcasted_iota(jnp.int32, (rows, cols), 0)
    col = lax.broadcasted_iota(jnp.int32, (rows, cols), 1)
    return (row >= col) & (seg_col == seg_row)


def lower_ones(size):
    row = lax.broadcasted_iota(jnp.int32, (size, size), 0)
    col = lax.broadcasted_iota(jnp.int32, (size, size), 1)
    return (row >= col).astype(F32)


def turned(value):
    return jnp.transpose(value)


def column_of(tile):
    rows = tile.shape[1]
    return jnp.transpose(jnp.broadcast_to(tile[0:1, :], (rows, rows)))[:, 0:1]


def tile_of(column):
    rows = column.shape[0]
    return jnp.transpose(jnp.broadcast_to(column, (rows, rows)))[0:8, :]


def later_ones(seg_col, seg_row):
    rows, cols = seg_col.shape[0], seg_row.shape[1]
    row = lax.broadcasted_iota(jnp.int32, (rows, cols), 0)
    col = lax.broadcasted_iota(jnp.int32, (rows, cols), 1)
    return ((row <= col) & (seg_col == seg_row)).astype(F32)


def earlier_ones(seg_col, seg_row):
    rows, cols = seg_col.shape[0], seg_row.shape[1]
    row = lax.broadcasted_iota(jnp.int32, (rows, cols), 0)
    col = lax.broadcasted_iota(jnp.int32, (rows, cols), 1)
    return ((row > col) & (seg_col == seg_row)).astype(F32)


def token_meta(segment, size):
    tokens = segment.shape[0]
    seg = segment.astype(F32)

    def back(k):
        return jnp.concatenate([jnp.full((k,), -1.0, F32), seg[:-k]])

    blocks = seg.reshape(-1, size)
    gone = jnp.full((1,), -1.0, F32)
    before = jnp.concatenate([gone, blocks[:-1, -1]])
    after = jnp.concatenate([blocks[1:, 0], gone])
    per = lambda v: jnp.broadcast_to(v[:, None], blocks.shape)
    end = per(blocks[:, -1])
    columns = [
        seg,
        (back(1) == seg).astype(F32),
        (back(2) == seg).astype(F32),
        (back(3) == seg).astype(F32),
        (blocks == per(before)).astype(F32).reshape(-1),
        (blocks == end).astype(F32).reshape(-1),
        (end == per(before)).astype(F32).reshape(-1),
        (blocks == per(after)).astype(F32).reshape(-1),
    ]
    rows = jnp.stack(columns)
    return rows.T, rows


def span_of(dims):
    found = [0]
    for d in dims:
        found = found + [r ^ d for r in found]
    return found


def most_first(offsets):
    return sorted(offsets, key=lambda r: -bin(r).count("1"))


class Cube:
    def __init__(self, size):
        self.size = size
        self.links = [1 << b for b in range(1, size.bit_length() - 1)]
        self.orders = [self.links, self.links[::-1]]
        self.offsets = most_first(span_of(self.links))

    def gather_dims(self, q):
        return self.orders[q] + [1]

    def gather_last(self, q, r):
        return max([i for i, d in enumerate(self.gather_dims(q)) if r & d], default=-1)

    def gather_steps(self, q):
        found = [r for r in span_of(self.links) if r]
        return sorted(found, key=lambda r: (self.gather_last(q, r), r & (r - 1) != 0))


def reduce_steps(order):
    steps = []
    for i, d in enumerate(order):
        for s in most_first(span_of(order[i + 1 :])):
            steps.append((i, d ^ s))
    return steps + [(len(order), 0)]


def arrival_slots(order, first=0):
    found = {}
    for i, r in reduce_steps(order):
        for j in range(i):
            found[(j, r)] = first + len(found)
    return found


def remote(src, dst, send, recv, target, axis=AXIS):
    return pltpu.make_async_remote_copy(
        src_ref=src, dst_ref=dst, send_sem=send, recv_sem=recv,
        device_id={axis: target}, device_id_type=pl.DeviceIdType.MESH,
    )


def greet(targets, across=()):
    barrier = pltpu.get_barrier_semaphore()
    for axis, group in ((AXIS, targets), (DATA, across)):
        for target in group:
            pl.semaphore_signal(barrier, inc=1, device_id={axis: target}, device_id_type=pl.DeviceIdType.MESH)
    pl.semaphore_wait(barrier, len(targets) + len(across))


def rows_of(block, rows, many=1):
    return pl.ds(pl.multiple_of(block * rows, rows), rows * many)


def dma(*shape):
    return pltpu.SemaphoreType.DMA(shape)


def gather_sems(ex):
    return dma(2, ex.size), dma(2, ex.size)


def gather_rows(ex, rows, row_buf, out, sems, visit, ahead=None):
    me = lax.axis_index(AXIS)
    send_sem, recv_sem = sems
    half = rows // 2
    copies, arrived = {}, set()

    def forward(q, r):
        dims = ex.gather_dims(q)
        place = pl.ds(pl.multiple_of((me ^ r) * rows + q * half, half), half)
        src = row_buf.at[pl.ds(q * half, half), :] if r == 0 else out.at[place, :]
        for i in range(ex.gather_last(q, r) + 1, len(dims)):
            beyond = r ^ dims[i]
            yield beyond, remote(src, out.at[place, :], send_sem.at[q, beyond], recv_sem.at[q, beyond], me ^ dims[i])

    def need(q, r):
        if (q, r) not in arrived:
            copies[(q, r)].wait_recv()
            arrived.add((q, r))
            for beyond, copy in forward(q, r):
                copy.start()
                copies[(q, beyond)] = copy

    first = [list(forward(q, 0)) for q in range(2)]
    for i in range(len(first[0])):
        for q in range(2):
            beyond, copy = first[q][i]
            copy.start()
            copies[(q, beyond)] = copy
    out[rows_of(me, rows), :] = row_buf[...]
    if ahead is not None:
        ahead()
    steps = [ex.gather_steps(q) for q in range(2)]
    visits = sorted(span_of(ex.links), key=lambda g: (ex.gather_last(0, g), g & (g - 1) != 0))
    k = 0
    for g in visits:
        while g and not all((q, g) in arrived for q in range(2)):
            for q in range(2):
                need(q, steps[q][k])
            k += 1
        for q in range(2):
            need(q, g ^ 1)
        visit(g)
    return list(copies.values())


def reduce_scratch(ex, rows, depth):
    slots, half = ex.size // 2, rows // 2
    return dict(
        pair=pltpu.VMEM((slots, rows, depth), BF),
        stage=pltpu.VMEM((2 * slots, half, depth), BF),
        got=pltpu.VMEM((2 * (slots - 1), half, depth), BF),
    )


def reduce_sems(ex):
    slots = ex.size // 2
    return dma(slots), dma(slots), dma(2 * slots), dma(2 * (slots - 1))


def reduce_rows(ex, rows, part, pair, stage, got, sems, produce, pending):
    me = lax.axis_index(AXIS)
    pair_send, pair_recv, link_send, link_recv = sems
    n, half = ex.size, rows // 2
    slot_of = {r: i for i, r in enumerate(ex.offsets)}
    steps = [reduce_steps(order) for order in ex.orders]
    slots = [arrival_slots(order, q * (n // 2 - 1)) for q, order in enumerate(ex.orders)]
    waiting = list(ex.offsets)
    pairs, ready, arrivals, final = {}, set(), {}, [None, None]

    def advance():
        r = waiting.pop(0)
        produce(r)
        i = slot_of[r]
        pairs[r] = remote(part.at[rows_of(me ^ r ^ 1, rows), :], pair.at[i], pair_send.at[i], pair_recv.at[i], me ^ 1)
        pairs[r].start()

    advance()
    for k in range(len(steps[0])):
        if waiting:
            advance()
        for q in range(2):
            i, r = steps[q][k]
            while r not in pairs:
                advance()
            if r not in ready:
                pairs[r].wait_recv()
                ready.add(r)
            own = part[pl.ds(pl.multiple_of((me ^ r) * rows + q * half, half), half), :]
            value = own.astype(F32) + pair[slot_of[r], pl.ds(q * half, half), :].astype(F32)
            for j in range(i):
                arrivals[(q, j, r)].wait_recv()
                value = value + got[slots[q][(j, r)]].astype(F32)
            if r == 0:
                final[q] = value
                continue
            d = ex.orders[q][i]
            s = q * (n // 2) + slot_of[r]
            stage[s] = value.astype(BF)
            at = slots[q][(i, r ^ d)]
            copy = remote(stage.at[s], got.at[at], link_send.at[s], link_recv.at[at], me ^ d)
            copy.start()
            arrivals[(q, i, r ^ d)] = copy
            pending.append(copy)
    pending.extend(pairs.values())
    return jnp.concatenate(final, axis=0)


def row_scale_of(resid):
    return lax.rsqrt(jnp.mean(resid * resid, axis=1, keepdims=True) + EPS)


def group_rows(ex, g, rows):
    me = lax.axis_index(AXIS)
    return pl.ds(pl.multiple_of(((me ^ g) // 2) * (2 * rows), 2 * rows), 2 * rows)


class Sizes(NamedTuple):
    tokens: int
    rows: int
    depth: int
    inner: int
    heads: int
    both: int
    taps: int
    inner_all: int
    across: int

    @property
    def width(self):
        return self.inner // self.heads

    @property
    def half(self):
        return self.both // 2

    @property
    def count(self):
        return self.tokens // SIZE


def weight_scratch(z, layers):
    return dict(
        win=pltpu.VMEM((layers, 2, z.depth, z.inner), BF),
        wst=pltpu.VMEM((layers, z.depth, z.both), BF),
        wstep=pltpu.VMEM((layers, z.heads, z.depth), BF),
        wout=pltpu.VMEM((layers, z.inner, z.depth), BF),
        weight_sem=dma(LAYERS, 4),
    )


def weight_loads(s, a, layer, slot):
    return [
        pltpu.make_async_copy(src.at[layer], dst.at[slot], s.weight_sem.at[layer, i])
        for i, (src, dst) in enumerate(
            ((a.inner_weight, s.win), (a.state_weight, s.wst), (a.step_weight, s.wstep), (a.out_weight, s.wout))
        )
    ]


def saved_shapes(z):
    t, i = z.tokens, z.inner
    return dict(
        normed=((t, z.depth), BF), gate=((t, i), F32), pre_v=((t, i), F32), y=((t, i), F32), pre_s=((t, z.both), F32),
        step_in=((t, z.heads), F32), value=((t, i), BF), raw=((t, z.both), BF), scaled=((t, i), BF),
        entering=((z.count, z.half, i), BF),
    )


def mix_forward(z, layer, s, a, meta, segrow):
    at = slice(layer, layer + 1)
    inner, width, half = z.inner, z.width, z.half
    s.state[...] = jnp.zeros_like(s.state)
    group = 2 if z.count % 2 == 0 else 1

    def chunk(c, before):
        rows = pl.ds(pl.multiple_of(c * SIZE, SIZE), SIZE)
        window = pl.ds(pl.multiple_of(c * SIZE, SIZE), SIZE + 8)
        m = meta[rows, :]

        def conv(buf, w_ref, b_ref):
            win = buf[window, :]
            total = b_ref[at, :] + w_ref[layer, 0:1, :] * win[8:, :]
            for k in range(1, z.taps):
                total = total + w_ref[layer, k : k + 1, :] * (win[8 - k : 8 - k + SIZE, :] * m[:, k : k + 1])
            return total, win[8:, :]

        pre_v, value = conv(s.vbuf, a.conv_weight, a.conv_bias)
        pre_s, raw = conv(s.sbuf, a.state_conv_weight, a.state_conv_bias)
        s.value[rows, :] = value.astype(BF)
        s.raw[rows, :] = raw.astype(BF)
        s.pre_v[rows, :] = pre_v
        s.pre_s[rows, :] = pre_s
        x = pre_v * sigmoid(pre_v)
        st = pre_s * sigmoid(pre_s)
        b_mat = st[:, :half].astype(BF)
        c_mat = st[:, half:].astype(BF)
        dt = softplus(s.step_in[rows, :] + a.step_bias[at, :])
        log_decay = -dt * jnp.exp(a.decay_log[at, :])
        cum = exact(lower_ones(SIZE), log_decay)
        cum_t = turned(cum)
        last = cum[SIZE - 1 : SIZE, :]
        xt = (x * expand(dt, inner, width)).astype(BF)
        from_state = jnp.exp(cum) * m[:, 4:5]
        to_end = jnp.exp(last - cum) * m[:, 5:6]
        carry = jnp.exp(last) * m[0:1, 6:7]
        before_b = before.astype(BF)
        s.entering[c] = before_b
        scores = dot_t(c_mat, b_mat)
        mask = pair_mask(m[:, 0:1], segrow[0:1, rows])
        parts = []
        for start, wide, first, number in tiles_of(inner, width):
            mats = []
            for h in range(first, first + number):
                differ = cum[:, h : h + 1] - cum_t[h : h + 1, :]
                mats.append((jnp.exp(jnp.where(mask, differ, -1e30)) * scores).astype(BF))
            left = mats[0] if number == 1 else jnp.concatenate(mats, axis=1)
            parts.append(dot(left, head_split(xt[:, start : start + wide], width, number)))
        intra = parts[0] if len(parts) == 1 else jnp.concatenate(parts, axis=1)
        inter = dot(c_mat, before_b) * expand(from_state, inner, width)
        y = intra + inter + expand(a.skip_gain[at, :], inner, width) * x
        s.y[rows, :] = y
        ended = (xt.astype(F32) * expand(to_end, inner, width)).astype(BF)
        after = expand(carry, inner, width) * before + t_dot(b_mat, ended)
        gate = s.gate[rows, :]
        gated = y * (gate * sigmoid(gate))
        square = jnp.sum(gated * gated, axis=1, keepdims=True)
        tile = tile_of(square)
        per = SIZE // z.rows if SIZE > z.rows else 1
        wide = SIZE // per
        for k in range(per):
            s.squares[c * per + k] = tile[:, k * wide : (k + 1) * wide]
        s.scaled[rows, :] = (gated * a.gate_gain[at, :]).astype(BF)
        return after

    def body(i, carry):
        before = s.state[...]
        for k in range(group):
            before = chunk(i * group + k, before)
        s.state[...] = before
        return carry

    lax.fori_loop(0, z.count // group, body, 0)


def forward_kernel(ex, z, names_in, names_out, names_scratch, *refs):
    count_in, count_out = len(names_in), len(names_out)
    a = SimpleNamespace(**dict(zip(names_in, refs)))
    o = SimpleNamespace(**dict(zip(names_out, refs[count_in:])))
    s = SimpleNamespace(**dict(zip(names_scratch, refs[count_in + count_out :])))
    me = lax.axis_index(AXIS)
    n = ex.size
    greet([me ^ r for r in range(1, n)])
    loads = [weight_loads(s, a, layer, layer) for layer in range(LAYERS)]
    for copy in loads[0] + loads[1]:
        copy.start()
    s.vbuf[0:8, :] = jnp.zeros((8, z.inner), F32)
    s.sbuf[0:8, :] = jnp.zeros((8, z.both), F32)
    pending, saves = [], []
    hidden = a.residual[...]
    for layer in range(LAYERS):
        s.row_buf[...] = (hidden * row_scale_of(hidden) * a.norm_gain[layer : layer + 1, :]).astype(BF)
        normed = s.normed.at[layer]
        for copy in saves:
            copy.wait()
        saves = []

        def project(g, layer=layer, normed=normed):
            if g == 0:
                for copy in loads[layer]:
                    copy.wait()
            here = group_rows(ex, g, z.rows)
            beyond = pl.ds(pl.multiple_of(((me ^ g) // 2) * (2 * z.rows) + 8, 8), 2 * z.rows)
            nb = normed[here, :]
            s.gate[here, :] = dot(nb, s.win[layer, 0])
            s.vbuf[beyond, :] = dot(nb, s.win[layer, 1])
            s.sbuf[beyond, :] = dot(nb, s.wst[layer])
            s.step_in[here, :] = dot_t(nb, s.wstep[layer])

        sent = gather_rows(ex, z.rows, s.row_buf, normed, (s.gather_send.at[layer], s.gather_recv.at[layer]), project)
        mix_forward(z, layer, s, a, a.meta, a.segrow)
        for i, name in enumerate(names_out[: len(saved_shapes(z))]):
            src = normed if i == 0 else getattr(s, name)
            saves.append(pltpu.make_async_copy(src, getattr(o, name).at[layer], s.save_sem.at[layer, i]))
            saves[-1].start()
        for copy in sent:
            copy.wait_send()

        def produce(g, layer=layer):
            here = group_rows(ex, g, z.rows)
            s.part[here, :] = dot(s.scaled[here, :], s.wout[layer]).astype(BF)

        squares = []
        for r in range(1, n):
            squares.append(
                remote(s.squares.at[me ^ r], s.square_got.at[layer, r], s.square_send.at[layer, r], s.square_recv.at[layer, r], me ^ r)
            )
            squares[-1].start()
        links = []
        total = reduce_rows(
            ex, z.rows, s.part, s.pair, s.stage, s.got,
            (s.pair_send.at[layer], s.pair_recv.at[layer], s.link_send.at[layer], s.link_recv.at[layer]), produce, links,
        )
        square = s.squares[me]
        for r, copy in enumerate(squares, 1):
            copy.wait_recv()
            square = square + s.square_got[layer, r]
        gate = lax.rsqrt(column_of(square) / z.inner_all + EPS)
        mixed = gate * total
        hidden = hidden + mixed
        if layer + 1 < LAYERS:
            o.resids[layer] = hidden
            o.mixeds[layer] = mixed
            o.gates[layer] = gate
        for copy in links + squares:
            copy.wait_send()
    o.block_output[...] = hidden
    grad = a.cotangent[...]
    o.sent[...] = (gate * grad).astype(BF)
    o.mean[...] = tile_of(-0.5 * gate * gate * jnp.sum(mixed * grad, axis=1, keepdims=True))
    for copy in saves:
        copy.wait()


def run_kernel(kernel, ex, z, inputs, outputs, scratch, collective, name):
    vm, anywhere = pl.BlockSpec(memory_space=pltpu.VMEM), pl.BlockSpec(memory_space=pl.ANY)
    made = pl.pallas_call(
        functools.partial(kernel, ex, z, tuple(inputs), tuple(outputs), tuple(scratch)),
        out_shape=tuple(jax.ShapeDtypeStruct(shape, kind) for shape, kind, _ in outputs.values()),
        in_specs=[vm if inside else anywhere for _, inside in inputs.values()],
        out_specs=tuple(vm if inside else anywhere for _, _, inside in outputs.values()),
        scratch_shapes=list(scratch.values()),
        compiler_params=pltpu.CompilerParams(collective_id=collective, has_side_effects=True, vmem_limit_bytes=VM),
        cost_estimate=cost_of(1 << 35),
        name=name,
    )(*[array for array, _ in inputs.values()])
    return SimpleNamespace(**dict(zip(outputs, made)))


def small_inputs(w):
    return dict(
        norm_gain=(w.norm_gain, True), step_bias=(w.step_bias, True), decay_log=(w.decay_log, True),
        skip_gain=(w.skip_gain, True), conv_weight=(w.conv_weight, True), conv_bias=(w.conv_bias, True),
        state_conv_weight=(w.state_conv_weight, True), state_conv_bias=(w.state_conv_bias, True), gate_gain=(w.gate_gain, True),
        inner_weight=(w.inner_weight, False), state_weight=(w.state_weight, False), step_weight=(w.step_weight, False),
        out_weight=(w.out_weight, False),
    )


def forward_pass(ex, z, residual, cotangent, meta, segrow, w):
    n = ex.size
    saved = saved_shapes(z)
    inputs = dict(residual=(residual, True), cotangent=(cotangent, True), meta=(meta, True), segrow=(segrow, True), **small_inputs(w))
    rows = (z.rows, z.depth)
    outputs = {k: ((LAYERS,) + shape, kind, False) for k, (shape, kind) in saved.items()}
    outputs.update(
        resids=((LAYERS - 1,) + rows, F32, True), mixeds=((LAYERS - 1,) + rows, F32, True),
        gates=((LAYERS - 1, z.rows, 1), F32, True), block_output=(rows, F32, True),
        sent=(rows, BF, True), mean=((8, z.rows), F32, True),
    )
    scratch = {k: pltpu.VMEM(shape, kind) for k, (shape, kind) in saved.items()}
    scratch.update(normed=pltpu.VMEM((LAYERS, z.tokens, z.depth), BF))
    scratch.update(weight_scratch(z, LAYERS))
    scratch.update(reduce_scratch(ex, z.rows, z.depth))
    slots = n // 2
    scratch.update(
        vbuf=pltpu.VMEM((z.tokens + 8, z.inner), F32), sbuf=pltpu.VMEM((z.tokens + 8, z.both), F32),
        state=pltpu.VMEM((z.half, z.inner), F32), part=pltpu.VMEM((z.tokens, z.depth), BF), row_buf=pltpu.VMEM(rows, BF),
        squares=pltpu.VMEM((n, 8, z.rows), F32), square_got=pltpu.VMEM((LAYERS, n, 8, z.rows), F32),
        square_send=dma(LAYERS, n), square_recv=dma(LAYERS, n), save_sem=dma(LAYERS, len(saved)),
        gather_send=dma(LAYERS, 2, n), gather_recv=dma(LAYERS, 2, n), pair_send=dma(LAYERS, slots), pair_recv=dma(LAYERS, slots),
        link_send=dma(LAYERS, 2 * slots), link_recv=dma(LAYERS, 2 * (slots - 1)),
    )
    return run_kernel(forward_kernel, ex, z, inputs, outputs, scratch, 0, "forward")


class Piece:
    def __init__(self, across, own, stage, got, send, recv):
        self.order = [1 << b for b in range(across.bit_length() - 1)]
        self.own, self.stage, self.got, self.send, self.recv = own, stage, got, send, recv
        self.slots = arrival_slots(self.order)
        self.row = lax.axis_index(DATA)
        self.arrivals, self.sent = {}, []

    def value(self, i, r):
        total = self.own[self.row ^ r].astype(F32)
        for j in range(i):
            self.arrivals[(j, r)].wait_recv()
            total = total + self.got[self.slots[(j, r)]].astype(F32)
        return total

    def phase(self, k):
        for number, (i, r) in enumerate(reduce_steps(self.order)):
            if i != k or r == 0:
                continue
            src = self.own.at[self.row ^ r]
            if i:
                self.stage[number] = self.value(i, r).astype(BF)
                src = self.stage.at[number]
            d = self.order[i]
            at = self.slots[(i, r ^ d)]
            copy = remote(src, self.got.at[at], self.send.at[number], self.recv.at[at], self.row ^ d, DATA)
            copy.start()
            self.arrivals[(i, r ^ d)] = copy
            self.sent.append(copy)

    def last(self):
        total = self.value(len(self.order), 0)
        for copy in self.sent:
            copy.wait_send()
        return total


def mix_backward(z, layer, s, a, meta, segrow):
    at = slice(layer, layer + 1)
    inner, width, half, heads, taps = z.inner, z.width, z.half, z.heads, z.taps
    s.state[...] = jnp.zeros_like(s.state)
    group = 2 if z.count % 2 == 0 else 1

    def chunk(c, after):
        rows = pl.ds(pl.multiple_of(c * SIZE, SIZE), SIZE)
        m = meta[rows, :]
        y, dy = s.y[rows, :], s.dy[rows, :]
        pre_v, pre_s = s.pre_v[rows, :], s.pre_s[rows, :]
        sig_v, sig_s = sigmoid(pre_v), sigmoid(pre_s)
        x = pre_v * sig_v
        st = pre_s * sig_s
        b_mat = st[:, :half].astype(BF)
        c_mat = st[:, half:].astype(BF)
        raw_step = s.step_in[rows, :] + a.step_bias[at, :]
        dt = softplus(raw_step)
        rate = jnp.exp(a.decay_log[at, :])
        log_decay = -dt * rate
        cum = exact(lower_ones(SIZE), log_decay)
        cum_t = turned(cum)
        last = cum[SIZE - 1 : SIZE, :]
        dt_all = expand(dt, inner, width)
        skip_all = expand(a.skip_gain[at, :], inner, width)
        xt = (x * dt_all).astype(BF)
        dy_b = dy.astype(BF)
        from_state = expand(jnp.exp(cum) * m[:, 4:5], inner, width)
        to_end = expand(jnp.exp(last - cum) * m[:, 5:6], inner, width)
        carry = expand(jnp.exp(last) * m[0:1, 6:7], inner, width)
        scores = dot_t(c_mat, b_mat)
        mask = pair_mask(m[:, 0:1], segrow[0:1, rows])
        d_scores = jnp.zeros((SIZE, SIZE), F32)
        parts = []
        for start, wide, first, number in tiles_of(inner, width):
            dy_split = head_split(dy_b[:, start : start + wide], width, number)
            d_mats = dot_t(dy_split, xt[:, start : start + wide])
            mats = []
            for j in range(number):
                h = first + j
                differ = cum[:, h : h + 1] - cum_t[h : h + 1, :]
                decay = jnp.exp(jnp.where(mask, differ, -1e30))
                mats.append((decay * scores).astype(BF))
                d_scores = d_scores + d_mats[j * SIZE : (j + 1) * SIZE, :] * decay
            left = mats[0] if number == 1 else jnp.concatenate(mats, axis=0)
            parts.append(t_dot(left, dy_split))
        intra = parts[0] if len(parts) == 1 else jnp.concatenate(parts, axis=1)
        d_scores = d_scores.astype(BF)
        before = s.entering[c]
        after_b = after.astype(BF)
        dy_in = (dy * from_state).astype(BF)
        xt_f = xt.astype(F32)
        ended = (xt_f * to_end).astype(BF)
        from_later = dot(b_mat, after_b) * to_end
        d_xt = intra + from_later
        d_c = dot(d_scores, b_mat) + dot_t(dy_in, before)
        d_b = t_dot(d_scores, c_mat) + dot_t(ended, after_b)
        across = carry * jnp.sum(before.astype(F32) * after, axis=0, keepdims=True)
        fresh = carry * after + t_dot(c_mat, dy_in)
        sums = head_sum(
            jnp.concatenate(
                [
                    dy_b.astype(F32) * (y - skip_all * x) - xt_f * intra,
                    xt_f * from_later,
                    x * d_xt,
                    jnp.broadcast_to(across, (8, inner)),
                ],
                axis=0,
            ),
            inner, heads, width,
        )
        seg_col, seg_row = m[:, 0:1], segrow[0:1, rows]
        d_log = (
            exact(later_ones(seg_col, seg_row), sums[0:SIZE])
            + exact(earlier_ones(seg_col, seg_row), sums[SIZE : 2 * SIZE])
            + sums[3 * SIZE : 3 * SIZE + 1]
        )
        d_raw = (sums[2 * SIZE : 3 * SIZE] - rate * d_log) * sigmoid(raw_step)
        s.rd[rows, :] = d_raw.astype(BF)
        d_x = dy * skip_all + d_xt * dt_all
        s.d_pre_v[rows, :] = d_x * (sig_v * (1.0 + pre_v * (1.0 - sig_v)))
        d_st = jnp.concatenate([d_b, d_c], axis=1)
        s.d_pre_s[rows, :] = d_st * (sig_s * (1.0 + pre_s * (1.0 - sig_s)))
        total = lambda v: jnp.sum(v, axis=0, keepdims=True)
        return fresh, (total(dy * x), total(d_raw), total(d_log * log_decay))

    def body(i, sums):
        after = s.state[...]
        for k in range(group):
            after, more = chunk(z.count - 1 - (i * group + k), after)
            sums = tuple(u + v for u, v in zip(sums, more))
        s.state[...] = after
        return sums

    zero = lambda wide: jnp.zeros((1, wide), F32)
    skip, bias, decay = lax.fori_loop(0, z.count // group, body, (zero(inner), zero(heads), zero(heads)))
    s.narrow[layer, taps + 2 : taps + 3, :] = skip
    s.narrow[layer, taps + 3 : taps + 4, 0:heads] = bias
    s.narrow[layer, taps + 4 : taps + 5, 0:heads] = decay

    def conv_body(c, sums):
        rows = pl.ds(pl.multiple_of(c * SIZE, SIZE), SIZE)
        window = pl.ds(pl.multiple_of(c * SIZE, SIZE), SIZE + 8)
        m = meta[window, :]
        more = []
        for src, w_ref, value_ref, dst in ((s.d_pre_v, a.conv_weight, s.value, s.rv), (s.d_pre_s, a.state_conv_weight, s.raw, s.rs)):
            win = src[window, :]
            value = value_ref[rows, :].astype(F32)
            now = win[0:SIZE, :]
            total = w_ref[layer, 0:1, :] * now
            lines = [jnp.sum(now * value, axis=0, keepdims=True)]
            for k in range(1, taps):
                moved = win[k : k + SIZE, :] * m[k : k + SIZE, k : k + 1]
                total = total + w_ref[layer, k : k + 1, :] * moved
                lines.append(jnp.sum(moved * value, axis=0, keepdims=True))
            lines.append(jnp.sum(now, axis=0, keepdims=True))
            dst[rows, :] = total.astype(BF)
            more.extend(lines)
        return tuple(u + v for u, v in zip(sums, more))

    lines = lax.fori_loop(0, z.count, conv_body, (zero(inner),) * (taps + 1) + (zero(z.both),) * (taps + 1))
    for k in range(taps + 1):
        s.narrow[layer, k : k + 1, :] = lines[k]
        s.wide[layer, k : k + 1, :] = lines[taps + 1 + k]


def norm_backward(total, resid, grad, gain):
    scale = row_scale_of(resid)
    weighted = total * gain
    inner = jnp.sum(weighted * resid, axis=1, keepdims=True)
    gain_grad = jnp.sum(total * resid * scale, axis=0, keepdims=True)
    return grad + scale * weighted - resid * (scale * scale * scale * inner / resid.shape[1]), gain_grad


def exchange(src, got, send, recv, place, number, axis):
    copies = [remote(src, got.at[r], send.at[r], recv.at[r], place ^ r, axis) for r in range(1, number)]
    for copy in copies:
        copy.start()
    return copies


def collected(own, got, copies):
    total = own
    for r, copy in enumerate(copies, 1):
        copy.wait_recv()
        total = total + got[r]
    return total


def backward_kernel(ex, z, names_in, names_out, names_scratch, *refs):
    count_in, count_out = len(names_in), len(names_out)
    a = SimpleNamespace(**dict(zip(names_in, refs)))
    o = SimpleNamespace(**dict(zip(names_out, refs[count_in:])))
    s = SimpleNamespace(**dict(zip(names_scratch, refs[count_in + count_out :])))
    me, row = lax.axis_index(AXIS), lax.axis_index(DATA)
    n, across, taps, heads = ex.size, z.across, z.taps, z.heads
    share = z.depth // across
    cells = z.depth // (n * across)
    padded = padded_cells(z, n)
    greet([me ^ r for r in range(1, n)], [row ^ r for r in range(1, across)])
    saved = list(saved_shapes(z))

    def start_loads(layer):
        found = weight_loads(s, a, layer, 0)
        found += [pltpu.make_async_copy(getattr(a, k).at[layer], getattr(s, k), s.save_sem.at[layer, i]) for i, k in enumerate(saved)]
        for copy in found:
            copy.start()
        return found

    loads = start_loads(LAYERS - 1)
    for ref in (s.narrow, s.wide, s.gain):
        ref[...] = jnp.zeros_like(ref)
    s.d_pre_v[z.tokens :, :] = jnp.zeros((8, z.inner), F32)
    s.d_pre_s[z.tokens :, :] = jnp.zeros((8, z.both), F32)
    if padded != cells:
        s.state_part[...] = jnp.zeros_like(s.state_part)
    grad = a.cotangent[...]
    s.row_buf[...] = a.sent[...]
    tile = a.mean[...]
    narrow_copies, outs, older = [None] * LAYERS, [], None

    def finish(piece, k, layer):
        s.done[k] = piece.last()
        target = o.g_out.at[layer] if k == 0 else o.g_inner.at[layer, k - 1]
        copy = pltpu.make_async_copy(s.done.at[k], target, s.done_sem.at[layer, k])
        copy.start()
        return copy

    for layer in range(LAYERS - 1, -1, -1):
        s.mean_own[layer] = tile
        means = []

        def ahead(layer=layer, means=means):
            for r in range(1, n):
                means.append(
                    remote(s.mean_own.at[layer], s.mean_all.at[layer, me], s.mean_send.at[layer, r], s.mean_recv.at[layer, r], me ^ r)
                )
                means[-1].start()
            s.mean_all[layer, me] = s.mean_own[layer]

        def visit(g, layer=layer, means=means, loads=loads):
            if g == 0:
                for copy in loads:
                    copy.wait()
            here = group_rows(ex, g, z.rows)
            first = (me ^ g) // 2 * 2
            for r in (g, g ^ 1):
                if r:
                    means[r - 1].wait_recv()
            mean = jnp.concatenate([column_of(s.mean_all[layer, first]), column_of(s.mean_all[layer, first + 1])], axis=0)
            at = slice(layer, layer + 1)
            grad_scaled = dot_t(s.sent_all[here, :], s.wout[0])
            gate, y = s.gate[here, :], s.y[here, :]
            gate_sig = sigmoid(gate)
            silu_gate = gate * gate_sig
            gated = y * silu_gate
            s.narrow[layer, taps + 1 : taps + 2, :] += jnp.sum(grad_scaled * gated, axis=0, keepdims=True)
            grad_gated = grad_scaled * a.gate_gain[at, :] + (2.0 / z.inner_all) * mean * gated
            s.rg[here, :] = (grad_gated * y * (gate_sig * (1.0 + gate * (1.0 - gate_sig)))).astype(BF)
            s.dy[here, :] = grad_gated * silu_gate

        sent = gather_rows(ex, z.rows, s.row_buf, s.sent_all, (s.gather_send.at[layer], s.gather_recv.at[layer]), visit, ahead)
        pieces = [
            Piece(
                across, own, s.piece_stage.at[k], s.piece_got.at[layer, k], s.piece_send.at[layer, k], s.piece_recv.at[layer, k]
            )
            for k, own in enumerate((s.own_out, s.own_inner.at[0], s.own_inner.at[1]))
        ]
        if older is not None:
            older[2].phase(1)
            for copy in outs:
                copy.wait()
            outs.clear()
        for i in range(across):
            s.own_out[i] = t_dot(s.scaled[...], s.sent_all[:, i * share : (i + 1) * share]).astype(BF)
        pieces[0].phase(0)
        for i in range(across):
            s.own_inner[0, i] = t_dot(s.normed[:, i * share : (i + 1) * share], s.rg[...]).astype(BF)
        pieces[1].phase(0)
        mix_backward(z, layer, s, a, a.meta, a.segrow)
        if older is not None:
            for k in range(2, len(older[2].order)):
                older[2].phase(k)
            outs.append(finish(older[2], 2, layer + 1))
        pieces[0].phase(1)
        narrow_copies[layer] = exchange(
            s.narrow.at[layer], s.narrow_got.at[layer], s.narrow_send.at[layer], s.narrow_recv.at[layer], row, across, DATA
        )
        for i in range(across):
            s.own_inner[1, i] = t_dot(s.normed[:, i * share : (i + 1) * share], s.rv[...]).astype(BF)
        pieces[2].phase(0)

        def produce(g, layer=layer):
            here = group_rows(ex, g, z.rows)
            total = dot_t(s.rg[here, :], s.win[0, 0]) + dot_t(s.rv[here, :], s.win[0, 1])
            total = total + dot_t(s.rs[here, :], s.wst[0]) + dot(s.rd[here, :], s.wstep[0])
            s.part[here, :] = total.astype(BF)

        for copy in sent + means:
            copy.wait_send()
        links = []
        total = reduce_rows(
            ex, z.rows, s.part, s.pair, s.stage, s.got,
            (s.pair_send.at[layer], s.pair_recv.at[layer], s.link_send.at[layer], s.link_recv.at[layer]), produce, links,
        )
        pieces[1].phase(1)
        resid = a.residual[...] if layer == 0 else a.resids[layer - 1]
        grad, gain_grad = norm_backward(total, resid, grad, a.norm_gain[layer : layer + 1, :])
        eighth = z.depth // 8
        for k in range(8):
            s.gain[layer, k : k + 1, :] = gain_grad[:, k * eighth : (k + 1) * eighth]
        for copy in links:
            copy.wait_send()
        if layer:
            mixed, gate = a.mixeds[layer - 1], a.gates[layer - 1]
            s.row_buf[...] = (gate * grad).astype(BF)
            tile = tile_of(-0.5 * gate * gate * jnp.sum(mixed * grad, axis=1, keepdims=True))
        for i in range(across):
            here = slice(i * share, (i + 1) * share)
            state = t_dot(s.normed[:, here], s.rs[...])
            for j in range(n):
                to = ((j * LAYERS + layer) * across + i) * padded
                s.state_part[to : to + cells, :] = state[j * cells : (j + 1) * cells, :].astype(BF)
            s.step_part[layer, i, 0:heads, :] = t_dot(s.rd[...], s.normed[:, here])
        if layer:
            loads = start_loads(layer - 1)
            for piece, k in ((pieces[0], 0), (pieces[1], 1)):
                for j in range(2, len(piece.order)):
                    piece.phase(j)
                outs.append(finish(piece, k, layer))
            older = pieces
    o.input_grad[...] = grad
    gains = exchange(s.gain, s.gain_got, s.gain_send, s.gain_recv, me, n, AXIS)
    wides = exchange(s.wide, s.wide_got, s.wide_send, s.wide_recv, me, n, AXIS)
    pieces[2].phase(1)
    links = []
    cell_rows = LAYERS * across * padded
    state = reduce_rows(
        ex, cell_rows, s.state_part, s.state_pair, s.state_stage, s.state_got,
        (s.cell_pair_send, s.cell_pair_recv, s.cell_link_send, s.cell_link_recv), lambda g: None, links,
    )
    s.gain_mid[...] = collected(s.gain[...], s.gain_got, gains)
    s.wide_mid[...] = collected(s.wide[...], s.wide_got, wides)
    gains_two = exchange(s.gain_mid, s.gain_two, s.gain_send_two, s.gain_recv_two, row, across, DATA)
    wides_two = exchange(s.wide_mid, s.wide_two, s.wide_send_two, s.wide_recv_two, row, across, DATA)
    for layer in range(LAYERS):
        for i in range(across):
            at = (layer * across + i) * padded
            s.cell_own[i, layer * padded : (layer + 1) * padded, :] = state[at : at + padded, :].astype(BF)
            s.step_own[i, layer * 16 : layer * 16 + 8, :] = s.step_part[layer, i].astype(BF)
    cell = Piece(across, s.cell_own, s.cell_stage, s.cell_got, s.cell_send, s.cell_recv)
    step = Piece(across, s.step_own, s.step_stage, s.step_got, s.step_send, s.step_recv)
    for k in range(len(cell.order)):
        cell.phase(k)
        step.phase(k)
    for layer in range(LAYERS):
        o.narrow[layer] = collected(s.narrow[layer], s.narrow_got.at[layer], narrow_copies[layer])
    o.gain[...] = collected(s.gain_mid[...], s.gain_two, gains_two)
    o.wide[...] = collected(s.wide_mid[...], s.wide_two, wides_two)
    state, steps = cell.last(), step.last()
    for layer in range(LAYERS):
        o.g_state[layer] = state[layer * padded : layer * padded + cells, :]
        o.g_step[layer] = steps[layer * 16 : layer * 16 + 8, :]
    for copy in outs:
        copy.wait()
    for k, piece in enumerate(pieces):
        for j in range(2, len(piece.order)):
            piece.phase(j)
    last = [finish(piece, k, 0) for k, piece in enumerate(pieces)]
    for copy in links + gains + wides + gains_two + wides_two + [c for copies in narrow_copies for c in copies]:
        copy.wait_send()
    for copy in last:
        copy.wait()


def padded_cells(z, n):
    cells = z.depth // (n * z.across)
    return -(-cells // 16) * 16


def piece_slots(across):
    order = [1 << b for b in range(across.bit_length() - 1)]
    return len(reduce_steps(order)), len(arrival_slots(order))


def backward_pass(ex, z, forward, residual, cotangent, meta, segrow, w):
    n, across = ex.size, z.across
    share = z.depth // across
    if share != z.inner:
        raise ValueError(share)
    saved = saved_shapes(z)
    rows = (z.rows, z.depth)
    inputs = dict(
        residual=(residual, True), cotangent=(cotangent, True), sent=(forward.sent, True), mean=(forward.mean, True),
        resids=(forward.resids, True), mixeds=(forward.mixeds, True), gates=(forward.gates, True),
        meta=(meta, True), segrow=(segrow, True), **small_inputs(w),
    )
    for k in saved:
        inputs[k] = (getattr(forward, k), False)
    cells, padded = z.depth // (n * across), padded_cells(z, n)
    narrow, wide, gain = (LAYERS, 16, z.inner), (LAYERS, 8, z.both), (LAYERS, 8, z.depth // 8)
    outputs = dict(
        input_grad=(rows, F32, True),
        g_inner=((LAYERS, 2, share, z.inner), F32, False), g_out=((LAYERS, z.inner, share), F32, False),
        g_state=((LAYERS, cells, z.both), F32, True), g_step=((LAYERS, 8, share), F32, True),
        narrow=(narrow, F32, True), wide=(wide, F32, True), gain=(gain, F32, True),
    )
    scratch = {k: pltpu.VMEM(shape, kind) for k, (shape, kind) in saved.items()}
    scratch.update(weight_scratch(z, 1))
    scratch.update(reduce_scratch(ex, z.rows, z.depth))
    slots = n // 2
    stages, arrivals = piece_slots(across)
    cell_rows = LAYERS * across * padded
    state = {"state_" + k: v for k, v in reduce_scratch(ex, cell_rows, z.both).items()}
    scratch.update(
        state_part=pltpu.VMEM((n * cell_rows, z.both), BF), **state,
        sent_all=pltpu.VMEM((z.tokens, z.depth), BF), part=pltpu.VMEM((z.tokens, z.depth), BF), row_buf=pltpu.VMEM(rows, BF),
        dy=pltpu.VMEM((z.tokens, z.inner), F32), rg=pltpu.VMEM((z.tokens, z.inner), BF), rv=pltpu.VMEM((z.tokens, z.inner), BF),
        rs=pltpu.VMEM((z.tokens, z.both), BF), rd=pltpu.VMEM((z.tokens, z.heads), BF), state=pltpu.VMEM((z.half, z.inner), F32),
        d_pre_v=pltpu.VMEM((z.tokens + 8, z.inner), F32), d_pre_s=pltpu.VMEM((z.tokens + 8, z.both), F32),
        mean_own=pltpu.VMEM((LAYERS, 8, z.rows), F32), mean_all=pltpu.VMEM((LAYERS, n, 8, z.rows), F32),
        mean_send=dma(LAYERS, n), mean_recv=dma(LAYERS, n), save_sem=dma(LAYERS, len(saved)),
        own_out=pltpu.VMEM((across, z.inner, share), BF), own_inner=pltpu.VMEM((2, across, share, z.inner), BF),
        piece_stage=pltpu.VMEM((3, stages, share, z.inner), BF), piece_got=pltpu.VMEM((LAYERS, 3, arrivals, share, z.inner), BF),
        piece_send=dma(LAYERS, 3, stages), piece_recv=dma(LAYERS, 3, arrivals),
        done=pltpu.VMEM((3, share, z.inner), F32), done_sem=dma(LAYERS, 3),
        narrow=pltpu.VMEM(narrow, F32), narrow_got=pltpu.VMEM((LAYERS, across) + narrow[1:], F32),
        narrow_send=dma(LAYERS, across), narrow_recv=dma(LAYERS, across),
        wide=pltpu.VMEM(wide, F32), wide_mid=pltpu.VMEM(wide, F32),
        wide_got=pltpu.VMEM((n,) + wide, F32), wide_two=pltpu.VMEM((across,) + wide, F32),
        gain=pltpu.VMEM(gain, F32), gain_mid=pltpu.VMEM(gain, F32),
        gain_got=pltpu.VMEM((n,) + gain, F32), gain_two=pltpu.VMEM((across,) + gain, F32),
        wide_send=dma(n), wide_recv=dma(n), gain_send=dma(n), gain_recv=dma(n),
        wide_send_two=dma(across), wide_recv_two=dma(across), gain_send_two=dma(across), gain_recv_two=dma(across),
        step_part=pltpu.VMEM((LAYERS, across, 8, share), F32), step_own=pltpu.VMEM((across, LAYERS * 16, share), BF),
        step_stage=pltpu.VMEM((stages, LAYERS * 16, share), BF), step_got=pltpu.VMEM((arrivals, LAYERS * 16, share), BF),
        step_send=dma(stages), step_recv=dma(arrivals),
        cell_own=pltpu.VMEM((across, LAYERS * padded, z.both), BF),
        cell_stage=pltpu.VMEM((stages, LAYERS * padded, z.both), BF), cell_got=pltpu.VMEM((arrivals, LAYERS * padded, z.both), BF),
        cell_send=dma(stages), cell_recv=dma(arrivals),
        cell_pair_send=dma(slots), cell_pair_recv=dma(slots), cell_link_send=dma(2 * slots), cell_link_recv=dma(2 * (slots - 1)),
        gather_send=dma(LAYERS, 2, n), gather_recv=dma(LAYERS, 2, n), pair_send=dma(LAYERS, slots), pair_recv=dma(LAYERS, slots),
        link_send=dma(LAYERS, 2 * slots), link_recv=dma(LAYERS, 2 * (slots - 1)),
    )
    return run_kernel(backward_kernel, ex, z, inputs, outputs, scratch, 1, "backward")


def sizes_of(ex, across, residual, segments, w):
    inner = w.inner_weight.shape[3]
    return Sizes(
        segments.shape[1], residual.shape[0], residual.shape[1], inner, w.step_weight.shape[2], w.state_weight.shape[2],
        w.conv_weight.shape[1], inner * ex.size, across,
    )


def shards(ex, across, residual, cotangent, segments, *weights):
    w = Weights(*weights)
    z = sizes_of(ex, across, residual, segments, w)
    w = w._replace(step_weight=jnp.transpose(w.step_weight, (0, 2, 1)))
    meta, segrow = token_meta(segments[0], SIZE)
    meta = jnp.concatenate([meta, jnp.zeros((8, 8), F32)], axis=0)
    f = forward_pass(ex, z, residual, cotangent, meta, segrow, w)
    b = backward_pass(ex, z, f, residual, cotangent, meta, segrow, w)
    taps, heads = z.taps, z.heads
    cells = z.depth // (ex.size * across)
    device = lax.axis_index(DATA) * ex.size + lax.axis_index(AXIS)
    return (
        f.block_output,
        b.input_grad,
        lax.dynamic_slice_in_dim(b.gain.reshape(LAYERS, z.depth), device * cells, cells, 1),
        b.g_inner,
        b.g_state,
        jnp.transpose(b.g_step[:, :heads], (0, 2, 1)),
        b.narrow[:, taps + 3, :heads],
        b.narrow[:, taps + 4, :heads],
        b.narrow[:, taps + 2].reshape(LAYERS, heads, -1).sum(2),
        b.narrow[:, :taps],
        b.narrow[:, taps],
        b.wide[:, :taps],
        b.wide[:, taps],
        b.narrow[:, taps + 1],
        b.g_out,
    )


def solution(mesh):
    ex = Cube(mesh.shape[AXIS])
    both, rest = (DATA, AXIS), None
    return jax.shard_map(
        functools.partial(shards, ex, mesh.shape[DATA]),
        mesh=mesh,
        in_specs=(
            P(both, rest),
            P(both, rest),
            P(DATA, rest),
            P(),
            P(rest, rest, rest, AXIS),
            P(),
            P(rest, rest, AXIS),
            P(rest, AXIS),
            P(rest, AXIS),
            P(rest, AXIS),
            P(rest, rest, AXIS),
            P(rest, AXIS),
            P(),
            P(),
            P(rest, AXIS),
            P(rest, AXIS, rest),
        ),
        out_specs=(
            P(both, rest),
            P(both, rest),
            P(rest, both),
            P(rest, rest, DATA, AXIS),
            P(rest, both, rest),
            P(rest, DATA, AXIS),
            P(rest, AXIS),
            P(rest, AXIS),
            P(rest, AXIS),
            P(rest, rest, AXIS),
            P(rest, AXIS),
            P(),
            P(),
            P(rest, AXIS),
            P(rest, AXIS, DATA),
        ),
        check_vma=False,
    )
```

time: 1170 us -> 308 us (0.26)
  waiting for transfers between devices: 484 us -> 0 us
  Pallas kernels: 0 us -> 279 us
  matrix products: 244 us -> 0 us
  other arithmetic: 186 us -> 2.34 us
  blocking collectives: 104 us -> 0 us
  local copies, waits for them, and re-layouts: 116 us -> 20.8 us
  between operations: 17.8 us -> 0.89 us
    reduce_scatter x8 -> x0, waiting for transfers between devices: 333 us -> none  [the longest x1 106 us: shards(): lax.psum_scatter(stacked[2], ('dp', 'tensor'), scatter_dimension=1, tiled...]
    pallas_call x0 -> x2, Pallas kernels: none -> 279 us  [run_kernel(): pl.pallas_call(functools.partial(kernel, ex, z, tuple(inputs), tuple(outp...]
    dot_general x60 -> x0, matrix products: 244 us -> none  [the longest x8 68 us: state_scan(): jnp.einsum('chts,cshp->cthp', decay_mat * scores[:, None], weighted, prec...]
    unnamed x18 -> x0, waiting for transfers between devices: 91.7 us -> none
    another operation x31 -> x1, other arithmetic: 87 us -> 0.08 us  [token_meta(): rows = jnp.stack(columns)]
    psum x4 -> x0, blocking collectives: 86.8 us -> none  [the longest x1 40.9 us: shards(): shared_small = lax.psum((stacked[9], stacked[10]), ('dp', 'tensor'))]
    all_gather x4 -> x0, waiting for transfers between devices: 59.3 us -> none  [the longest x2 59.3 us: forward_layer(): normed = lax.all_gather(normed_rows, 'tensor', axis=0, tiled=True)]
    unnamed x526 -> x22, local copies, waits for them, and re-layouts: 47 us -> 11.6 us
  transfers between devices with their start and end apart: 15 -> 0, of which waited for: 9 -> 0; matrix products, arithmetic and copies ran while one was open for 23% -> 0% of each run, Pallas kernels for 0% -> 0%
where the time goes in v3:
time: 308 us; the launch traced here: 303 us
  Pallas kernels  279 us (91%)
  local copies, waits for them, and re-layouts  20.8 us (7%)
    pallas_call x2, Pallas kernels, run_kernel(): pl.pallas_call(functools.partial(kernel, ex, z, tuple(inputs), tuple(outp...  279 us
    unnamed x22, local copies, waits for them, and re-layouts  11.6 us

profile of v3, /device:TPU:0, one launch (start us, length us, event | category | flops | bytes accessed | tf_op | source)
XLA Modules:
  0.0 302.7 jit_solution(11695874571940304101)
XLA Ops:
  0.6 0.7 convert_element_type.37
  1.3 0.1 fusion.4
  1.4 0.1 copy.48
  1.5 0.1 copy.50
  1.6 0.1 pad_maximum_fusion
  1.7 0.1 broadcast_in_dim.38
  1.8 0.1 broadcast_in_dim.32
  1.8 0.1 slice.58
  1.9 0.1 copy.49
  2.0 0.1 broadcast_in_dim.35
  2.1 0.8 compare_convert_fusion
  2.8 0.1 fusion.1
  2.9 0.1 compare_convert_fusion.4
  3.0 0.1 broadcast_in_dim.37
  3.0 0.1 stack.21.refs_3_.refs_8_
  3.1 0.0 copy-start.2
  3.1 0.2 copy.51
  3.3 0.8 concatenate.24.clone.refs_2_.refs_7_
  4.2 1.4 copy.56
  5.6 0.0 copy-done.2
  5.6 99.8 %forward.1 = (bf16[2,1024,1536]{2,1,0:T(8,128)(2,1)}, f32[2,1024,384]{2,1,0:T(8,128)}, f32[2,1024,384]{2,1,0:T(8,128)}, f32[2,1024,384]{2,1,0:T(8,128)}, f32[2,1...) custom-call(f32[128,1536]{1,0:T(8,128)} %refs_0_.3, ...), custom_call_target="tpu_custom_call" | custom-call | flops 34359738368 | bytes 16777216 | tf_op jit(solution)/shard_map/forward/pallas_call | solution.py:580
  105.4 178.8 %backward.1 = (f32[128,1536]{1,0:T(8,128)}, f32[2,2,384,384]{3,2,1,0:T(8,128)}, f32[2,384,384]{2,1,0:T(8,128)}, f32[2,48,256]{2,1,0:T(8,128)}, f32[2,8,384]{2,1,...) custom-call(f32[128,1536]{1,0:T(8,128)} %refs_0_.3, f32[128,1536]{1,0:T(8,128)} %refs_1_.3, ...), custom_call_target="tpu_custom_call" | custom-call | flops 34359738368 | bytes 16777216 | tf_op jit(solution)/shard_map/backward/pallas_call | solution.py:580
  284.2 0.0 copy-start
  284.2 1.0 reshape.54
  285.2 0.6 constant_dynamic-slice_fusion
  285.8 0.7 slice_bitcast_fusion
  286.5 0.6 copy.44
  287.2 1.3 fusion.3
  288.4 0.9 fusion.2
  289.3 0.1 reshape_squeeze.3
  289.4 0.7 reduce_sum.9
  290.0 1.3 slice.64
  291.4 0.6 copy.58
  292.0 1.3 slice.66
  293.3 0.7 slice.67
  294.0 0.6 copy.59
  294.6 0.6 copy.57
  295.2 2.1 copy.65
  297.2 2.1 copy.66
  299.3 0.0 copy-done
  299.3 0.0 copy-start.3
  299.3 0.0 copy-start.1
  299.3 1.4 copy.67
  300.7 0.0 copy-done.3
  300.7 0.6 copy.68
  301.4 0.1 copy-done.1
  301.5 1.0 copy.69
Async XLA Ops:
  3.1 2.4 copy-start.2
  284.2 15.1 %copy-start = (f32[2,2,384,384]{3,2,1,0:T(8,128)S(1)}, f32[2,2,384,384]{3,2,1,0:T(8,128)}, u32[]{:S(2)}) copy-start(f32[2,2,384,384]{3,2,1,0:T(8,128)} %get-tuple-element.126) | copy-start | bytes 7077892
  299.3 1.4 copy-start.3
  299.3 2.2 copy-start.1

commit v4 on v3

--- a/solution.py
+++ b/solution.py
@@ -11,6 +11,7 @@
 
 LAYERS = 2
 SIZE = 128
+CHUNKS = 2
 AXIS = "tensor"
 DATA = "dp"
 EPS = 1e-05
@@ -91,11 +92,12 @@
     return ((row >= col * width) & (row < (col + 1) * width)).astype(BF)
 
 
-def head_sum(value, inner, heads, width):
+def head_sum(value, inner, heads, width, parts=1):
     ones = head_sum_matrix(inner, heads, width)
     high = value.astype(BF)
-    low = (value - high.astype(F32)).astype(BF)
-    return dot(high, ones) + dot(low, ones)
+    if parts == 1:
+        return dot(high, ones)
+    return dot(high, ones) + dot((value - high.astype(F32)).astype(BF), ones)
 
 
 def head_split(tile, width, number):
@@ -153,31 +155,29 @@
     return ((row > col) & (seg_col == seg_row)).astype(F32)
 
 
-def token_meta(segment, size):
-    tokens = segment.shape[0]
-    seg = segment.astype(F32)
-
-    def back(k):
-        return jnp.concatenate([jnp.full((k,), -1.0, F32), seg[:-k]])
-
-    blocks = seg.reshape(-1, size)
-    gone = jnp.full((1,), -1.0, F32)
-    before = jnp.concatenate([gone, blocks[:-1, -1]])
-    after = jnp.concatenate([blocks[1:, 0], gone])
-    per = lambda v: jnp.broadcast_to(v[:, None], blocks.shape)
-    end = per(blocks[:, -1])
-    columns = [
-        seg,
-        (back(1) == seg).astype(F32),
-        (back(2) == seg).astype(F32),
-        (back(3) == seg).astype(F32),
-        (blocks == per(before)).astype(F32).reshape(-1),
-        (blocks == end).astype(F32).reshape(-1),
-        (end == per(before)).astype(F32).reshape(-1),
-        (blocks == per(after)).astype(F32).reshape(-1),
-    ]
-    rows = jnp.stack(columns)
-    return rows.T, rows
+def build_meta(count, seg_ref, column, meta, segrow):
+    row = seg_ref[...].astype(F32)
+    segrow[0:1, :] = row
+    wide = column.shape[1]
+    column[0:8, :] = jnp.full((8, wide), -1.0, F32)
+    for c in range(count):
+        part = row[:, c * SIZE : (c + 1) * SIZE]
+        column[8 + c * SIZE : 8 + (c + 1) * SIZE, :] = jnp.transpose(jnp.broadcast_to(part, (SIZE, SIZE)))
+    lane = lax.broadcasted_iota(jnp.int32, (SIZE, wide), 1)
+    for c in range(count):
+        first = 8 + c * SIZE
+        now = column[first : first + SIZE, :]
+        before = column[first - 1 : first, :]
+        end = column[first + SIZE - 1 : first + SIZE, :]
+        value = now
+        for k in range(1, 4):
+            kept = (column[first - k : first - k + SIZE, :] == now).astype(F32)
+            value = jnp.where(lane == k, kept, value)
+        value = jnp.where(lane == 4, (now == before).astype(F32), value)
+        value = jnp.where(lane == 5, (now == end).astype(F32), value)
+        value = jnp.where(lane == 6, jnp.broadcast_to((end == before).astype(F32), (SIZE, wide)), value)
+        meta[c * SIZE : (c + 1) * SIZE, :] = value[:, 0:8]
+    meta[count * SIZE :, :] = jnp.zeros((8, 8), F32)
 
 
 def span_of(dims):
@@ -199,7 +199,7 @@
         self.offsets = most_first(span_of(self.links))
 
     def gather_dims(self, q):
-        return self.orders[q] + [1]
+        return self.orders[q % 2] + [1]
 
     def gather_last(self, q, r):
         return max([i for i, d in enumerate(self.gather_dims(q)) if r & d], default=-1)
@@ -248,78 +248,83 @@
     return pltpu.SemaphoreType.DMA(shape)
 
 
-def gather_sems(ex):
-    return dma(2, ex.size), dma(2, ex.size)
-
-
-def gather_rows(ex, rows, row_buf, out, sems, visit, ahead=None):
-    me = lax.axis_index(AXIS)
-    send_sem, recv_sem = sems
-    half = rows // 2
-    copies, arrived = {}, set()
-
-    def forward(q, r):
-        dims = ex.gather_dims(q)
-        place = pl.ds(pl.multiple_of((me ^ r) * rows + q * half, half), half)
-        src = row_buf.at[pl.ds(q * half, half), :] if r == 0 else out.at[place, :]
-        for i in range(ex.gather_last(q, r) + 1, len(dims)):
-            beyond = r ^ dims[i]
-            yield beyond, remote(src, out.at[place, :], send_sem.at[q, beyond], recv_sem.at[q, beyond], me ^ dims[i])
-
-    def need(q, r):
-        if (q, r) not in arrived:
-            copies[(q, r)].wait_recv()
-            arrived.add((q, r))
-            for beyond, copy in forward(q, r):
+class Gather:
+    def __init__(self, ex, rows, row_buf, out, send_sem, recv_sem):
+        self.ex, self.rows, self.row_buf, self.out = ex, rows, row_buf, out
+        self.send_sem, self.recv_sem = send_sem, recv_sem
+        self.me = lax.axis_index(AXIS)
+        self.copies, self.arrived = {}, set()
+
+    def hops(self, q, r):
+        dims, part = self.ex.gather_dims(q), self.rows // CHUNKS
+        place = pl.ds(pl.multiple_of((self.me ^ r) * self.rows + q * part, part), part)
+        src = self.row_buf.at[pl.ds(q * part, part), :] if r == 0 else self.out.at[place, :]
+        found = []
+        for i in range(self.ex.gather_last(q, r) + 1, len(dims)):
+            b = r ^ dims[i]
+            found.append((b, remote(src, self.out.at[place, :], self.send_sem.at[q, b], self.recv_sem.at[q, b], self.me ^ dims[i])))
+        return found
+
+    def start(self, *pieces):
+        part = self.rows // CHUNKS
+        hops = [self.hops(q, 0) for q in pieces]
+        for step in zip(*hops):
+            for q, (b, copy) in zip(pieces, step):
                 copy.start()
-                copies[(q, beyond)] = copy
-
-    first = [list(forward(q, 0)) for q in range(2)]
-    for i in range(len(first[0])):
-        for q in range(2):
-            beyond, copy = first[q][i]
-            copy.start()
-            copies[(q, beyond)] = copy
-    out[rows_of(me, rows), :] = row_buf[...]
-    if ahead is not None:
-        ahead()
-    steps = [ex.gather_steps(q) for q in range(2)]
-    visits = sorted(span_of(ex.links), key=lambda g: (ex.gather_last(0, g), g & (g - 1) != 0))
-    k = 0
-    for g in visits:
-        while g and not all((q, g) in arrived for q in range(2)):
-            for q in range(2):
-                need(q, steps[q][k])
-            k += 1
-        for q in range(2):
-            need(q, g ^ 1)
-        visit(g)
-    return list(copies.values())
+                self.copies[(q, b)] = copy
+        for q in pieces:
+            here = pl.ds(pl.multiple_of(self.me * self.rows + q * part, part), part)
+            self.out[here, :] = self.row_buf[q * part : (q + 1) * part, :]
+
+    def need(self, q, r):
+        if (q, r) not in self.arrived:
+            self.copies[(q, r)].wait_recv()
+            self.arrived.add((q, r))
+            for b, copy in self.hops(q, r):
+                copy.start()
+                self.copies[(q, b)] = copy
+
+    def run(self, visit):
+        ex = self.ex
+        steps = [ex.gather_steps(q) for q in range(CHUNKS)]
+        visits = sorted(span_of(ex.links), key=lambda g: (ex.gather_last(0, g), g & (g - 1) != 0))
+        k = 0
+        for g in visits:
+            while g and not all((q, g) in self.arrived for q in range(CHUNKS)):
+                for q in range(CHUNKS):
+                    self.need(q, steps[q][k])
+                k += 1
+            for q in range(CHUNKS):
+                self.need(q, g ^ 1)
+            visit(g)
+        return list(self.copies.values())
 
 
 def reduce_scratch(ex, rows, depth):
-    slots, half = ex.size // 2, rows // 2
+    slots, part = ex.size // 2, rows // CHUNKS
     return dict(
         pair=pltpu.VMEM((slots, rows, depth), BF),
-        stage=pltpu.VMEM((2 * slots, half, depth), BF),
-        got=pltpu.VMEM((2 * (slots - 1), half, depth), BF),
-    )
-
-
-def reduce_sems(ex):
-    slots = ex.size // 2
-    return dma(slots), dma(slots), dma(2 * slots), dma(2 * (slots - 1))
-
-
-def reduce_rows(ex, rows, part, pair, stage, got, sems, produce, pending):
+        stage=pltpu.VMEM((CHUNKS * slots, part, depth), BF),
+        got=pltpu.VMEM((CHUNKS * (slots - 1), part, depth), BF),
+    )
+
+
+def reduce_rows(*args, idle=None):
+    for t, _ in enumerate(reduce_steps_of(*args)):
+        if idle is not None:
+            idle(t)
+
+
+def reduce_steps_of(ex, rows, part, pair, stage, got, sems, produce, final, pending):
     me = lax.axis_index(AXIS)
     pair_send, pair_recv, link_send, link_recv = sems
-    n, half = ex.size, rows // 2
+    n, size = ex.size, rows // CHUNKS
     slot_of = {r: i for i, r in enumerate(ex.offsets)}
-    steps = [reduce_steps(order) for order in ex.orders]
-    slots = [arrival_slots(order, q * (n // 2 - 1)) for q, order in enumerate(ex.orders)]
+    orders = [ex.orders[q % 2] for q in range(CHUNKS)]
+    steps = [reduce_steps(order) for order in orders]
+    slots = [arrival_slots(order, q * (n // 2 - 1)) for q, order in enumerate(orders)]
     waiting = list(ex.offsets)
-    pairs, ready, arrivals, final = {}, set(), {}, [None, None]
+    pairs, ready, arrivals = {}, set(), {}
 
     def advance():
         r = waiting.pop(0)
@@ -328,35 +333,42 @@
         pairs[r] = remote(part.at[rows_of(me ^ r ^ 1, rows), :], pair.at[i], pair_send.at[i], pair_recv.at[i], me ^ 1)
         pairs[r].start()
 
+    def step(q, k):
+        i, r = steps[q][k]
+        while r not in pairs:
+            advance()
+        if r not in ready:
+            pairs[r].wait_recv()
+            ready.add(r)
+        own = part[pl.ds(pl.multiple_of((me ^ r) * rows + q * size, size), size), :]
+        value = own.astype(F32) + pair[slot_of[r], pl.ds(q * size, size), :].astype(F32)
+        for j in range(i):
+            arrivals[(q, j, r)].wait_recv()
+            value = value + got[slots[q][(j, r)]].astype(F32)
+        if r == 0:
+            final(q, value)
+            return
+        d = orders[q][i]
+        s = q * (n // 2) + slot_of[r]
+        stage[s] = value.astype(BF)
+        at = slots[q][(i, r ^ d)]
+        copy = remote(stage.at[s], got.at[at], link_send.at[s], link_recv.at[at], me ^ d)
+        copy.start()
+        arrivals[(q, i, r ^ d)] = copy
+        pending.append(copy)
+
     advance()
-    for k in range(len(steps[0])):
+    waves = CHUNKS // 2
+    for t in range(len(steps[0]) + waves - 1):
         if waiting:
             advance()
-        for q in range(2):
-            i, r = steps[q][k]
-            while r not in pairs:
-                advance()
-            if r not in ready:
-                pairs[r].wait_recv()
-                ready.add(r)
-            own = part[pl.ds(pl.multiple_of((me ^ r) * rows + q * half, half), half), :]
-            value = own.astype(F32) + pair[slot_of[r], pl.ds(q * half, half), :].astype(F32)
-            for j in range(i):
-                arrivals[(q, j, r)].wait_recv()
-                value = value + got[slots[q][(j, r)]].astype(F32)
-            if r == 0:
-                final[q] = value
-                continue
-            d = ex.orders[q][i]
-            s = q * (n // 2) + slot_of[r]
-            stage[s] = value.astype(BF)
-            at = slots[q][(i, r ^ d)]
-            copy = remote(stage.at[s], got.at[at], link_send.at[s], link_recv.at[at], me ^ d)
-            copy.start()
-            arrivals[(q, i, r ^ d)] = copy
-            pending.append(copy)
-    pending.extend(pairs.values())
-    return jnp.concatenate(final, axis=0)
+        for p in range(waves):
+            if 0 <= t - p < len(steps[0]):
+                step(2 * p, t - p)
+                step(2 * p + 1, t - p)
+        if t + 1 == len(steps[0]) + waves - 1:
+            pending.extend(pairs.values())
+        yield t
 
 
 def row_scale_of(resid):
@@ -396,9 +408,20 @@
     return dict(
         win=pltpu.VMEM((layers, 2, z.depth, z.inner), BF),
         wst=pltpu.VMEM((layers, z.depth, z.both), BF),
-        wstep=pltpu.VMEM((layers, z.heads, z.depth), BF),
+        wstep=pltpu.VMEM((layers, z.heads, z.depth), F32),
         wout=pltpu.VMEM((layers, z.inner, z.depth), BF),
-        weight_sem=dma(LAYERS, 4),
+        weight_sem=dma(LAYERS, 3),
+    )
+
+
+def step_rows(z, a, s, layer, slot):
+    for h in range(z.heads):
+        s.wstep[slot, h : h + 1, :] = a.step_weight[h, layer : layer + 1, :].astype(F32)
+
+
+def meta_scratch(z):
+    return dict(
+        column=pltpu.VMEM((z.tokens + 8, SIZE), F32), meta=pltpu.VMEM((z.tokens + 8, 8), F32), segrow=pltpu.VMEM((8, z.tokens), F32)
     )
 
 
@@ -406,7 +429,7 @@
     return [
         pltpu.make_async_copy(src.at[layer], dst.at[slot], s.weight_sem.at[layer, i])
         for i, (src, dst) in enumerate(
-            ((a.inner_weight, s.win), (a.state_weight, s.wst), (a.step_weight, s.wstep), (a.out_weight, s.wout))
+            ((a.inner_weight, s.win), (a.state_weight, s.wst), (a.out_weight, s.wout))
         )
     ]
 
@@ -509,14 +532,21 @@
         copy.start()
     s.vbuf[0:8, :] = jnp.zeros((8, z.inner), F32)
     s.sbuf[0:8, :] = jnp.zeros((8, z.both), F32)
-    pending, saves = [], []
+    saves = []
+    size = z.rows // CHUNKS
+    gathers = [
+        Gather(ex, z.rows, s.row_buf, s.normed.at[layer], s.gather_send.at[layer], s.gather_recv.at[layer]) for layer in range(LAYERS)
+    ]
     hidden = a.residual[...]
+    s.hidden[...] = hidden
+    s.row_buf[...] = (hidden * row_scale_of(hidden) * a.norm_gain[0:1, :]).astype(BF)
+    gathers[0].start(*range(CHUNKS))
+    build_meta(z.count, a.segments, s.column, s.meta, s.segrow)
     for layer in range(LAYERS):
-        s.row_buf[...] = (hidden * row_scale_of(hidden) * a.norm_gain[layer : layer + 1, :]).astype(BF)
+        step_rows(z, a, s, layer, layer)
+    means = []
+    for layer in range(LAYERS):
         normed = s.normed.at[layer]
-        for copy in saves:
-            copy.wait()
-        saves = []
 
         def project(g, layer=layer, normed=normed):
             if g == 0:
@@ -528,10 +558,10 @@
             s.gate[here, :] = dot(nb, s.win[layer, 0])
             s.vbuf[beyond, :] = dot(nb, s.win[layer, 1])
             s.sbuf[beyond, :] = dot(nb, s.wst[layer])
-            s.step_in[here, :] = dot_t(nb, s.wstep[layer])
-
-        sent = gather_rows(ex, z.rows, s.row_buf, normed, (s.gather_send.at[layer], s.gather_recv.at[layer]), project)
-        mix_forward(z, layer, s, a, a.meta, a.segrow)
+            s.step_in[here, :] = dot_t(nb, s.wstep[layer].astype(BF))
+
+        sent = gathers[layer].run(project)
+        mix_forward(z, layer, s, a, s.meta, s.segrow)
         for i, name in enumerate(names_out[: len(saved_shapes(z))]):
             src = normed if i == 0 else getattr(s, name)
             saves.append(pltpu.make_async_copy(src, getattr(o, name).at[layer], s.save_sem.at[layer, i]))
@@ -549,30 +579,44 @@
                 remote(s.squares.at[me ^ r], s.square_got.at[layer, r], s.square_send.at[layer, r], s.square_recv.at[layer, r], me ^ r)
             )
             squares[-1].start()
+        gates = []
+
+        def final(q, value, layer=layer, squares=squares, gates=gates):
+            if not gates:
+                square = s.squares[me]
+                for r, copy in enumerate(squares, 1):
+                    copy.wait_recv()
+                    square = square + s.square_got[layer, r]
+                gates.append(lax.rsqrt(column_of(square) / z.inner_all + EPS))
+                if layer + 1 < LAYERS:
+                    o.gates[layer] = gates[0]
+            rows = slice(q * size, (q + 1) * size)
+            gate = gates[0][rows, :]
+            mixed = gate * value
+            hidden = s.hidden[rows, :] + mixed
+            if layer + 1 < LAYERS:
+                s.row_buf[rows, :] = (hidden * row_scale_of(hidden) * a.norm_gain[layer + 1 : layer + 2, :]).astype(BF)
+                gathers[layer + 1].start(q)
+                s.hidden[rows, :] = hidden
+                o.resids[layer, rows, :] = hidden
+                o.mixeds[layer, rows, :] = mixed
+            else:
+                grad = a.cotangent[rows, :]
+                o.block_output[rows, :] = hidden
+                o.sent[rows, :] = (gate * grad).astype(BF)
+                means.append((q, -0.5 * gate * gate * jnp.sum(mixed * grad, axis=1, keepdims=True)))
+
         links = []
-        total = reduce_rows(
+        reduce_rows(
             ex, z.rows, s.part, s.pair, s.stage, s.got,
-            (s.pair_send.at[layer], s.pair_recv.at[layer], s.link_send.at[layer], s.link_recv.at[layer]), produce, links,
+            (s.pair_send.at[layer], s.pair_recv.at[layer], s.link_send.at[layer], s.link_recv.at[layer]), produce, final, links,
         )
-        square = s.squares[me]
-        for r, copy in enumerate(squares, 1):
-            copy.wait_recv()
-            square = square + s.square_got[layer, r]
-        gate = lax.rsqrt(column_of(square) / z.inner_all + EPS)
-        mixed = gate * total
-        hidden = hidden + mixed
-        if layer + 1 < LAYERS:
-            o.resids[layer] = hidden
-            o.mixeds[layer] = mixed
-            o.gates[layer] = gate
         for copy in links + squares:
             copy.wait_send()
-    o.block_output[...] = hidden
-    grad = a.cotangent[...]
-    o.sent[...] = (gate * grad).astype(BF)
-    o.mean[...] = tile_of(-0.5 * gate * gate * jnp.sum(mixed * grad, axis=1, keepdims=True))
-    for copy in saves:
-        copy.wait()
+        for copy in saves:
+            copy.wait()
+        saves = []
+    o.mean[...] = tile_of(jnp.concatenate([v for _, v in sorted(means, key=lambda m: m[0])], axis=0))
 
 
 def run_kernel(kernel, ex, z, inputs, outputs, scratch, collective, name):
@@ -595,15 +639,15 @@
         norm_gain=(w.norm_gain, True), step_bias=(w.step_bias, True), decay_log=(w.decay_log, True),
         skip_gain=(w.skip_gain, True), conv_weight=(w.conv_weight, True), conv_bias=(w.conv_bias, True),
         state_conv_weight=(w.state_conv_weight, True), state_conv_bias=(w.state_conv_bias, True), gate_gain=(w.gate_gain, True),
-        inner_weight=(w.inner_weight, False), state_weight=(w.state_weight, False), step_weight=(w.step_weight, False),
+        inner_weight=(w.inner_weight, False), state_weight=(w.state_weight, False), step_weight=(w.step_weight, True),
         out_weight=(w.out_weight, False),
     )
 
 
-def forward_pass(ex, z, residual, cotangent, meta, segrow, w):
+def forward_pass(ex, z, residual, cotangent, segments, w):
     n = ex.size
     saved = saved_shapes(z)
-    inputs = dict(residual=(residual, True), cotangent=(cotangent, True), meta=(meta, True), segrow=(segrow, True), **small_inputs(w))
+    inputs = dict(residual=(residual, True), cotangent=(cotangent, True), segments=(segments, True), **small_inputs(w))
     rows = (z.rows, z.depth)
     outputs = {k: ((LAYERS,) + shape, kind, False) for k, (shape, kind) in saved.items()}
     outputs.update(
@@ -614,6 +658,7 @@
     scratch = {k: pltpu.VMEM(shape, kind) for k, (shape, kind) in saved.items()}
     scratch.update(normed=pltpu.VMEM((LAYERS, z.tokens, z.depth), BF))
     scratch.update(weight_scratch(z, LAYERS))
+    scratch.update(meta_scratch(z))
     scratch.update(reduce_scratch(ex, z.rows, z.depth))
     slots = n // 2
     scratch.update(
@@ -621,8 +666,9 @@
         state=pltpu.VMEM((z.half, z.inner), F32), part=pltpu.VMEM((z.tokens, z.depth), BF), row_buf=pltpu.VMEM(rows, BF),
         squares=pltpu.VMEM((n, 8, z.rows), F32), square_got=pltpu.VMEM((LAYERS, n, 8, z.rows), F32),
         square_send=dma(LAYERS, n), square_recv=dma(LAYERS, n), save_sem=dma(LAYERS, len(saved)),
-        gather_send=dma(LAYERS, 2, n), gather_recv=dma(LAYERS, 2, n), pair_send=dma(LAYERS, slots), pair_recv=dma(LAYERS, slots),
-        link_send=dma(LAYERS, 2 * slots), link_recv=dma(LAYERS, 2 * (slots - 1)),
+        gather_send=dma(LAYERS, CHUNKS, n), gather_recv=dma(LAYERS, CHUNKS, n),
+        pair_send=dma(LAYERS, slots), pair_recv=dma(LAYERS, slots), hidden=pltpu.VMEM(rows, F32),
+        link_send=dma(LAYERS, CHUNKS * slots), link_recv=dma(LAYERS, CHUNKS * (slots - 1)),
     )
     return run_kernel(forward_kernel, ex, z, inputs, outputs, scratch, 0, "forward")
 
@@ -723,25 +769,17 @@
         d_b = t_dot(d_scores, c_mat) + dot_t(ended, after_b)
         across = carry * jnp.sum(before.astype(F32) * after, axis=0, keepdims=True)
         fresh = carry * after + t_dot(c_mat, dy_in)
+        pairs = head_sum(dy_b.astype(F32) * (y - skip_all * x) - xt_f * intra, inner, heads, width, 2)
         sums = head_sum(
-            jnp.concatenate(
-                [
-                    dy_b.astype(F32) * (y - skip_all * x) - xt_f * intra,
-                    xt_f * from_later,
-                    x * d_xt,
-                    jnp.broadcast_to(across, (8, inner)),
-                ],
-                axis=0,
-            ),
-            inner, heads, width,
+            jnp.concatenate([xt_f * from_later, x * d_xt, jnp.broadcast_to(across, (8, inner))], axis=0), inner, heads, width
         )
         seg_col, seg_row = m[:, 0:1], segrow[0:1, rows]
         d_log = (
-            exact(later_ones(seg_col, seg_row), sums[0:SIZE])
-            + exact(earlier_ones(seg_col, seg_row), sums[SIZE : 2 * SIZE])
-            + sums[3 * SIZE : 3 * SIZE + 1]
+            exact(later_ones(seg_col, seg_row), pairs)
+            + exact(earlier_ones(seg_col, seg_row), sums[0:SIZE])
+            + sums[2 * SIZE : 2 * SIZE + 1]
         )
-        d_raw = (sums[2 * SIZE : 3 * SIZE] - rate * d_log) * sigmoid(raw_step)
+        d_raw = (sums[SIZE : 2 * SIZE] - rate * d_log) * sigmoid(raw_step)
         s.rd[rows, :] = d_raw.astype(BF)
         d_x = dy * skip_all + d_xt * dt_all
         s.d_pre_v[rows, :] = d_x * (sig_v * (1.0 + pre_v * (1.0 - sig_v)))
@@ -826,23 +864,28 @@
     greet([me ^ r for r in range(1, n)], [row ^ r for r in range(1, across)])
     saved = list(saved_shapes(z))
 
-    def start_loads(layer):
-        found = weight_loads(s, a, layer, 0)
-        found += [pltpu.make_async_copy(getattr(a, k).at[layer], getattr(s, k), s.save_sem.at[layer, i]) for i, k in enumerate(saved)]
+    def start_loads(layer, late):
+        found = weight_loads(s, a, layer, 0) if late else []
+        for i, k in enumerate(saved):
+            if late == (i == 0):
+                found.append(pltpu.make_async_copy(getattr(a, k).at[layer], getattr(s, k), s.save_sem.at[layer, i]))
         for copy in found:
             copy.start()
         return found
 
-    loads = start_loads(LAYERS - 1)
+    loads = start_loads(LAYERS - 1, False) + start_loads(LAYERS - 1, True)
+    size = z.rows // CHUNKS
+    s.row_buf[...] = a.sent[...]
+    s.grad[...] = a.cotangent[...]
+    gather = Gather(ex, z.rows, s.row_buf, s.sent_all, s.gather_send.at[LAYERS - 1], s.gather_recv.at[LAYERS - 1])
+    gather.start(*range(CHUNKS))
+    tile = a.mean[...]
     for ref in (s.narrow, s.wide, s.gain):
         ref[...] = jnp.zeros_like(ref)
     s.d_pre_v[z.tokens :, :] = jnp.zeros((8, z.inner), F32)
     s.d_pre_s[z.tokens :, :] = jnp.zeros((8, z.both), F32)
     if padded != cells:
         s.state_part[...] = jnp.zeros_like(s.state_part)
-    grad = a.cotangent[...]
-    s.row_buf[...] = a.sent[...]
-    tile = a.mean[...]
     narrow_copies, outs, older = [None] * LAYERS, [], None
 
     def finish(piece, k, layer):
@@ -852,17 +895,24 @@
         copy.start()
         return copy
 
+    cell_links, cell_sums = [], {}
+    cell_rows = LAYERS * across * padded
+    state_steps = reduce_steps_of(
+        ex, cell_rows, s.state_part, s.state_pair, s.state_stage, s.state_got,
+        (s.cell_pair_send, s.cell_pair_recv, s.cell_link_send, s.cell_link_recv), lambda g: None, cell_sums.__setitem__, cell_links,
+    )
     for layer in range(LAYERS - 1, -1, -1):
         s.mean_own[layer] = tile
         means = []
-
-        def ahead(layer=layer, means=means):
-            for r in range(1, n):
-                means.append(
-                    remote(s.mean_own.at[layer], s.mean_all.at[layer, me], s.mean_send.at[layer, r], s.mean_recv.at[layer, r], me ^ r)
-                )
-                means[-1].start()
-            s.mean_all[layer, me] = s.mean_own[layer]
+        for r in range(1, n):
+            means.append(
+                remote(s.mean_own.at[layer], s.mean_all.at[layer, me], s.mean_send.at[layer, r], s.mean_recv.at[layer, r], me ^ r)
+            )
+            means[-1].start()
+        s.mean_all[layer, me] = tile
+        step_rows(z, a, s, layer, 0)
+        if layer + 1 == LAYERS:
+            build_meta(z.count, a.segments, s.column, s.meta, s.segrow)
 
         def visit(g, layer=layer, means=means, loads=loads):
             if g == 0:
@@ -885,7 +935,7 @@
             s.rg[here, :] = (grad_gated * y * (gate_sig * (1.0 + gate * (1.0 - gate_sig)))).astype(BF)
             s.dy[here, :] = grad_gated * silu_gate
 
-        sent = gather_rows(ex, z.rows, s.row_buf, s.sent_all, (s.gather_send.at[layer], s.gather_recv.at[layer]), visit, ahead)
+        sent = gather.run(visit)
         pieces = [
             Piece(
                 across, own, s.piece_stage.at[k], s.piece_got.at[layer, k], s.piece_send.at[layer, k], s.piece_recv.at[layer, k]
@@ -894,16 +944,20 @@
         ]
         if older is not None:
             older[2].phase(1)
-            for copy in outs:
-                copy.wait()
-            outs.clear()
+            for k in range(2):
+                for j in range(2, len(older[k].order)):
+                    older[k].phase(j)
+                outs.append(finish(older[k], k, layer + 1))
         for i in range(across):
             s.own_out[i] = t_dot(s.scaled[...], s.sent_all[:, i * share : (i + 1) * share]).astype(BF)
         pieces[0].phase(0)
         for i in range(across):
             s.own_inner[0, i] = t_dot(s.normed[:, i * share : (i + 1) * share], s.rg[...]).astype(BF)
         pieces[1].phase(0)
-        mix_backward(z, layer, s, a, a.meta, a.segrow)
+        mix_backward(z, layer, s, a, s.meta, s.segrow)
+        for copy in sent + means:
+            copy.wait_send()
+        loads = start_loads(layer - 1, False) if layer else []
         if older is not None:
             for k in range(2, len(older[2].order)):
                 older[2].phase(k)
@@ -912,59 +966,83 @@
         narrow_copies[layer] = exchange(
             s.narrow.at[layer], s.narrow_got.at[layer], s.narrow_send.at[layer], s.narrow_recv.at[layer], row, across, DATA
         )
-        for i in range(across):
-            s.own_inner[1, i] = t_dot(s.normed[:, i * share : (i + 1) * share], s.rv[...]).astype(BF)
-        pieces[2].phase(0)
+
+        def value_grads(pieces=pieces):
+            for i in range(across):
+                s.own_inner[1, i] = t_dot(s.normed[:, i * share : (i + 1) * share], s.rv[...]).astype(BF)
+            pieces[2].phase(0)
+
+        def state_grads(layer=layer):
+            for i in range(across):
+                here = slice(i * share, (i + 1) * share)
+                state = t_dot(s.normed[:, here], s.rs[...])
+                for j in range(n):
+                    to = ((j * LAYERS + layer) * across + i) * padded
+                    s.state_part[to : to + cells, :] = state[j * cells : (j + 1) * cells, :].astype(BF)
+                s.step_part[layer, i, 0:heads, :] = t_dot(s.rd[...], s.normed[:, here])
+
+        if layer == 0:
+            value_grads()
+
+        def idle(t, layer=layer, pieces=pieces, value_grads=value_grads, state_grads=state_grads):
+            if t == 1:
+                if layer:
+                    value_grads()
+                else:
+                    state_grads()
+            elif t == 2 and layer:
+                state_grads()
+            elif t == 3:
+                pieces[1].phase(1)
+            if t >= 2 and not layer:
+                next(state_steps)
 
         def produce(g, layer=layer):
             here = group_rows(ex, g, z.rows)
             total = dot_t(s.rg[here, :], s.win[0, 0]) + dot_t(s.rv[here, :], s.win[0, 1])
-            total = total + dot_t(s.rs[here, :], s.wst[0]) + dot(s.rd[here, :], s.wstep[0])
+            total = total + dot_t(s.rs[here, :], s.wst[0]) + dot(s.rd[here, :], s.wstep[0].astype(BF))
             s.part[here, :] = total.astype(BF)
 
-        for copy in sent + means:
-            copy.wait_send()
+        after = Gather(ex, z.rows, s.row_buf, s.sent_all, s.gather_send.at[layer - 1], s.gather_recv.at[layer - 1]) if layer else None
+        found = []
+
+        def final(q, value, layer=layer, after=after, found=found):
+            rows = slice(q * size, (q + 1) * size)
+            resid = a.resids[layer - 1, rows, :] if layer else a.residual[rows, :]
+            fresh, gain_grad = norm_backward(value, resid, s.grad[rows, :], a.norm_gain[layer : layer + 1, :])
+            mean = None
+            if layer:
+                mixed, gate = a.mixeds[layer - 1, rows, :], a.gates[layer - 1, rows, :]
+                s.row_buf[rows, :] = (gate * fresh).astype(BF)
+                after.start(q)
+                s.grad[rows, :] = fresh
+                mean = -0.5 * gate * gate * jnp.sum(mixed * fresh, axis=1, keepdims=True)
+            else:
+                o.input_grad[rows, :] = fresh
+            found.append((q, gain_grad, mean))
+
         links = []
-        total = reduce_rows(
+        reduce_rows(
             ex, z.rows, s.part, s.pair, s.stage, s.got,
-            (s.pair_send.at[layer], s.pair_recv.at[layer], s.link_send.at[layer], s.link_recv.at[layer]), produce, links,
+            (s.pair_send.at[layer], s.pair_recv.at[layer], s.link_send.at[layer], s.link_recv.at[layer]), produce, final, links, idle=idle,
         )
-        pieces[1].phase(1)
-        resid = a.residual[...] if layer == 0 else a.resids[layer - 1]
-        grad, gain_grad = norm_backward(total, resid, grad, a.norm_gain[layer : layer + 1, :])
+        found.sort(key=lambda item: item[0])
+        gain_grad = sum(item[1] for item in found)
         eighth = z.depth // 8
         for k in range(8):
             s.gain[layer, k : k + 1, :] = gain_grad[:, k * eighth : (k + 1) * eighth]
         for copy in links:
             copy.wait_send()
         if layer:
-            mixed, gate = a.mixeds[layer - 1], a.gates[layer - 1]
-            s.row_buf[...] = (gate * grad).astype(BF)
-            tile = tile_of(-0.5 * gate * gate * jnp.sum(mixed * grad, axis=1, keepdims=True))
-        for i in range(across):
-            here = slice(i * share, (i + 1) * share)
-            state = t_dot(s.normed[:, here], s.rs[...])
-            for j in range(n):
-                to = ((j * LAYERS + layer) * across + i) * padded
-                s.state_part[to : to + cells, :] = state[j * cells : (j + 1) * cells, :].astype(BF)
-            s.step_part[layer, i, 0:heads, :] = t_dot(s.rd[...], s.normed[:, here])
-        if layer:
-            loads = start_loads(layer - 1)
-            for piece, k in ((pieces[0], 0), (pieces[1], 1)):
-                for j in range(2, len(piece.order)):
-                    piece.phase(j)
-                outs.append(finish(piece, k, layer))
+            tile = tile_of(jnp.concatenate([item[2] for item in found], axis=0))
+            loads = loads + start_loads(layer - 1, True)
+            gather = after
             older = pieces
-    o.input_grad[...] = grad
     gains = exchange(s.gain, s.gain_got, s.gain_send, s.gain_recv, me, n, AXIS)
     wides = exchange(s.wide, s.wide_got, s.wide_send, s.wide_recv, me, n, AXIS)
-    pieces[2].phase(1)
-    links = []
-    cell_rows = LAYERS * across * padded
-    state = reduce_rows(
-        ex, cell_rows, s.state_part, s.state_pair, s.state_stage, s.state_got,
-        (s.cell_pair_send, s.cell_pair_recv, s.cell_link_send, s.cell_link_recv), lambda g: None, links,
-    )
+    for _ in state_steps:
+        pass
+    state = jnp.concatenate([cell_sums[q] for q in range(CHUNKS)], axis=0)
     s.gain_mid[...] = collected(s.gain[...], s.gain_got, gains)
     s.wide_mid[...] = collected(s.wide[...], s.wide_got, wides)
     gains_two = exchange(s.gain_mid, s.gain_two, s.gain_send_two, s.gain_recv_two, row, across, DATA)
@@ -974,6 +1052,7 @@
             at = (layer * across + i) * padded
             s.cell_own[i, layer * padded : (layer + 1) * padded, :] = state[at : at + padded, :].astype(BF)
             s.step_own[i, layer * 16 : layer * 16 + 8, :] = s.step_part[layer, i].astype(BF)
+    pieces[2].phase(1)
     cell = Piece(across, s.cell_own, s.cell_stage, s.cell_got, s.cell_send, s.cell_recv)
     step = Piece(across, s.step_own, s.step_stage, s.step_got, s.step_send, s.step_recv)
     for k in range(len(cell.order)):
@@ -993,7 +1072,7 @@
         for j in range(2, len(piece.order)):
             piece.phase(j)
     last = [finish(piece, k, 0) for k, piece in enumerate(pieces)]
-    for copy in links + gains + wides + gains_two + wides_two + [c for copies in narrow_copies for c in copies]:
+    for copy in cell_links + gains + wides + gains_two + wides_two + [c for copies in narrow_copies for c in copies]:
         copy.wait_send()
     for copy in last:
         copy.wait()
@@ -1009,7 +1088,7 @@
     return len(reduce_steps(order)), len(arrival_slots(order))
 
 
-def backward_pass(ex, z, forward, residual, cotangent, meta, segrow, w):
+def backward_pass(ex, z, forward, residual, cotangent, segments, w):
     n, across = ex.size, z.across
     share = z.depth // across
     if share != z.inner:
@@ -1019,7 +1098,7 @@
     inputs = dict(
         residual=(residual, True), cotangent=(cotangent, True), sent=(forward.sent, True), mean=(forward.mean, True),
         resids=(forward.resids, True), mixeds=(forward.mixeds, True), gates=(forward.gates, True),
-        meta=(meta, True), segrow=(segrow, True), **small_inputs(w),
+        segments=(segments, True), **small_inputs(w),
     )
     for k in saved:
         inputs[k] = (getattr(forward, k), False)
@@ -1033,6 +1112,7 @@
     )
     scratch = {k: pltpu.VMEM(shape, kind) for k, (shape, kind) in saved.items()}
     scratch.update(weight_scratch(z, 1))
+    scratch.update(meta_scratch(z))
     scratch.update(reduce_scratch(ex, z.rows, z.depth))
     slots = n // 2
     stages, arrivals = piece_slots(across)
@@ -1064,11 +1144,76 @@
         cell_own=pltpu.VMEM((across, LAYERS * padded, z.both), BF),
         cell_stage=pltpu.VMEM((stages, LAYERS * padded, z.both), BF), cell_got=pltpu.VMEM((arrivals, LAYERS * padded, z.both), BF),
         cell_send=dma(stages), cell_recv=dma(arrivals),
-        cell_pair_send=dma(slots), cell_pair_recv=dma(slots), cell_link_send=dma(2 * slots), cell_link_recv=dma(2 * (slots - 1)),
-        gather_send=dma(LAYERS, 2, n), gather_recv=dma(LAYERS, 2, n), pair_send=dma(LAYERS, slots), pair_recv=dma(LAYERS, slots),
-        link_send=dma(LAYERS, 2 * slots), link_recv=dma(LAYERS, 2 * (slots - 1)),
+        cell_pair_send=dma(slots), cell_pair_recv=dma(slots), cell_link_send=dma(CHUNKS * slots),
+        cell_link_recv=dma(CHUNKS * (slots - 1)), grad=pltpu.VMEM(rows, F32),
+        gather_send=dma(LAYERS, CHUNKS, n), gather_recv=dma(LAYERS, CHUNKS, n),
+        pair_send=dma(LAYERS, slots), pair_recv=dma(LAYERS, slots),
+        link_send=dma(LAYERS, CHUNKS * slots), link_recv=dma(LAYERS, CHUNKS * (slots - 1)),
     )
     return run_kernel(backward_kernel, ex, z, inputs, outputs, scratch, 1, "backward")
+
+
+def final_kernel(z, n, *refs):
+    block, grad, inner, out, state, step, narrow, wide, gain = refs[:9]
+    (o_block, o_grad, o_norm, o_inner, o_state, o_step, o_bias, o_decay, o_skip, o_conv, o_cbias, o_sconv, o_sbias, o_gate, o_out) = refs[9:]
+    o_block[...] = block[...]
+    o_grad[...] = grad[...]
+    o_inner[...] = inner[...]
+    o_out[...] = out[...]
+
+    @pl.when(pl.program_id(0) == 0)
+    def _():
+        taps, heads = z.taps, z.heads
+        o_state[...] = state[...]
+        cells, eighth = o_norm.shape[1], gain.shape[2]
+        per = eighth // cells
+        device = lax.axis_index(DATA) * n + lax.axis_index(AXIS)
+        pick = lax.broadcasted_iota(jnp.int32, (eighth, cells), 0)
+        pick = (pick == lax.broadcasted_iota(jnp.int32, (eighth, cells), 1) + (device % per) * cells).astype(F32)
+        line = lax.broadcasted_iota(jnp.int32, (8, eighth), 0) == device // per
+        ones = head_sum_matrix(z.inner, heads, z.width).astype(F32)
+        for layer in range(LAYERS):
+            at = slice(layer, layer + 1)
+            row = jnp.sum(jnp.where(line, gain[layer], 0.0), axis=0, keepdims=True)
+            o_norm[at, :] = exact(jnp.broadcast_to(row, (8, eighth)), pick)[0:1, :]
+            lines = narrow[layer]
+            for h in range(heads):
+                o_step[h, at, :] = step[layer, h : h + 1, :]
+            skip = jnp.broadcast_to(lines[taps + 2 : taps + 3, :], (8, z.inner))
+            o_skip[at, :] = exact(skip, ones)[0:1, :]
+            o_bias[at, :] = lines[taps + 3 : taps + 4, 0:heads]
+            o_decay[at, :] = lines[taps + 4 : taps + 5, 0:heads]
+            o_conv[layer] = lines[0:taps, :]
+            o_cbias[at, :] = lines[taps : taps + 1, :]
+            o_gate[at, :] = lines[taps + 1 : taps + 2, :]
+            o_sconv[layer] = wide[layer, 0:taps, :]
+            o_sbias[at, :] = wide[layer, taps : taps + 1, :]
+
+
+def final_pass(ex, z, block_output, b):
+    share, both, heads, taps, inner = z.depth // z.across, z.both, z.heads, z.taps, z.inner
+    cells = z.depth // (ex.size * z.across)
+    steps = 4 if z.rows % 32 == 0 and share % 32 == 0 and inner % 32 == 0 else 1
+    whole = lambda shape: pl.BlockSpec(shape, lambda i: (0,) * len(shape))
+    rows = pl.BlockSpec((z.rows // steps, z.depth), lambda i: (i, 0))
+    inner_spec = pl.BlockSpec((LAYERS, 2, share // steps, inner), lambda i: (0, 0, i, 0))
+    out_spec = pl.BlockSpec((LAYERS, inner // steps, share), lambda i: (0, i, 0))
+    arrays = (block_output, b.input_grad, b.g_inner, b.g_out, b.g_state, b.g_step, b.narrow, b.wide, b.gain)
+    small = [
+        (LAYERS, cells, both), (heads, LAYERS, share), (LAYERS, heads), (LAYERS, heads), (LAYERS, heads), (LAYERS, taps, inner),
+        (LAYERS, inner), (LAYERS, taps, both), (LAYERS, both), (LAYERS, inner),
+    ]
+    shapes = [(z.rows, z.depth), (z.rows, z.depth), (LAYERS, cells), b.g_inner.shape] + small + [b.g_out.shape]
+    return pl.pallas_call(
+        functools.partial(final_kernel, z, ex.size),
+        grid=(steps,),
+        out_shape=tuple(jax.ShapeDtypeStruct(shape, F32) for shape in shapes),
+        in_specs=[rows, rows, inner_spec, out_spec] + [whole(v.shape) for v in arrays[4:]],
+        out_specs=tuple([rows, rows, whole((LAYERS, cells)), inner_spec] + [whole(shape) for shape in small] + [out_spec]),
+        compiler_params=pltpu.CompilerParams(vmem_limit_bytes=VM),
+        cost_estimate=cost_of(1 << 20),
+        name="final",
+    )(*arrays)
 
 
 def sizes_of(ex, across, residual, segments, w):
@@ -1082,31 +1227,12 @@
 def shards(ex, across, residual, cotangent, segments, *weights):
     w = Weights(*weights)
     z = sizes_of(ex, across, residual, segments, w)
-    w = w._replace(step_weight=jnp.transpose(w.step_weight, (0, 2, 1)))
-    meta, segrow = token_meta(segments[0], SIZE)
-    meta = jnp.concatenate([meta, jnp.zeros((8, 8), F32)], axis=0)
-    f = forward_pass(ex, z, residual, cotangent, meta, segrow, w)
-    b = backward_pass(ex, z, f, residual, cotangent, meta, segrow, w)
-    taps, heads = z.taps, z.heads
-    cells = z.depth // (ex.size * across)
-    device = lax.axis_index(DATA) * ex.size + lax.axis_index(AXIS)
-    return (
-        f.block_output,
-        b.input_grad,
-        lax.dynamic_slice_in_dim(b.gain.reshape(LAYERS, z.depth), device * cells, cells, 1),
-        b.g_inner,
-        b.g_state,
-        jnp.transpose(b.g_step[:, :heads], (0, 2, 1)),
-        b.narrow[:, taps + 3, :heads],
-        b.narrow[:, taps + 4, :heads],
-        b.narrow[:, taps + 2].reshape(LAYERS, heads, -1).sum(2),
-        b.narrow[:, :taps],
-        b.narrow[:, taps],
-        b.wide[:, :taps],
-        b.wide[:, taps],
-        b.narrow[:, taps + 1],
-        b.g_out,
-    )
+    w = w._replace(step_weight=jnp.transpose(w.step_weight, (2, 0, 1)))
+    f = forward_pass(ex, z, residual, cotangent, segments, w)
+    b = backward_pass(ex, z, f, residual, cotangent, segments, w)
+    made = list(final_pass(ex, z, f.block_output, b))
+    made[5] = jnp.transpose(made[5], (1, 2, 0))
+    return tuple(made)
 
 
 def solution(mesh):

time: 308 us -> 274 us (0.89)
  local copies, waits for them, and re-layouts: 20.8 us -> 0 us
  Pallas kernels: 279 us -> 268 us
    pallas_call x2, Pallas kernels: 279 us -> 262 us  [run_kernel(): pl.pallas_call(functools.partial(kernel, ex, z, tuple(inputs), tuple(outp...]
    unnamed x22 -> x0, local copies, waits for them, and re-layouts: 11.6 us -> none
    pallas_call x0 -> x1, Pallas kernels: none -> 5.94 us  [final_pass(): pl.pallas_call(functools.partial(final_kernel, z, ex.size), grid=(steps,)...]
    slice x7 -> x0, local copies, waits for them, and re-layouts: 5.67 us -> none  [the longest x1 1.34 us: shards(): b.narrow[:, :taps]]
where the time goes in v4:
time: 274 us; the launch traced here: 269 us
  Pallas kernels  268 us (98%)
    pallas_call x2, Pallas kernels, run_kernel(): pl.pallas_call(functools.partial(kernel, ex, z, tuple(inputs), tuple(outp...  262 us
    pallas_call x1, Pallas kernels, final_pass(): pl.pallas_call(functools.partial(final_kernel, z, ex.size), grid=(steps,)...  5.94 us

profile of v4, /device:TPU:0, one launch (start us, length us, event | category | flops | bytes accessed | tf_op | source)
XLA Modules:
  0.0 269.0 jit_solution(3908248241351249503)
XLA Ops:
  0.6 100.3 %forward.1 = (bf16[2,1024,1536]{2,1,0:T(8,128)(2,1)}, f32[2,1024,384]{2,1,0:T(8,128)}, f32[2,1024,384]{2,1,0:T(8,128)}, f32[2,1024,384]{2,1,0:T(8,128)}, f32[2,1...) custom-call(f32[128,1536]{1,0:T(8,128)} %refs_0_.3, ...), custom_call_target="tpu_custom_call" | custom-call | flops 34359738368 | bytes 16777216 | tf_op jit(solution)/shard_map/forward/pallas_call | solution.py:624
  100.9 161.9 %backward.1 = (f32[128,1536]{1,0:T(8,128)}, f32[2,2,384,384]{3,2,1,0:T(8,128)}, f32[2,384,384]{2,1,0:T(8,128)}, f32[2,48,256]{2,1,0:T(8,128)}, f32[2,8,384]{2,1,...) custom-call(f32[128,1536]{1,0:T(8,128)} %refs_0_.3, f32[128,1536]{1,0:T(8,128)} %refs_1_.3, ...), custom_call_target="tpu_custom_call" | custom-call | flops 34359738368 | bytes 16777216 | tf_op jit(solution)/shard_map/backward/pallas_call | solution.py:624
  262.9 5.9 %final.1 = (f32[128,1536]{1,0:T(8,128)}, f32[128,1536]{1,0:T(8,128)}, f32[2,48]{1,0:T(2,128)}, f32[2,2,384,384]{3,2,1,0:T(8,128)}, f32[2,48,256]{2,1,0:T(8,128)}...) custom-call(f32[128,1536]{1,0:T(8,128)} %get-tuple-element.54.refs_0, ...), custom_call_target="tpu_custom_call" | custom-call | flops 1048576 | bytes 16777216 | tf_op jit(solution)/shard_map/final/pallas_call | solution.py:1207

commit v5 on v4

--- a/solution.py
+++ b/solution.py
@@ -309,13 +309,13 @@
     )
 
 
-def reduce_rows(*args, idle=None):
-    for t, _ in enumerate(reduce_steps_of(*args)):
+def reduce_rows(*args, idle=None, ahead=True):
+    for t, _ in enumerate(reduce_steps_of(*args, ahead=ahead)):
         if idle is not None:
             idle(t)
 
 
-def reduce_steps_of(ex, rows, part, pair, stage, got, sems, produce, final, pending):
+def reduce_steps_of(ex, rows, part, pair, stage, got, sems, produce, final, pending, ahead=True):
     me = lax.axis_index(AXIS)
     pair_send, pair_recv, link_send, link_recv = sems
     n, size = ex.size, rows // CHUNKS
@@ -328,10 +328,11 @@
 
     def advance():
         r = waiting.pop(0)
-        produce(r)
+        produce(r, False)
         i = slot_of[r]
         pairs[r] = remote(part.at[rows_of(me ^ r ^ 1, rows), :], pair.at[i], pair_send.at[i], pair_recv.at[i], me ^ 1)
         pairs[r].start()
+        produce(r, True)
 
     def step(q, k):
         i, r = steps[q][k]
@@ -360,12 +361,14 @@
     advance()
     waves = CHUNKS // 2
     for t in range(len(steps[0]) + waves - 1):
-        if waiting:
+        if waiting and ahead:
             advance()
         for p in range(waves):
             if 0 <= t - p < len(steps[0]):
                 step(2 * p, t - p)
                 step(2 * p + 1, t - p)
+        if waiting and not ahead:
+            advance()
         if t + 1 == len(steps[0]) + waves - 1:
             pending.extend(pairs.values())
         yield t
@@ -443,13 +446,12 @@
     )
 
 
-def mix_forward(z, layer, s, a, meta, segrow):
+def mix_states(z, layer, s, a, meta):
     at = slice(layer, layer + 1)
     inner, width, half = z.inner, z.width, z.half
     s.state[...] = jnp.zeros_like(s.state)
-    group = 2 if z.count % 2 == 0 else 1
-
-    def chunk(c, before):
+
+    def chunk(c, carry):
         rows = pl.ds(pl.multiple_of(c * SIZE, SIZE), SIZE)
         window = pl.ds(pl.multiple_of(c * SIZE, SIZE), SIZE + 8)
         m = meta[rows, :]
@@ -468,55 +470,57 @@
         s.pre_v[rows, :] = pre_v
         s.pre_s[rows, :] = pre_s
         x = pre_v * sigmoid(pre_v)
-        st = pre_s * sigmoid(pre_s)
-        b_mat = st[:, :half].astype(BF)
-        c_mat = st[:, half:].astype(BF)
+        st = (pre_s * sigmoid(pre_s)).astype(BF)
         dt = softplus(s.step_in[rows, :] + a.step_bias[at, :])
-        log_decay = -dt * jnp.exp(a.decay_log[at, :])
-        cum = exact(lower_ones(SIZE), log_decay)
-        cum_t = turned(cum)
+        cum = exact(lower_ones(SIZE), -dt * jnp.exp(a.decay_log[at, :]))
         last = cum[SIZE - 1 : SIZE, :]
         xt = (x * expand(dt, inner, width)).astype(BF)
-        from_state = jnp.exp(cum) * m[:, 4:5]
+        s.x[rows, :] = x
+        s.xt[rows, :] = xt
+        s.states[rows, :] = st
+        s.cum[rows, :] = cum
+        before = s.state[...]
+        s.entering[c] = before.astype(BF)
         to_end = jnp.exp(last - cum) * m[:, 5:6]
-        carry = jnp.exp(last) * m[0:1, 6:7]
-        before_b = before.astype(BF)
-        s.entering[c] = before_b
-        scores = dot_t(c_mat, b_mat)
-        mask = pair_mask(m[:, 0:1], segrow[0:1, rows])
-        parts = []
-        for start, wide, first, number in tiles_of(inner, width):
-            mats = []
-            for h in range(first, first + number):
-                differ = cum[:, h : h + 1] - cum_t[h : h + 1, :]
-                mats.append((jnp.exp(jnp.where(mask, differ, -1e30)) * scores).astype(BF))
-            left = mats[0] if number == 1 else jnp.concatenate(mats, axis=1)
-            parts.append(dot(left, head_split(xt[:, start : start + wide], width, number)))
-        intra = parts[0] if len(parts) == 1 else jnp.concatenate(parts, axis=1)
-        inter = dot(c_mat, before_b) * expand(from_state, inner, width)
-        y = intra + inter + expand(a.skip_gain[at, :], inner, width) * x
-        s.y[rows, :] = y
         ended = (xt.astype(F32) * expand(to_end, inner, width)).astype(BF)
-        after = expand(carry, inner, width) * before + t_dot(b_mat, ended)
-        gate = s.gate[rows, :]
-        gated = y * (gate * sigmoid(gate))
-        square = jnp.sum(gated * gated, axis=1, keepdims=True)
-        tile = tile_of(square)
-        per = SIZE // z.rows if SIZE > z.rows else 1
-        wide = SIZE // per
-        for k in range(per):
-            s.squares[c * per + k] = tile[:, k * wide : (k + 1) * wide]
-        s.scaled[rows, :] = (gated * a.gate_gain[at, :]).astype(BF)
-        return after
-
-    def body(i, carry):
-        before = s.state[...]
-        for k in range(group):
-            before = chunk(i * group + k, before)
-        s.state[...] = before
+        s.state[...] = expand(jnp.exp(last) * m[0:1, 6:7], inner, width) * before + t_dot(st[:, :half], ended)
         return carry
 
-    lax.fori_loop(0, z.count // group, body, 0)
+    lax.fori_loop(0, z.count, chunk, 0)
+
+
+def mix_outputs(z, layer, s, a, meta, segrow, c):
+    at = slice(layer, layer + 1)
+    inner, width, half = z.inner, z.width, z.half
+    rows = pl.ds(pl.multiple_of(c * SIZE, SIZE), SIZE)
+    m = meta[rows, :]
+    st, cum, xt = s.states[rows, :], s.cum[rows, :], s.xt[rows, :]
+    b_mat, c_mat = st[:, :half], st[:, half:]
+    cum_t = turned(cum)
+    from_state = jnp.exp(cum) * m[:, 4:5]
+    scores = dot_t(c_mat, b_mat)
+    mask = pair_mask(m[:, 0:1], segrow[0:1, rows])
+    parts = []
+    for start, wide, first, number in tiles_of(inner, width):
+        mats = []
+        for h in range(first, first + number):
+            differ = cum[:, h : h + 1] - cum_t[h : h + 1, :]
+            mats.append((jnp.exp(jnp.where(mask, differ, -1e30)) * scores).astype(BF))
+        left = mats[0] if number == 1 else jnp.concatenate(mats, axis=1)
+        parts.append(dot(left, head_split(xt[:, start : start + wide], width, number)))
+    intra = parts[0] if len(parts) == 1 else jnp.concatenate(parts, axis=1)
+    inter = dot(c_mat, s.entering[c]) * expand(from_state, inner, width)
+    y = intra + inter + expand(a.skip_gain[at, :], inner, width) * s.x[rows, :]
+    s.y[rows, :] = y
+    gate = s.gate[rows, :]
+    gated = y * (gate * sigmoid(gate))
+    square = jnp.sum(gated * gated, axis=1, keepdims=True)
+    tile = tile_of(square)
+    per = SIZE // z.rows if SIZE > z.rows else 1
+    wide = SIZE // per
+    for k in range(per):
+        s.squares[c * per + k] = tile[:, k * wide : (k + 1) * wide]
+    s.scaled[rows, :] = (gated * a.gate_gain[at, :]).astype(BF)
 
 
 def forward_kernel(ex, z, names_in, names_out, names_scratch, *refs):
@@ -561,30 +565,47 @@
             s.step_in[here, :] = dot_t(nb, s.wstep[layer].astype(BF))
 
         sent = gathers[layer].run(project)
-        mix_forward(z, layer, s, a, s.meta, s.segrow)
-        for i, name in enumerate(names_out[: len(saved_shapes(z))]):
-            src = normed if i == 0 else getattr(s, name)
-            saves.append(pltpu.make_async_copy(src, getattr(o, name).at[layer], s.save_sem.at[layer, i]))
-            saves[-1].start()
+        mix_states(z, layer, s, a, s.meta)
+
+        def save(late, layer=layer, normed=normed):
+            for i, name in enumerate(names_out[: len(saved_shapes(z))]):
+                src = normed if i == 0 else getattr(s, name)
+                if late == (src is s.y or src is s.scaled):
+                    saves.append(pltpu.make_async_copy(src, getattr(o, name).at[layer], s.save_sem.at[layer, i]))
+                    saves[-1].start()
+
+        save(False)
         for copy in sent:
             copy.wait_send()
-
-        def produce(g, layer=layer):
-            here = group_rows(ex, g, z.rows)
-            s.part[here, :] = dot(s.scaled[here, :], s.wout[layer]).astype(BF)
-
-        squares = []
-        for r in range(1, n):
-            squares.append(
-                remote(s.squares.at[me ^ r], s.square_got.at[layer, r], s.square_send.at[layer, r], s.square_recv.at[layer, r], me ^ r)
-            )
-            squares[-1].start()
+        squares = {}
+
+        def produce(g, own, layer=layer, squares=squares):
+            if 2 * z.rows > SIZE:
+                block = me ^ g if own else me ^ g ^ 1
+                here, first, many = rows_of(block, z.rows), block * (z.rows // SIZE), z.rows // SIZE
+            elif not own:
+                here, first, many = group_rows(ex, g, z.rows), (me ^ g) // 2, 1
+            if own <= (2 * z.rows > SIZE):
+                for i in range(many):
+                    mix_outputs(z, layer, s, a, s.meta, s.segrow, first + i)
+                s.part[here, :] = dot(s.scaled[here, :], s.wout[layer]).astype(BF)
+            for r in (g, g ^ 1) if own else ():
+                if r:
+                    squares[r] = remote(
+                        s.squares.at[me ^ r], s.square_got.at[layer, r], s.square_send.at[layer, r], s.square_recv.at[layer, r], me ^ r
+                    )
+                    squares[r].start()
+
+        def idle(t, save=save):
+            if t == 2:
+                save(True)
+
         gates = []
 
         def final(q, value, layer=layer, squares=squares, gates=gates):
             if not gates:
                 square = s.squares[me]
-                for r, copy in enumerate(squares, 1):
+                for r, copy in squares.items():
                     copy.wait_recv()
                     square = square + s.square_got[layer, r]
                 gates.append(lax.rsqrt(column_of(square) / z.inner_all + EPS))
@@ -609,9 +630,9 @@
         links = []
         reduce_rows(
             ex, z.rows, s.part, s.pair, s.stage, s.got,
-            (s.pair_send.at[layer], s.pair_recv.at[layer], s.link_send.at[layer], s.link_recv.at[layer]), produce, final, links,
+            (s.pair_send.at[layer], s.pair_recv.at[layer], s.link_send.at[layer], s.link_recv.at[layer]), produce, final, links, idle=idle, ahead=False,
         )
-        for copy in links + squares:
+        for copy in links + list(squares.values()):
             copy.wait_send()
         for copy in saves:
             copy.wait()
@@ -663,7 +684,8 @@
     slots = n // 2
     scratch.update(
         vbuf=pltpu.VMEM((z.tokens + 8, z.inner), F32), sbuf=pltpu.VMEM((z.tokens + 8, z.both), F32),
-        state=pltpu.VMEM((z.half, z.inner), F32), part=pltpu.VMEM((z.tokens, z.depth), BF), row_buf=pltpu.VMEM(rows, BF),
+        x=pltpu.VMEM((z.tokens, z.inner), F32), xt=pltpu.VMEM((z.tokens, z.inner), BF), states=pltpu.VMEM((z.tokens, z.both), BF),
+        cum=pltpu.VMEM((z.tokens, z.heads), F32), state=pltpu.VMEM((z.half, z.inner), F32), part=pltpu.VMEM((z.tokens, z.depth), BF), row_buf=pltpu.VMEM(rows, BF),
         squares=pltpu.VMEM((n, 8, z.rows), F32), square_got=pltpu.VMEM((LAYERS, n, 8, z.rows), F32),
         square_send=dma(LAYERS, n), square_recv=dma(LAYERS, n), save_sem=dma(LAYERS, len(saved)),
         gather_send=dma(LAYERS, CHUNKS, n), gather_recv=dma(LAYERS, CHUNKS, n),
@@ -899,7 +921,7 @@
     cell_rows = LAYERS * across * padded
     state_steps = reduce_steps_of(
         ex, cell_rows, s.state_part, s.state_pair, s.state_stage, s.state_got,
-        (s.cell_pair_send, s.cell_pair_recv, s.cell_link_send, s.cell_link_recv), lambda g: None, cell_sums.__setitem__, cell_links,
+        (s.cell_pair_send, s.cell_pair_recv, s.cell_link_send, s.cell_link_recv), lambda g, own: None, cell_sums.__setitem__, cell_links,
     )
     for layer in range(LAYERS - 1, -1, -1):
         s.mean_own[layer] = tile
@@ -914,10 +936,27 @@
         if layer + 1 == LAYERS:
             build_meta(z.count, a.segments, s.column, s.meta, s.segrow)
 
-        def visit(g, layer=layer, means=means, loads=loads):
+        pieces = [
+            Piece(
+                across, own, s.piece_stage.at[k], s.piece_got.at[layer, k], s.piece_send.at[layer, k], s.piece_recv.at[layer, k]
+            )
+            for k, own in enumerate((s.own_out, s.own_inner.at[0], s.own_inner.at[1]))
+        ]
+
+        def visit(g, layer=layer, means=means, loads=loads, older=older, pieces=pieces):
             if g == 0:
                 for copy in loads:
                     copy.wait()
+            if g == sum(ex.links):
+                if older is not None:
+                    older[2].phase(1)
+                    for k in range(2):
+                        for j in range(2, len(older[k].order)):
+                            older[k].phase(j)
+                    outs.append(finish(older[0], 0, layer + 1))
+                for i in range(across):
+                    s.own_out[i] = t_dot(s.scaled[...], s.sent_all[:, i * share : (i + 1) * share]).astype(BF)
+                pieces[0].phase(0)
             here = group_rows(ex, g, z.rows)
             first = (me ^ g) // 2 * 2
             for r in (g, g ^ 1):
@@ -936,21 +975,8 @@
             s.dy[here, :] = grad_gated * silu_gate
 
         sent = gather.run(visit)
-        pieces = [
-            Piece(
-                across, own, s.piece_stage.at[k], s.piece_got.at[layer, k], s.piece_send.at[layer, k], s.piece_recv.at[layer, k]
-            )
-            for k, own in enumerate((s.own_out, s.own_inner.at[0], s.own_inner.at[1]))
-        ]
         if older is not None:
-            older[2].phase(1)
-            for k in range(2):
-                for j in range(2, len(older[k].order)):
-                    older[k].phase(j)
-                outs.append(finish(older[k], k, layer + 1))
-        for i in range(across):
-            s.own_out[i] = t_dot(s.scaled[...], s.sent_all[:, i * share : (i + 1) * share]).astype(BF)
-        pieces[0].phase(0)
+            outs.append(finish(older[1], 1, layer + 1))
         for i in range(across):
             s.own_inner[0, i] = t_dot(s.normed[:, i * share : (i + 1) * share], s.rg[...]).astype(BF)
         pieces[1].phase(0)
@@ -997,7 +1023,9 @@
             if t >= 2 and not layer:
                 next(state_steps)
 
-        def produce(g, layer=layer):
+        def produce(g, own, layer=layer):
+            if own:
+                return
             here = group_rows(ex, g, z.rows)
             total = dot_t(s.rg[here, :], s.win[0, 0]) + dot_t(s.rv[here, :], s.win[0, 1])
             total = total + dot_t(s.rs[here, :], s.wst[0]) + dot(s.rd[here, :], s.wstep[0].astype(BF))
@@ -1052,12 +1080,22 @@
             at = (layer * across + i) * padded
             s.cell_own[i, layer * padded : (layer + 1) * padded, :] = state[at : at + padded, :].astype(BF)
             s.step_own[i, layer * 16 : layer * 16 + 8, :] = s.step_part[layer, i].astype(BF)
-    pieces[2].phase(1)
     cell = Piece(across, s.cell_own, s.cell_stage, s.cell_got, s.cell_send, s.cell_recv)
     step = Piece(across, s.step_own, s.step_stage, s.step_got, s.step_send, s.step_recv)
-    for k in range(len(cell.order)):
+    cell.phase(0)
+    step.phase(0)
+    for copy in outs:
+        copy.wait()
+    for j in range(2, len(pieces[0].order)):
+        pieces[0].phase(j)
+    last = [finish(pieces[0], 0, 0)]
+    pieces[2].phase(1)
+    for k in range(1, len(cell.order)):
         cell.phase(k)
         step.phase(k)
+    for j in range(2, len(pieces[1].order)):
+        pieces[1].phase(j)
+    last.append(finish(pieces[1], 1, 0))
     for layer in range(LAYERS):
         o.narrow[layer] = collected(s.narrow[layer], s.narrow_got.at[layer], narrow_copies[layer])
     o.gain[...] = collected(s.gain_mid[...], s.gain_two, gains_two)
@@ -1066,12 +1104,9 @@
     for layer in range(LAYERS):
         o.g_state[layer] = state[layer * padded : layer * padded + cells, :]
         o.g_step[layer] = steps[layer * 16 : layer * 16 + 8, :]
-    for copy in outs:
-        copy.wait()
-    for k, piece in enumerate(pieces):
-        for j in range(2, len(piece.order)):
-            piece.phase(j)
-    last = [finish(piece, k, 0) for k, piece in enumerate(pieces)]
+    for j in range(2, len(pieces[2].order)):
+        pieces[2].phase(j)
+    last.append(finish(pieces[2], 2, 0))
     for copy in cell_links + gains + wides + gains_two + wides_two + [c for copies in narrow_copies for c in copies]:
         copy.wait_send()
     for copy in last:
@@ -1193,7 +1228,7 @@
 def final_pass(ex, z, block_output, b):
     share, both, heads, taps, inner = z.depth // z.across, z.both, z.heads, z.taps, z.inner
     cells = z.depth // (ex.size * z.across)
-    steps = 4 if z.rows % 32 == 0 and share % 32 == 0 and inner % 32 == 0 else 1
+    steps = 2 if z.rows % 16 == 0 and share % 16 == 0 and inner % 16 == 0 else 1
     whole = lambda shape: pl.BlockSpec(shape, lambda i: (0,) * len(shape))
     rows = pl.BlockSpec((z.rows // steps, z.depth), lambda i: (i, 0))
     inner_spec = pl.BlockSpec((LAYERS, 2, share // steps, inner), lambda i: (0, 0, i, 0))

time: 274 us -> 266 us (0.971)
  Pallas kernels: 268 us -> 261 us
    pallas_call x2, Pallas kernels: 262 us -> 256 us  [run_kernel(): pl.pallas_call(functools.partial(kernel, ex, z, tuple(inputs), tuple(outp...]
where the time goes in v5:
time: 266 us; the launch traced here: 262 us
  Pallas kernels  261 us (98%)
    pallas_call x2, Pallas kernels, run_kernel(): pl.pallas_call(functools.partial(kernel, ex, z, tuple(inputs), tuple(outp...  256 us

profile of v5, /device:TPU:0, one launch (start us, length us, event | category | flops | bytes accessed | tf_op | source)
XLA Modules:
  0.0 261.7 jit_solution(13760544117804156759)
XLA Ops:
  0.6 94.5 %forward.1 = (bf16[2,1024,1536]{2,1,0:T(8,128)(2,1)}, f32[2,1024,384]{2,1,0:T(8,128)}, f32[2,1024,384]{2,1,0:T(8,128)}, f32[2,1024,384]{2,1,0:T(8,128)}, f32[2,1...) custom-call(f32[128,1536]{1,0:T(8,128)} %refs_0_.3, ...), custom_call_target="tpu_custom_call" | custom-call | flops 34359738368 | bytes 16777216 | tf_op jit(solution)/shard_map/forward/pallas_call | solution.py:645
  95.2 161.3 %backward.1 = (f32[128,1536]{1,0:T(8,128)}, f32[2,2,384,384]{3,2,1,0:T(8,128)}, f32[2,384,384]{2,1,0:T(8,128)}, f32[2,48,256]{2,1,0:T(8,128)}, f32[2,8,384]{2,1,...) custom-call(f32[128,1536]{1,0:T(8,128)} %refs_0_.3, f32[128,1536]{1,0:T(8,128)} %refs_1_.3, ...), custom_call_target="tpu_custom_call" | custom-call | flops 34359738368 | bytes 16777216 | tf_op jit(solution)/shard_map/backward/pallas_call | solution.py:645
  256.5 4.8 %final.1 = (f32[128,1536]{1,0:T(8,128)}, f32[128,1536]{1,0:T(8,128)}, f32[2,48]{1,0:T(2,128)}, f32[2,2,384,384]{3,2,1,0:T(8,128)}, f32[2,48,256]{2,1,0:T(8,128)}...) custom-call(f32[128,1536]{1,0:T(8,128)} %get-tuple-element.54.refs_0, ...), custom_call_target="tpu_custom_call" | custom-call | flops 1048576 | bytes 16777216 | tf_op jit(solution)/shard_map/final/pallas_call | solution.py:1242

commit v6 on v5

--- a/solution.py
+++ b/solution.py
@@ -59,6 +59,16 @@
     )
 
 
+def masked_sum(mask, value, parts=3):
+    ones = mask.astype(BF)
+    total = None
+    for _ in range(parts):
+        part = value.astype(BF)
+        total = dot(ones, part) if total is None else total + dot(ones, part)
+        value = value - part.astype(F32)
+    return total
+
+
 def sigmoid(x):
     return 1.0 / (1.0 + jnp.exp(-x))
 
@@ -75,7 +85,13 @@
 
 
 def expand(cols, inner, width):
-    rows = cols.shape[0]
+    rows, heads = cols.shape
+    if rows > 8:
+        row = lax.broadcasted_iota(jnp.int32, (heads, inner), 0)
+        col = lax.broadcasted_iota(jnp.int32, (heads, inner), 1)
+        ones = ((col >= row * width) & (col < (row + 1) * width)).astype(BF)
+        high = cols.astype(BF)
+        return dot(high, ones) + dot((cols - high.astype(F32)).astype(BF), ones)
     parts = []
     for _, wide, first, number in tiles_of(inner, width):
         lane = lax.broadcasted_iota(jnp.int32, (rows, wide), 1)
@@ -472,7 +488,7 @@
         x = pre_v * sigmoid(pre_v)
         st = (pre_s * sigmoid(pre_s)).astype(BF)
         dt = softplus(s.step_in[rows, :] + a.step_bias[at, :])
-        cum = exact(lower_ones(SIZE), -dt * jnp.exp(a.decay_log[at, :]))
+        cum = masked_sum(lower_ones(SIZE), -dt * jnp.exp(a.decay_log[at, :]))
         last = cum[SIZE - 1 : SIZE, :]
         xt = (x * expand(dt, inner, width)).astype(BF)
         s.x[rows, :] = x
@@ -752,7 +768,7 @@
         dt = softplus(raw_step)
         rate = jnp.exp(a.decay_log[at, :])
         log_decay = -dt * rate
-        cum = exact(lower_ones(SIZE), log_decay)
+        cum = masked_sum(lower_ones(SIZE), log_decay)
         cum_t = turned(cum)
         last = cum[SIZE - 1 : SIZE, :]
         dt_all = expand(dt, inner, width)
@@ -797,8 +813,8 @@
         )
         seg_col, seg_row = m[:, 0:1], segrow[0:1, rows]
         d_log = (
-            exact(later_ones(seg_col, seg_row), pairs)
-            + exact(earlier_ones(seg_col, seg_row), sums[0:SIZE])
+            masked_sum(later_ones(seg_col, seg_row), pairs, 2)
+            + masked_sum(earlier_ones(seg_col, seg_row), sums[0:SIZE], 2)
             + sums[2 * SIZE : 2 * SIZE + 1]
         )
         d_raw = (sums[SIZE : 2 * SIZE] - rate * d_log) * sigmoid(raw_step)

time: 266 us -> 263 us (0.989)
  Pallas kernels: 261 us -> 257 us
    pallas_call x2, Pallas kernels: 256 us -> 253 us  [run_kernel(): pl.pallas_call(functools.partial(kernel, ex, z, tuple(inputs), tuple(outp...]
where the time goes in v6:
time: 263 us; the launch traced here: 258 us
  Pallas kernels  257 us (98%)
    pallas_call x2, Pallas kernels, run_kernel(): pl.pallas_call(functools.partial(kernel, ex, z, tuple(inputs), tuple(outp...  253 us

profile of v6, /device:TPU:0, one launch (start us, length us, event | category | flops | bytes accessed | tf_op | source)
XLA Modules:
  0.0 258.5 jit_solution(16640259505924112011)
XLA Ops:
  0.6 94.3 %forward.1 = (bf16[2,1024,1536]{2,1,0:T(8,128)(2,1)}, f32[2,1024,384]{2,1,0:T(8,128)}, f32[2,1024,384]{2,1,0:T(8,128)}, f32[2,1024,384]{2,1,0:T(8,128)}, f32[2,1...) custom-call(f32[128,1536]{1,0:T(8,128)} %refs_0_.3, ...), custom_call_target="tpu_custom_call" | custom-call | flops 34359738368 | bytes 16777216 | tf_op jit(solution)/shard_map/forward/pallas_call | solution.py:661
  95.0 158.3 %backward.1 = (f32[128,1536]{1,0:T(8,128)}, f32[2,2,384,384]{3,2,1,0:T(8,128)}, f32[2,384,384]{2,1,0:T(8,128)}, f32[2,48,256]{2,1,0:T(8,128)}, f32[2,8,384]{2,1,...) custom-call(f32[128,1536]{1,0:T(8,128)} %refs_0_.3, f32[128,1536]{1,0:T(8,128)} %refs_1_.3, ...), custom_call_target="tpu_custom_call" | custom-call | flops 34359738368 | bytes 16777216 | tf_op jit(solution)/shard_map/backward/pallas_call | solution.py:661
  253.3 4.8 %final.1 = (f32[128,1536]{1,0:T(8,128)}, f32[128,1536]{1,0:T(8,128)}, f32[2,48]{1,0:T(2,128)}, f32[2,2,384,384]{3,2,1,0:T(8,128)}, f32[2,48,256]{2,1,0:T(8,128)}...) custom-call(f32[128,1536]{1,0:T(8,128)} %get-tuple-element.54.refs_0, ...), custom_call_target="tpu_custom_call" | custom-call | flops 1048576 | bytes 16777216 | tf_op jit(solution)/shard_map/final/pallas_call | solution.py:1258

commit v7 on v6

--- a/solution.py
+++ b/solution.py
@@ -964,12 +964,6 @@
                 for copy in loads:
                     copy.wait()
             if g == sum(ex.links):
-                if older is not None:
-                    older[2].phase(1)
-                    for k in range(2):
-                        for j in range(2, len(older[k].order)):
-                            older[k].phase(j)
-                    outs.append(finish(older[0], 0, layer + 1))
                 for i in range(across):
                     s.own_out[i] = t_dot(s.scaled[...], s.sent_all[:, i * share : (i + 1) * share]).astype(BF)
                 pieces[0].phase(0)
@@ -989,6 +983,12 @@
             grad_gated = grad_scaled * a.gate_gain[at, :] + (2.0 / z.inner_all) * mean * gated
             s.rg[here, :] = (grad_gated * y * (gate_sig * (1.0 + gate * (1.0 - gate_sig)))).astype(BF)
             s.dy[here, :] = grad_gated * silu_gate
+            if g == ex.links[-1] and older is not None:
+                older[2].phase(1)
+                for k in range(2):
+                    for j in range(2, len(older[k].order)):
+                        older[k].phase(j)
+                outs.append(finish(older[0], 0, layer + 1))
 
         sent = gather.run(visit)
         if older is not None:

time: 263 us -> 263 us (level)
  no operation moved by 1% of the time
where the time goes in v7:
time: 263 us; the launch traced here: 258 us
  Pallas kernels  257 us (98%)
    pallas_call x2, Pallas kernels, run_kernel(): pl.pallas_call(functools.partial(kernel, ex, z, tuple(inputs), tuple(outp...  252 us

profile of v7, /device:TPU:0, one launch (start us, length us, event | category | flops | bytes accessed | tf_op | source)
XLA Modules:
  0.0 258.1 jit_solution(16662463113849164982)
XLA Ops:
  0.6 94.3 %forward.1 = (bf16[2,1024,1536]{2,1,0:T(8,128)(2,1)}, f32[2,1024,384]{2,1,0:T(8,128)}, f32[2,1024,384]{2,1,0:T(8,128)}, f32[2,1024,384]{2,1,0:T(8,128)}, f32[2,1...) custom-call(f32[128,1536]{1,0:T(8,128)} %refs_0_.3, ...), custom_call_target="tpu_custom_call" | custom-call | flops 34359738368 | bytes 16777216 | tf_op jit(solution)/shard_map/forward/pallas_call | solution.py:661
  95.0 157.9 %backward.1 = (f32[128,1536]{1,0:T(8,128)}, f32[2,2,384,384]{3,2,1,0:T(8,128)}, f32[2,384,384]{2,1,0:T(8,128)}, f32[2,48,256]{2,1,0:T(8,128)}, f32[2,8,384]{2,1,...) custom-call(f32[128,1536]{1,0:T(8,128)} %refs_0_.3, f32[128,1536]{1,0:T(8,128)} %refs_1_.3, ...), custom_call_target="tpu_custom_call" | custom-call | flops 34359738368 | bytes 16777216 | tf_op jit(solution)/shard_map/backward/pallas_call | solution.py:661
  252.9 4.8 %final.1 = (f32[128,1536]{1,0:T(8,128)}, f32[128,1536]{1,0:T(8,128)}, f32[2,48]{1,0:T(2,128)}, f32[2,2,384,384]{3,2,1,0:T(8,128)}, f32[2,48,256]{2,1,0:T(8,128)}...) custom-call(f32[128,1536]{1,0:T(8,128)} %get-tuple-element.54.refs_0, ...), custom_call_target="tpu_custom_call" | custom-call | flops 1048576 | bytes 16777216 | tf_op jit(solution)/shard_map/final/pallas_call | solution.py:1258
